TPU v7x, 32 devices: a whole 2x2x4 slice. The times are simulated.
32 devices in a mesh: zero: 4 (over z), width: 4 (over y, x), unit: 2 (over core).
Axes of the slice: x: 2, y: 2, z: 4, core: 2. Of those that a mesh axis runs over, the one named last changes fastest.
Arguments:
- train_query: bfloat16 [8192, 4096], P(('unit', 'zero'), 'width'), parts along dimension 0, may hold values from -0.125 to 0.125
- low_query: bfloat16 [8192, 16], P(('unit', 'zero')), parts along dimension 0, may hold values from -0.09375 to 0.09375
- high_query: bfloat16 [32, 4096], P('unit', 'width'), parts along dimension 0, may hold values from -1.5 to 1.5
- train_key: bfloat16 [8192, 4096], P(('unit', 'zero'), 'width'), parts along dimension 0, may hold values from -0.125 to 0.125
- low_key: bfloat16 [8192, 16], P(('unit', 'zero')), parts along dimension 0, may hold values from -0.09375 to 0.09375
- high_key: bfloat16 [32, 4096], P('unit', 'width'), parts along dimension 0, may hold values from -1.5 to 1.5
- train_value: bfloat16 [8192, 4096], P(('unit', 'zero'), 'width'), parts along dimension 0, may hold values from -0.125 to 0.125
- low_value: bfloat16 [8192, 16], P(('unit', 'zero')), parts along dimension 0, may hold values from -0.09375 to 0.09375
- high_value: bfloat16 [32, 4096], P('unit', 'width'), parts along dimension 0, may hold values from -1.5 to 1.5
- norm_train: float32 [8192], P(('unit', 'zero', 'width')), parts along dimension 0, may hold values from 0.25 to 1.75
- norm_step: float32 [8192], P(('unit', 'zero', 'width')), parts along dimension 0, may hold values from -0.3 to 0.3
Outputs:
- serve_query: bfloat16 [8192, 4096], P('unit', 'width'), parts along dimension 0
- serve_key: bfloat16 [8192, 4096], P('unit', 'width'), parts along dimension 0
- serve_value: bfloat16 [8192, 4096], P('unit', 'width'), parts along dimension 0
- factor_query: float32 [8192], P(('unit', 'width')), parts along dimension 0
- factor_key: float32 [8192], P(('unit', 'width')), parts along dimension 0
- factor_value: float32 [8192], P(('unit', 'width')), parts along dimension 0
- serve_norm: bfloat16 [8192], P('unit'), parts along dimension 0
There are 2 independent parts, one for each index of `unit`. A program takes and returns all parts, laid end to end along the dimension named above; each array names one. Nothing has to cross between parts.
All inputs are finite; a program needn't handle non-finite values. Where the computation divides by a largest or mean magnitude, that divisor is 1e-20 or more.
Results may differ from a plain program's by a relative error of at most 0.001.
Values may be sent and summed in bfloat16 or wider, within the bound.
No kernel may reach another device: no remote copies, remote signals or barrier semaphores. Data moves between devices by JAX's collectives and lax.ppermute only.
A program may use at most 128 MiB of HBM per device.

v0:
```python
import functools

import jax
import jax.numpy as jnp
from jax import lax
from jax.experimental import pallas as pl
from jax.experimental.pallas import tpu as pltpu
from jax.sharding import PartitionSpec as P

mix_rate = 1.0


HBM = pltpu.MemorySpace.HBM
VMEM = pltpu.MemorySpace.VMEM


def tile_of(rows, most=256):
    tile = min(rows, most)
    while rows % tile:
        tile //= 2
    return tile


def merged(train, low_t, high):
    step = lax.dot_general(
        low_t, high, (((0,), (0,)), ((), ())), preferred_element_type=jnp.float32
    )
    return train.astype(jnp.float32) + mix_rate * step


def top_kernel(tq, tk, tv, lq, lk, lv, hq, hk, hv, norm, out, acc):
    step = pl.program_id(0)
    for index, (t, l, h) in enumerate(((tq, lq, hq), (tk, lk, hk), (tv, lv, hv))):
        size = jnp.abs(merged(t[...], l[...], h[...]))
        rows, cols = size.shape
        best = jnp.max(size.reshape(rows // 8, 8, cols), axis=0)

        @pl.when(step == 0)
        def _():
            acc[index] = best

        @pl.when(step > 0)
        def _():
            acc[index] = jnp.maximum(acc[index], best)

    @pl.when(step == pl.num_programs(0) - 1)
    def _():
        for index in range(3):
            out[pl.ds(index, 1), :] = jnp.max(acc[index], axis=0, keepdims=True)
        out[pl.ds(3, 1), :] = norm[...]


def column_tops(trains, lows, highs, norm):
    rows, cols = trains[0].shape
    rank = lows[0].shape[0]
    tile = tile_of(rows)
    return pl.pallas_call(
        top_kernel,
        grid=(rows // tile,),
        in_specs=[pl.BlockSpec((tile, cols), lambda i: (i, 0))] * 3
        + [pl.BlockSpec((rank, tile), lambda i: (0, i))] * 3
        + [pl.BlockSpec((rank, cols), lambda i: (0, 0))] * 3
        + [pl.BlockSpec((1, cols), lambda i: (0, 0))],
        out_specs=pl.BlockSpec((4, cols), lambda i: (0, 0)),
        out_shape=jax.ShapeDtypeStruct((4, cols), jnp.float32),
        scratch_shapes=[pltpu.VMEM((3, 8, cols), jnp.float32)],
        compiler_params=pltpu.CompilerParams(vmem_limit_bytes=16 * 2**20),
        name="tops",
        cost_estimate=pl.CostEstimate(
            flops=3 * 2 * rows * cols * rank, bytes_accessed=6 * rows * cols, transcendentals=0
        ),
    )(*trains, *lows, *highs, norm)


def join_kernel(count, place, *refs):
    parts, (factor, norm) = refs[:count], refs[count:]
    total = parts[0][...]
    for part in parts[1:]:
        total = jnp.maximum(total, part[...])
    factor[...] = total
    for shift, part in enumerate(parts):
        owner = lax.rem(place[0] - shift + count, count)
        norm[pl.ds(owner, 1), :] = part[pl.ds(3, 1), :]


def join_tops(place, parts):
    count, cols = len(parts), parts[0].shape[1]
    return pl.pallas_call(
        functools.partial(join_kernel, count),
        in_specs=[pl.BlockSpec(memory_space=pltpu.MemorySpace.SMEM)]
        + [pl.BlockSpec(memory_space=VMEM)] * count,
        out_specs=[pl.BlockSpec(memory_space=VMEM)] * 2,
        out_shape=[
            jax.ShapeDtypeStruct((4, cols), jnp.float32),
            jax.ShapeDtypeStruct((max(8, count), cols), jnp.float32),
        ],
        compiler_params=pltpu.CompilerParams(vmem_limit_bytes=16 * 2**20),
        name="join",
    )(place, *parts)


def scale_kernel(index, train, low_t, high, factor, serve):
    fresh = merged(train[...], low_t[...], high[...])
    serve[...] = (fresh / factor[pl.ds(index, 1), :]).astype(serve.dtype)


def scaled(index, train, low_t, high, factor, low_at=0):
    rows, cols = train.shape
    rank = high.shape[0]
    tile = tile_of(rows)
    first = low_at // tile
    return pl.pallas_call(
        functools.partial(scale_kernel, index),
        grid=(rows // tile,),
        in_specs=[
            pl.BlockSpec((tile, cols), lambda i: (i, 0)),
            pl.BlockSpec((rank, tile), lambda i: (0, i + first)),
            pl.BlockSpec((rank, cols), lambda i: (0, 0)),
            pl.BlockSpec((4, cols), lambda i: (0, 0)),
        ],
        out_specs=pl.BlockSpec((tile, cols), lambda i: (i, 0)),
        out_shape=jax.ShapeDtypeStruct((rows, cols), jnp.bfloat16),
        compiler_params=pltpu.CompilerParams(vmem_limit_bytes=16 * 2**20),
        name="scale",
        cost_estimate=pl.CostEstimate(
            flops=2 * rows * cols * rank, bytes_accessed=4 * rows * cols, transcendentals=0
        ),
    )(train, low_t, high, factor)


def place_kernel(plan, count, near, place, *refs):
    sources, out, buffers = refs[1 : 1 + len(plan)], refs[1 + len(plan)], refs[2 + len(plan) :]
    slots, (read, written) = buffers[:-2], buffers[-2:]
    mine = place[0]
    for index, (shift, at, shard) in enumerate(plan):
        owner = mine + shift
        rows = sources[index].shape[0]
        part = tile_of(rows)

        @pl.when((owner >= 0) & (owner < count))
        def _(index=index, owner=owner, rows=rows, part=part, at=at, shard=shard):
            begins = range(0, rows, part)
            loads, stores = [], []
            if not near:
                for p, begin in enumerate(begins):
                    loads.append(
                        pltpu.make_async_copy(
                            sources[index].at[pl.ds(begin, part)],
                            slots[index].at[pl.ds(begin, part)],
                            read.at[index, p],
                        )
                    )
                    loads[-1].start()
            held = sources[index] if near else slots[index]
            for p, begin in enumerate(begins):
                start = pl.multiple_of(owner * shard + at + begin, part)
                if not near:
                    loads[p].wait()
                stores.append(
                    pltpu.make_async_copy(
                        held.at[pl.ds(begin, part)],
                        out.at[pl.ds(start, part)],
                        written.at[index, p],
                    )
                )
                stores[-1].start()
            for store in stores:
                store.wait()


def placed(place, out, count, plan, sources, near=True):
    pieces = max(source.shape[0] // tile_of(source.shape[0]) for source in sources)
    if near:
        sources = [pltpu.with_memory_space_constraint(source, VMEM) for source in sources]
    return pl.pallas_call(
        functools.partial(place_kernel, plan, count, near),
        in_specs=[pl.BlockSpec(memory_space=pltpu.MemorySpace.SMEM)]
        + [pl.BlockSpec(memory_space=HBM)]
        + [pl.BlockSpec(memory_space=VMEM if near else HBM)] * len(sources),
        out_specs=pl.BlockSpec(memory_space=HBM),
        out_shape=jax.ShapeDtypeStruct(out.shape, out.dtype),
        scratch_shapes=[
            pltpu.VMEM((8, 128) if near else source.shape, source.dtype) for source in sources
        ]
        + [pltpu.SemaphoreType.DMA((len(sources), pieces))] * 2,
        input_output_aliases={1: 0},
        compiler_params=pltpu.CompilerParams(vmem_limit_bytes=16 * 2**20),
        name="place",
        cost_estimate=pl.CostEstimate(
            flops=sum(source.size for source in sources),
            bytes_accessed=sum(4 * source.size for source in sources),
            transcendentals=0,
        ),
    )(place, out, *sources)


def own_kernel(index, place, train, low_t, high, factor, serve, out):
    del place
    fresh = merged(train[...], low_t[...], high[...])
    block = (fresh / factor[pl.ds(index, 1), :]).astype(serve.dtype)
    serve[...] = block
    out[...] = block


def own_scaled(index, place, count, train, low_t, high, factor):
    rows, cols = train.shape
    rank = high.shape[0]
    tile = tile_of(rows)
    steps = rows // tile
    return pl.pallas_call(
        functools.partial(own_kernel, index),
        grid_spec=pltpu.PrefetchScalarGridSpec(
            num_scalar_prefetch=1,
            grid=(steps,),
            in_specs=[
                pl.BlockSpec((tile, cols), lambda i, place: (i, 0)),
                pl.BlockSpec((rank, tile), lambda i, place: (0, i)),
                pl.BlockSpec((rank, cols), lambda i, place: (0, 0)),
                pl.BlockSpec((4, cols), lambda i, place: (0, 0)),
            ],
            out_specs=[
                pl.BlockSpec((tile, cols), lambda i, place: (i, 0)),
                pl.BlockSpec((tile, cols), lambda i, place: (place[0] * steps + i, 0)),
            ],
        ),
        out_shape=[
            jax.ShapeDtypeStruct((rows, cols), jnp.bfloat16),
            jax.ShapeDtypeStruct((count * rows, cols), jnp.bfloat16),
        ],
        compiler_params=pltpu.CompilerParams(vmem_limit_bytes=16 * 2**20),
        name="own",
        cost_estimate=pl.CostEstimate(
            flops=2 * rows * cols * rank, bytes_accessed=6 * rows * cols, transcendentals=0
        ),
    )(place, train, low_t, high, factor)


def per_device(count, *operands):
    return merged_for_serving(count, *operands)


def merged_for_serving(
    count,
    train_query,
    low_query,
    high_query,
    train_key,
    low_key,
    high_key,
    train_value,
    low_value,
    high_value,
    norm_train,
    norm_step,
):
    rows, cols = train_query.shape
    half = rows // 2
    place = lax.axis_index("zero").astype(jnp.int32).reshape(1)
    lows = (low_query.T, low_key.T, low_value.T)
    highs = (high_query, high_key, high_value)
    trains = (train_query, train_key, train_value)

    def left(x, hop):
        return lax.ppermute(x, "zero", [(i, i - 1) for i in range(1, count - hop + 1)])

    def right(x, hop):
        return lax.ppermute(x, "zero", [(i, i + 1) for i in range(hop - 1, count - 1)])

    def both(pair, hop):
        from_right, from_left = pair
        return left(from_right, hop), right(from_left, hop)

    raw = [both((train_query[:half],) * 2, 1)]
    norm = jnp.pad(norm_train + norm_step, (0, cols - norm_train.shape[0])).reshape(1, cols)
    tops = column_tops(trains, lows, highs, norm)
    parts = [tops]
    for s in range(1, count):
        parts.append(lax.ppermute(tops, "zero", [(i, (i + s) % count) for i in range(count)]))
    raw.append(both((train_query[half:],) * 2, 1))
    near = left(lows[0], 1), right(lows[0], 1)
    factor, norms = join_tops(place, parts)

    outs, sends = [None] * 3, [None] * 3
    for index in (1, 2, 0):
        sends[index], outs[index] = own_scaled(
            index, place, count, trains[index], lows[index], highs[index], factor
        )
    pieces = []
    for p in range(2):
        pair = []
        for got, low in zip(raw[p], near):
            pair.append(scaled(0, got, low, high_query, factor, p * half))
        pieces.append((f"q{p}", 0, p * half, tuple(pair)))
    for index, name in ((1, "k"), (2, "v")):
        pieces.append((name, index, 0, both((sends[index],) * 2, 1)))

    for hop in range(1, count):
        later = []
        for name, index, at, pair in pieces:
            if hop + 1 < count:
                later.append((name, index, at, both(pair, hop + 1)))
            outs[index] = placed(
                place,
                outs[index],
                count,
                ((hop, at, rows), (-hop, at, rows)),
                pair,
            )
        pieces = later

    size = norm_train.shape[0]
    wide = lax.all_gather(norms[:count, :size].astype(jnp.bfloat16), "width", axis=1, tiled=True)
    serve_norm = wide.reshape(-1)
    return (*outs, factor[0], factor[1], factor[2], serve_norm)


def solution(mesh):
    count = mesh.shape["zero"]
    return jax.shard_map(
        functools.partial(per_device, count),
        mesh=mesh,
        in_specs=(
            P(("unit", "zero"), "width"),
            P(("unit", "zero"), None),
            P("unit", "width"),
            P(("unit", "zero"), "width"),
            P(("unit", "zero"), None),
            P("unit", "width"),
            P(("unit", "zero"), "width"),
            P(("unit", "zero"), None),
            P("unit", "width"),
            P(("unit", "zero", "width")),
            P(("unit", "zero", "width")),
        ),
        out_specs=(
            P("unit", "width"),
            P("unit", "width"),
            P("unit", "width"),
            P(("unit", "width")),
            P(("unit", "width")),
            P(("unit", "width")),
            P("unit"),
        ),
        check_vma=False,
    )
```

profile of v0, /device:TPU:24, one launch (start us, length us, event | category | flops | bytes accessed | tf_op | source)
XLA Modules:
  0.0 437.8 jit_solution(6397378072550431723)
XLA Ops:
  0.7 3.2 fusion
  3.9 1.3 collective-permute-start.5
  5.1 4.6 %collective-permute-start.3 = (bf16[512,1024]{1,0:T(8,128)(2,1)}, bf16[512,1024]{1,0:T(8,128)(2,1)S(1)}, u32[]{:S(2)}, u32[]{:S(2)}) collective-permute-start(bf16[512,1024]{1,0:T(8,128)(2,1)} %get-tuple-element.22), channel_id=1, source_target_pairs={{8,0},{16,8},{24,16},{9,1},{17,9},{25,17},{10,2},{18,10},{26,18},{... | collective-permute-start | bytes 3145736 | tf_op jit(solution)/shard_map/ppermute | solution.py:264
  9.8 1.6 copy-done.3
  15.2 4.7 %tops.1.refs_0_ = f32[4,1024]{1,0:T(4,128)S(1)} custom-call(bf16[1024,1024]{1,0:T(8,128)(2,1)S(1)} %copy-done, bf16[1024,1024]{1,0:T(8,128)(2,1)S(1)} %copy-done.1, bf16[1024,1024]{1,0:T(8,128)(2,1)S(1)} %copy-done.3, bf16[16,1024]{1,0:T(8,128)(2,1)} %bitcast.1.lq.low_t, bf16[16,1024]{1,0:T(8,128)(2,1)S(1)} %bitcast.12, bf16[16,1024]{1,0:T(8,128)(2,1)S(1)} %bitcast.14, ...), custom_call_target="tpu_custom_call" | custom-call | flops 100663296 | bytes 6291456 | tf_op jit(solution)/shard_map/tops/pallas_call | solution.py:57
  20.1 1.8 collective-permute-start.1
  21.8 1.3 collective-permute-start.6
  23.1 9.4 %collective-permute-done.refs_1_ = f32[4,1024]{1,0:T(4,128)S(1)} collective-permute-done((f32[4,1024]{1,0:T(4,128)S(1)}, f32[4,1024]{1,0:T(4,128)S(1)}, u32[]{:S(2)}, u32[]{:S(2)}) %collective-permute-start) | collective-permute-done | bytes 16416 | tf_op jit(solution)/shard_map/ppermute | solution.py:278
  32.6 1.9 collective-permute-start.4
  34.6 5.4 %collective-permute-done.2.refs_3_ = f32[4,1024]{1,0:T(4,128)S(1)} collective-permute-done((f32[4,1024]{1,0:T(4,128)S(1)}, f32[4,1024]{1,0:T(4,128)S(1)}, u32[]{:S(2)}, u32[]{:S(2)}) %collective-permute-start.2) | collective-permute-done | bytes 16416 | tf_op jit(solution)/shard_map/ppermute | solution.py:278
  40.0 4.2 collective-permute-start.7
  44.3 1.3 collective-permute-start.8
  45.6 1.9 scale.5.refs_2_
  47.5 1.3 collective-permute-start.10
  50.5 2.6 own.4
  53.1 8.6 %collective-permute-start.17 = (bf16[1024,1024]{1,0:T(8,128)(2,1)S(1)}, bf16[1024,1024]{1,0:T(8,128)(2,1)S(1)}, u32[]{:S(2)}, u32[]{:S(2)}) collective-permute-start(bf16[1024,1024]{1,0:T(8,128)(2,1)S(1)} %get-tuple-element.17), channel_id=1, source_target_pairs={{8,0},{16,8},{24,16},{9,1},{17,9},{25,17},{10,2},{18,10},{26,18},{... | collective-permute-start | bytes 6291464 | tf_op jit(solution)/shard_map/ppermute | solution.py:264
  61.7 5.4 %collective-permute-done.7.train = bf16[512,1024]{1,0:T(8,128)(2,1)} collective-permute-done((bf16[512,1024]{1,0:T(8,128)(2,1)}, bf16[512,1024]{1,0:T(8,128)(2,1)}, u32[]{:S(2)}, u32[]{:S(2)}) %collective-permute-start.7) | collective-permute-done | bytes 1048608 | tf_op jit(solution)/shard_map/ppermute | solution.py:264
  67.1 1.3 collective-permute-start.18
  68.4 1.7 scale.6.refs_1_
  70.2 2.3 collective-permute-done.8.train
  73.2 2.6 own.5
  75.8 19.1 %collective-permute-done.10.refs_2_ = bf16[512,1024]{1,0:T(8,128)(2,1)S(1)} collective-permute-done((bf16[512,1024]{1,0:T(8,128)(2,1)S(1)}, bf16[512,1024]{1,0:T(8,128)(2,1)S(1)}, u32[]{:S(2)}, u32[]{:S(2)}) %collective-permute-start.10) | collective-permute-done | bytes 1048608 | tf_op jit(solution)/shard_map/ppermute | solution.py:267
  94.9 3.4 collective-permute-start.23
  98.3 1.3 collective-permute-start.24
  100.3 1.3 collective-permute-start.12
  101.6 101.5 %collective-permute-done.12.refs_2_ = bf16[512,1024]{1,0:T(8,128)(2,1)S(1)} collective-permute-done((bf16[512,1024]{1,0:T(8,128)(2,1)S(1)}, bf16[512,1024]{1,0:T(8,128)(2,1)S(1)}, u32[]{:S(2)}, u32[]{:S(2)}) %collective-permute-start.12) | collective-permute-done | bytes 1048608 | tf_op jit(solution)/shard_map/ppermute | solution.py:267
  204.7 1.3 collective-permute-start.20
  206.8 1.3 collective-permute-start.26
  208.1 1.3 collective-permute-start.14
  209.4 108.2 %collective-permute-done.14.refs_2_ = bf16[512,1024]{1,0:T(8,128)(2,1)S(1)} collective-permute-done((bf16[512,1024]{1,0:T(8,128)(2,1)S(1)}, bf16[512,1024]{1,0:T(8,128)(2,1)S(1)}, u32[]{:S(2)}, u32[]{:S(2)}) %collective-permute-start.14) | collective-permute-done | bytes 1048608 | tf_op jit(solution)/shard_map/ppermute | solution.py:267
  319.1 1.3 collective-permute-start.22
  321.3 1.3 collective-permute-start.28
  322.6 1.3 collective-permute-start.16
  323.9 8.1 %all_gather.3 = bf16[4,1024]{1,0:T(4,128)(2,1)S(1)} all-gather(bf16[4,256]{1,0:T(4,128)(2,1)S(1)} %slice.27), channel_id=1, replica_groups=mesh['zero'=4,'width'=4,'unit'=2] {'width'}, dimensions={1}, use_global_device_ids=true | all-gather | bytes 10240 | tf_op jit(solution)/shard_map/all_gather | solution.py:312
  332.6 4.0 own.3
  337.2 1.0 place.12.refs_0_
  338.2 1.1 place.13.refs_0_
  339.3 1.1 place.14.refs_0_
  340.3 1.1 place.15.refs_0_
  341.4 1.5 place.18.refs_0_
  342.9 1.5 place.21.refs_0_
  344.3 1.1 place.16.refs_0_
  345.4 85.4 %collective-permute-done.16.refs_2_ = bf16[512,1024]{1,0:T(8,128)(2,1)S(1)} collective-permute-done((bf16[512,1024]{1,0:T(8,128)(2,1)S(1)}, bf16[512,1024]{1,0:T(8,128)(2,1)S(1)}, u32[]{:S(2)}, u32[]{:S(2)}) %collective-permute-start.16) | collective-permute-done | bytes 1048608 | tf_op jit(solution)/shard_map/ppermute | solution.py:267
  430.8 1.0 place.17
  431.8 1.5 place.19.refs_0_
  433.3 1.5 place.22.refs_0_
  434.8 1.5 place.20
  436.3 1.5 place.23
  (72 shorter events, 13.0 us)
Async XLA Ops:
  0.6 9.2 %copy-start = (bf16[1024,1024]{1,0:T(8,128)(2,1)S(1)}, bf16[1024,1024]{1,0:T(8,128)(2,1)}, u32[]{:S(2)}) copy-start(bf16[1024,1024]{1,0:T(8,128)(2,1)} %train.3) | copy-start | bytes 6291460
  0.6 9.1 %copy-start.15 = (f32[256]{0:T(256)S(1)}, f32[256]{0:T(256)}, u32[]{:S(2)}) copy-start(f32[256]{0:T(256)} %param.20) | copy-start | bytes 3076
  0.7 9.1 %copy-start.16 = (f32[256]{0:T(256)S(1)}, f32[256]{0:T(256)}, u32[]{:S(2)}) copy-start(f32[256]{0:T(256)} %param.21) | copy-start | bytes 3076
  0.7 9.2 %copy-start.1 = (bf16[1024,1024]{1,0:T(8,128)(2,1)S(1)}, bf16[1024,1024]{1,0:T(8,128)(2,1)}, u32[]{:S(2)}) copy-start(bf16[1024,1024]{1,0:T(8,128)(2,1)} %train.4) | copy-start | bytes 6291460
  3.9 41.7 %collective-permute-start.5 = (bf16[512,1024]{1,0:T(8,128)(2,1)}, bf16[512,1024]{1,0:T(8,128)(2,1)}, u32[]{:S(2)}, u32[]{:S(2)}) collective-permute-start(bf16[512,1024]{1,0:T(8,128)(2,1)} %get-tuple-element.22), channel_id=1, source_target_pairs={{0,8},{8,16},{16,24},{1,9},{9,17},{17,25},{2,10},{10,18},{18,26},{... | collective-permute-start | bytes 3145736 | tf_op jit(solution)/shard_map/ppermute | solution.py:267
  5.1 43.7 %collective-permute-start.3 = (bf16[512,1024]{1,0:T(8,128)(2,1)}, bf16[512,1024]{1,0:T(8,128)(2,1)S(1)}, u32[]{:S(2)}, u32[]{:S(2)}) collective-permute-start(bf16[512,1024]{1,0:T(8,128)(2,1)} %get-tuple-element.22), channel_id=1, source_target_pairs={{8,0},{16,8},{24,16},{9,1},{17,9},{25,17},{10,2},{18,10},{26,18},{... | collective-permute-start | bytes 3145736 | tf_op jit(solution)/shard_map/ppermute | solution.py:264
  9.8 1.6 copy-start.3
  11.4 0.8 copy-start.5
  12.2 0.8 copy-start.7
  12.9 0.8 copy-start.9
  13.7 0.8 copy-start.11
  14.5 0.8 copy-start.13
  15.2 30.4 %copy-start.6 = (bf16[16,1024]{1,0:T(8,128)(2,1)S(1)}, bf16[16,1024]{1,0:T(8,128)(2,1)}, u32[]{:S(2)}) copy-start(bf16[16,1024]{1,0:T(8,128)(2,1)} %high.11) | copy-start | bytes 98308
  19.9 12.6 %collective-permute-start = (f32[4,1024]{1,0:T(4,128)S(1)}, f32[4,1024]{1,0:T(4,128)S(1)}, u32[]{:S(2)}, u32[]{:S(2)}) collective-permute-start(f32[4,1024]{1,0:T(4,128)S(1)} %tops.1.refs_0_), channel_id=1, source_target_pairs={{0,8},{8,16},{16,24},{24,0},{1,9},{9,17},{17,25},{25,1},{2,10},{10... | collective-permute-start | bytes 49160 | tf_op jit(solution)/shard_map/ppermute | solution.py:278
  20.1 14.4 %collective-permute-start.1 = (f32[4,1024]{1,0:T(4,128)S(1)}, f32[4,1024]{1,0:T(4,128)S(1)}, u32[]{:S(2)}, u32[]{:S(2)}) collective-permute-start(f32[4,1024]{1,0:T(4,128)S(1)} %tops.1.refs_0_), channel_id=1, source_target_pairs={{0,16},{8,24},{16,0},{24,8},{1,17},{9,25},{17,1},{25,9},{2,18},{10... | collective-permute-start | bytes 49160 | tf_op jit(solution)/shard_map/ppermute | solution.py:278
  21.8 22.4 %collective-permute-start.6 = (bf16[16,1024]{1,0:T(8,128)(2,1)}, bf16[16,1024]{1,0:T(8,128)(2,1)S(1)}, u32[]{:S(2)}, u32[]{:S(2)}) collective-permute-start(bf16[16,1024]{1,0:T(8,128)(2,1)} %bitcast.1.lq.low_t), channel_id=1, source_target_pairs={{0,8},{8,16},{16,24},{1,9},{9,17},{17,25},{2,10},{10,18},{18,26},{... | collective-permute-start | bytes 98312 | tf_op jit(solution)/shard_map/ppermute | solution.py:267
  32.6 16.3 %collective-permute-start.4 = (bf16[16,1024]{1,0:T(8,128)(2,1)}, bf16[16,1024]{1,0:T(8,128)(2,1)S(1)}, u32[]{:S(2)}, u32[]{:S(2)}) collective-permute-start(bf16[16,1024]{1,0:T(8,128)(2,1)} %bitcast.1.lq.low_t), channel_id=1, source_target_pairs={{8,0},{16,8},{24,16},{9,1},{17,9},{25,17},{10,2},{18,10},{26,18},{... | collective-permute-start | bytes 98312 | tf_op jit(solution)/shard_map/ppermute | solution.py:264
  34.4 5.6 %collective-permute-start.2 = (f32[4,1024]{1,0:T(4,128)S(1)}, f32[4,1024]{1,0:T(4,128)S(1)}, u32[]{:S(2)}, u32[]{:S(2)}) collective-permute-start(f32[4,1024]{1,0:T(4,128)S(1)} %tops.1.refs_0_), channel_id=1, source_target_pairs={{0,24},{8,0},{16,8},{24,16},{1,25},{9,1},{17,9},{25,17},{2,26},{10... | collective-permute-start | bytes 49160 | tf_op jit(solution)/shard_map/ppermute | solution.py:278
  40.0 27.1 %collective-permute-start.7 = (bf16[512,1024]{1,0:T(8,128)(2,1)}, bf16[512,1024]{1,0:T(8,128)(2,1)}, u32[]{:S(2)}, u32[]{:S(2)}) collective-permute-start(bf16[512,1024]{1,0:T(8,128)(2,1)} %get-tuple-element.21), channel_id=1, source_target_pairs={{8,0},{16,8},{24,16},{9,1},{17,9},{25,17},{10,2},{18,10},{26,18},{... | collective-permute-start | bytes 3145736 | tf_op jit(solution)/shard_map/ppermute | solution.py:264
  44.3 28.1 %collective-permute-start.8 = (bf16[512,1024]{1,0:T(8,128)(2,1)}, bf16[512,1024]{1,0:T(8,128)(2,1)S(1)}, u32[]{:S(2)}, u32[]{:S(2)}) collective-permute-start(bf16[512,1024]{1,0:T(8,128)(2,1)} %get-tuple-element.21), channel_id=1, source_target_pairs={{0,8},{8,16},{16,24},{1,9},{9,17},{17,25},{2,10},{10,18},{18,26},{... | collective-permute-start | bytes 3145736 | tf_op jit(solution)/shard_map/ppermute | solution.py:267
  45.6 4.8 %copy-start.2 = (bf16[1024,1024]{1,0:T(8,128)(2,1)S(1)}, bf16[1024,1024]{1,0:T(8,128)(2,1)}, u32[]{:S(2)}) copy-start(bf16[1024,1024]{1,0:T(8,128)(2,1)} %train.4) | copy-start | bytes 6291460
  45.6 4.8 %copy-start.8 = (bf16[1024,16]{0,1:T(8,128)(2,1)S(1)}, bf16[1024,16]{0,1:T(8,128)(2,1)}, u32[]{:S(2)}) copy-start(bf16[1024,16]{0,1:T(8,128)(2,1)} %param.15) | copy-start | bytes 98308
  45.6 4.8 %copy-start.10 = (bf16[16,1024]{1,0:T(8,128)(2,1)S(1)}, bf16[16,1024]{1,0:T(8,128)(2,1)}, u32[]{:S(2)}) copy-start(bf16[16,1024]{1,0:T(8,128)(2,1)} %high.12) | copy-start | bytes 98308
  47.5 47.4 %collective-permute-start.10 = (bf16[512,1024]{1,0:T(8,128)(2,1)S(1)}, bf16[512,1024]{1,0:T(8,128)(2,1)S(1)}, u32[]{:S(2)}, u32[]{:S(2)}) collective-permute-start(bf16[512,1024]{1,0:T(8,128)(2,1)S(1)} %scale.5.refs_2_), channel_id=1, source_target_pairs={{8,16},{16,24},{9,17},{17,25},{10,18},{18,26},{11,19},{19,27},{12,... | collective-permute-start | bytes 3145736 | tf_op jit(solution)/shard_map/ppermute | solution.py:267
  49.5 23.6 %copy-start.4 = (bf16[1024,1024]{1,0:T(8,128)(2,1)S(1)}, bf16[1024,1024]{1,0:T(8,128)(2,1)}, u32[]{:S(2)}) copy-start(bf16[1024,1024]{1,0:T(8,128)(2,1)} %train.5) | copy-start | bytes 6291460
  49.6 23.6 %copy-start.12 = (bf16[1024,16]{0,1:T(8,128)(2,1)S(1)}, bf16[1024,16]{0,1:T(8,128)(2,1)}, u32[]{:S(2)}) copy-start(bf16[1024,16]{0,1:T(8,128)(2,1)} %param.18) | copy-start | bytes 98308
  49.6 23.6 %copy-start.14 = (bf16[16,1024]{1,0:T(8,128)(2,1)S(1)}, bf16[16,1024]{1,0:T(8,128)(2,1)}, u32[]{:S(2)}) copy-start(bf16[16,1024]{1,0:T(8,128)(2,1)} %high.13) | copy-start | bytes 98308
  49.6 48.7 %collective-permute-start.9 = (bf16[512,1024]{1,0:T(8,128)(2,1)S(1)}, bf16[512,1024]{1,0:T(8,128)(2,1)S(1)}, u32[]{:S(2)}, u32[]{:S(2)}) collective-permute-start(bf16[512,1024]{1,0:T(8,128)(2,1)S(1)} %scale.4.refs_1_), channel_id=1, source_target_pairs={{8,0},{16,8},{9,1},{17,9},{10,2},{18,10},{11,3},{19,11},{12,4},{20... | collective-permute-start | bytes 3145736 | tf_op jit(solution)/shard_map/ppermute | solution.py:264
  53.1 150.7 %collective-permute-start.17 = (bf16[1024,1024]{1,0:T(8,128)(2,1)S(1)}, bf16[1024,1024]{1,0:T(8,128)(2,1)S(1)}, u32[]{:S(2)}, u32[]{:S(2)}) collective-permute-start(bf16[1024,1024]{1,0:T(8,128)(2,1)S(1)} %get-tuple-element.17), channel_id=1, source_target_pairs={{8,0},{16,8},{24,16},{9,1},{17,9},{25,17},{10,2},{18,10},{26,18},{... | collective-permute-start | bytes 6291464 | tf_op jit(solution)/shard_map/ppermute | solution.py:264
  67.1 137.5 %collective-permute-start.18 = (bf16[1024,1024]{1,0:T(8,128)(2,1)S(1)}, bf16[1024,1024]{1,0:T(8,128)(2,1)S(1)}, u32[]{:S(2)}, u32[]{:S(2)}) collective-permute-start(bf16[1024,1024]{1,0:T(8,128)(2,1)S(1)} %get-tuple-element.17), channel_id=1, source_target_pairs={{0,8},{8,16},{16,24},{1,9},{9,17},{17,25},{2,10},{10,18},{18,26},{... | collective-permute-start | bytes 6291464 | tf_op jit(solution)/shard_map/ppermute | solution.py:267
  72.4 27.9 %collective-permute-start.11 = (bf16[512,1024]{1,0:T(8,128)(2,1)S(1)}, bf16[512,1024]{1,0:T(8,128)(2,1)S(1)}, u32[]{:S(2)}, u32[]{:S(2)}) collective-permute-start(bf16[512,1024]{1,0:T(8,128)(2,1)S(1)} %scale.6.refs_1_), channel_id=1, source_target_pairs={{8,0},{16,8},{9,1},{17,9},{10,2},{18,10},{11,3},{19,11},{12,4},{20... | collective-permute-start | bytes 3145736 | tf_op jit(solution)/shard_map/ppermute | solution.py:264
  94.9 111.1 %collective-permute-start.23 = (bf16[1024,1024]{1,0:T(8,128)(2,1)S(1)}, bf16[1024,1024]{1,0:T(8,128)(2,1)S(1)}, u32[]{:S(2)}, u32[]{:S(2)}) collective-permute-start(bf16[1024,1024]{1,0:T(8,128)(2,1)S(1)} %get-tuple-element.19), channel_id=1, source_target_pairs={{8,0},{16,8},{24,16},{9,1},{17,9},{25,17},{10,2},{18,10},{26,18},{... | collective-permute-start | bytes 6291464 | tf_op jit(solution)/shard_map/ppermute | solution.py:264
  98.3 108.5 %collective-permute-start.24 = (bf16[1024,1024]{1,0:T(8,128)(2,1)S(1)}, bf16[1024,1024]{1,0:T(8,128)(2,1)S(1)}, u32[]{:S(2)}, u32[]{:S(2)}) collective-permute-start(bf16[1024,1024]{1,0:T(8,128)(2,1)S(1)} %get-tuple-element.19), channel_id=1, source_target_pairs={{0,8},{8,16},{16,24},{1,9},{9,17},{17,25},{2,10},{10,18},{18,26},{... | collective-permute-start | bytes 6291464 | tf_op jit(solution)/shard_map/ppermute | solution.py:267
  100.3 102.8 %collective-permute-start.12 = (bf16[512,1024]{1,0:T(8,128)(2,1)S(1)}, bf16[512,1024]{1,0:T(8,128)(2,1)S(1)}, u32[]{:S(2)}, u32[]{:S(2)}) collective-permute-start(bf16[512,1024]{1,0:T(8,128)(2,1)S(1)} %scale.7.refs_2_), channel_id=1, source_target_pairs={{8,16},{16,24},{9,17},{17,25},{10,18},{18,26},{11,19},{19,27},{12,... | collective-permute-start | bytes 3145736 | tf_op jit(solution)/shard_map/ppermute | solution.py:267
  203.1 5.0 %collective-permute-start.13 = (bf16[512,1024]{1,0:T(8,128)(2,1)S(1)}, bf16[512,1024]{1,0:T(8,128)(2,1)S(1)}, u32[]{:S(2)}, u32[]{:S(2)}) collective-permute-start(bf16[512,1024]{1,0:T(8,128)(2,1)S(1)} %collective-permute-done.9.refs_1_), channel_id=1, source_target_pairs={{8,0},{9,1},{10,2},{11,3},{12,4},{13,5},{14,6},{15,7}} | collective-permute-start | bytes 3145736 | tf_op jit(solution)/shard_map/ppermute | solution.py:264
  203.8 114.5 %collective-permute-start.19 = (bf16[1024,1024]{1,0:T(8,128)(2,1)S(1)}, bf16[1024,1024]{1,0:T(8,128)(2,1)S(1)}, u32[]{:S(2)}, u32[]{:S(2)}) collective-permute-start(bf16[1024,1024]{1,0:T(8,128)(2,1)S(1)} %collective-permute-done.17.refs_1_), channel_id=1, source_target_pairs={{8,0},{16,8},{9,1},{17,9},{10,2},{18,10},{11,3},{19,11},{12,4},{20... | collective-permute-start | bytes 6291464 | tf_op jit(solution)/shard_map/ppermute | solution.py:264
  204.7 114.5 %collective-permute-start.20 = (bf16[1024,1024]{1,0:T(8,128)(2,1)S(1)}, bf16[1024,1024]{1,0:T(8,128)(2,1)S(1)}, u32[]{:S(2)}, u32[]{:S(2)}) collective-permute-start(bf16[1024,1024]{1,0:T(8,128)(2,1)S(1)} %collective-permute-done.18.refs_2_), channel_id=1, source_target_pairs={{8,16},{16,24},{9,17},{17,25},{10,18},{18,26},{11,19},{19,27},{12,... | collective-permute-start | bytes 6291464 | tf_op jit(solution)/shard_map/ppermute | solution.py:267
  206.0 114.5 %collective-permute-start.25 = (bf16[1024,1024]{1,0:T(8,128)(2,1)S(1)}, bf16[1024,1024]{1,0:T(8,128)(2,1)S(1)}, u32[]{:S(2)}, u32[]{:S(2)}) collective-permute-start(bf16[1024,1024]{1,0:T(8,128)(2,1)S(1)} %collective-permute-done.23.refs_1_), channel_id=1, source_target_pairs={{8,0},{16,8},{9,1},{17,9},{10,2},{18,10},{11,3},{19,11},{12,4},{20... | collective-permute-start | bytes 6291464 | tf_op jit(solution)/shard_map/ppermute | solution.py:264
  206.8 114.5 %collective-permute-start.26 = (bf16[1024,1024]{1,0:T(8,128)(2,1)S(1)}, bf16[1024,1024]{1,0:T(8,128)(2,1)S(1)}, u32[]{:S(2)}, u32[]{:S(2)}) collective-permute-start(bf16[1024,1024]{1,0:T(8,128)(2,1)S(1)} %collective-permute-done.24.refs_2_), channel_id=1, source_target_pairs={{8,16},{16,24},{9,17},{17,25},{10,18},{18,26},{11,19},{19,27},{12,... | collective-permute-start | bytes 6291464 | tf_op jit(solution)/shard_map/ppermute | solution.py:267
  208.1 109.5 %collective-permute-start.14 = (bf16[512,1024]{1,0:T(8,128)(2,1)S(1)}, bf16[512,1024]{1,0:T(8,128)(2,1)S(1)}, u32[]{:S(2)}, u32[]{:S(2)}) collective-permute-start(bf16[512,1024]{1,0:T(8,128)(2,1)S(1)} %collective-permute-done.10.refs_2_), channel_id=1, source_target_pairs={{16,24},{17,25},{18,26},{19,27},{20,28},{21,29},{22,30},{23,31}} | collective-permute-start | bytes 3145736 | tf_op jit(solution)/shard_map/ppermute | solution.py:267
  317.6 5.0 %collective-permute-start.15 = (bf16[512,1024]{1,0:T(8,128)(2,1)S(1)}, bf16[512,1024]{1,0:T(8,128)(2,1)S(1)}, u32[]{:S(2)}, u32[]{:S(2)}) collective-permute-start(bf16[512,1024]{1,0:T(8,128)(2,1)S(1)} %collective-permute-done.11.refs_1_), channel_id=1, source_target_pairs={{8,0},{9,1},{10,2},{11,3},{12,4},{13,5},{14,6},{15,7}} | collective-permute-start | bytes 3145736 | tf_op jit(solution)/shard_map/ppermute | solution.py:264
  318.3 116.5 %collective-permute-start.21 = (bf16[1024,1024]{1,0:T(8,128)(2,1)S(1)}, bf16[1024,1024]{1,0:T(8,128)(2,1)S(1)}, u32[]{:S(2)}, u32[]{:S(2)}) collective-permute-start(bf16[1024,1024]{1,0:T(8,128)(2,1)S(1)} %collective-permute-done.19.refs_1_), channel_id=1, source_target_pairs={{8,0},{9,1},{10,2},{11,3},{12,4},{13,5},{14,6},{15,7}} | collective-permute-start | bytes 6291464 | tf_op jit(solution)/shard_map/ppermute | solution.py:264
  319.1 115.7 %collective-permute-start.22 = (bf16[1024,1024]{1,0:T(8,128)(2,1)S(1)}, bf16[1024,1024]{1,0:T(8,128)(2,1)S(1)}, u32[]{:S(2)}, u32[]{:S(2)}) collective-permute-start(bf16[1024,1024]{1,0:T(8,128)(2,1)S(1)} %collective-permute-done.20.refs_2_), channel_id=1, source_target_pairs={{16,24},{17,25},{18,26},{19,27},{20,28},{21,29},{22,30},{23,31}} | collective-permute-start | bytes 6291464 | tf_op jit(solution)/shard_map/ppermute | solution.py:267
  320.5 115.8 %collective-permute-start.27 = (bf16[1024,1024]{1,0:T(8,128)(2,1)S(1)}, bf16[1024,1024]{1,0:T(8,128)(2,1)S(1)}, u32[]{:S(2)}, u32[]{:S(2)}) collective-permute-start(bf16[1024,1024]{1,0:T(8,128)(2,1)S(1)} %collective-permute-done.25.refs_1_), channel_id=1, source_target_pairs={{8,0},{9,1},{10,2},{11,3},{12,4},{13,5},{14,6},{15,7}} | collective-permute-start | bytes 6291464 | tf_op jit(solution)/shard_map/ppermute | solution.py:264
  321.3 115.0 %collective-permute-start.28 = (bf16[1024,1024]{1,0:T(8,128)(2,1)S(1)}, bf16[1024,1024]{1,0:T(8,128)(2,1)S(1)}, u32[]{:S(2)}, u32[]{:S(2)}) collective-permute-start(bf16[1024,1024]{1,0:T(8,128)(2,1)S(1)} %collective-permute-done.26.refs_2_), channel_id=1, source_target_pairs={{16,24},{17,25},{18,26},{19,27},{20,28},{21,29},{22,30},{23,31}} | collective-permute-start | bytes 6291464 | tf_op jit(solution)/shard_map/ppermute | solution.py:267
  322.6 108.2 %collective-permute-start.16 = (bf16[512,1024]{1,0:T(8,128)(2,1)S(1)}, bf16[512,1024]{1,0:T(8,128)(2,1)S(1)}, u32[]{:S(2)}, u32[]{:S(2)}) collective-permute-start(bf16[512,1024]{1,0:T(8,128)(2,1)S(1)} %collective-permute-done.12.refs_2_), channel_id=1, source_target_pairs={{16,24},{17,25},{18,26},{19,27},{20,28},{21,29},{22,30},{23,31}} | collective-permute-start | bytes 3145736 | tf_op jit(solution)/shard_map/ppermute | solution.py:267
where the time goes:
time: 439 us; the launch traced here: 438 us
  waiting for transfers between devices  337 us (77%)
  starting transfers between devices  47.7 us (11%)
  Pallas kernels  34 us (8%)
  local copies, waits for them, and re-layouts  9.84 us (2%)
  blocking collectives  8.1 us (2%)
    ppermute x13, waiting for transfers between devices, right(): lax.ppermute(x, 'zero', [(i, i + 1) for i in range(hop - 1, count - 1)])  317 us
    ppermute x13, starting transfers between devices, left(): lax.ppermute(x, 'zero', [(i, i - 1) for i in range(1, count - hop + 1)])  28.9 us
    ppermute x13, starting transfers between devices, right(): lax.ppermute(x, 'zero', [(i, i + 1) for i in range(hop - 1, count - 1)])  16.8 us
    pallas_call x12, Pallas kernels, placed(): pl.pallas_call(functools.partial(place_kernel, plan, count, near), in_spe...  15.1 us
    ppermute x3, waiting for transfers between devices, merged_for_serving(): lax.ppermute(tops, 'zero', [(i, (i + s) % count) for i in range(count)])  14.9 us
    pallas_call x3, Pallas kernels, own_scaled(): pl.pallas_call(functools.partial(own_kernel, index), grid_spec=pltpu.Pref...  9.19 us
  transfers between devices with their start and end apart: 29, of which 8 were waited for; matrix products, arithmetic and copies ran while one was open for 0% of the time, Pallas kernels for 7%

commit v1 on v0

v1 whole, which is shorter than its diff:
```python
import functools

import jax
import jax.numpy as jnp
from jax import lax
from jax.experimental import pallas as pl
from jax.experimental.pallas import tpu as pltpu
from jax.sharding import PartitionSpec as P

mix_rate = 1.0


GRANT = 16 * 2**20

HBM = pltpu.MemorySpace.HBM
VMEM = pltpu.MemorySpace.VMEM


def tile_of(rows, most=256):
    tile = min(rows, most)
    while rows % tile:
        tile //= 2
    return tile


def merged(train, low_t, high):
    step = lax.dot_general(
        low_t, high, (((0,), (0,)), ((), ())), preferred_element_type=jnp.float32
    )
    return train.astype(jnp.float32) + mix_rate * step


def top_kernel(tq, tk, tv, lq, lk, lv, hq, hk, hv, norm, out, acc):
    step = pl.program_id(0)
    for index, (t, l, h) in enumerate(((tq, lq, hq), (tk, lk, hk), (tv, lv, hv))):
        size = jnp.abs(merged(t[...], l[...], h[...]))
        rows, cols = size.shape
        best = jnp.max(size.reshape(rows // 8, 8, cols), axis=0)

        @pl.when(step == 0)
        def _():
            acc[index] = best

        @pl.when(step > 0)
        def _():
            acc[index] = jnp.maximum(acc[index], best)

    @pl.when(step == pl.num_programs(0) - 1)
    def _():
        for index in range(3):
            out[pl.ds(index, 1), :] = jnp.max(acc[index], axis=0, keepdims=True)
        out[pl.ds(3, 1), :] = norm[...]


def column_tops(trains, lows, highs, norm):
    rows, cols = trains[0].shape
    rank = lows[0].shape[0]
    tile = tile_of(rows)
    return pl.pallas_call(
        top_kernel,
        grid=(rows // tile,),
        in_specs=[pl.BlockSpec((tile, cols), lambda i: (i, 0))] * 3
        + [pl.BlockSpec((rank, tile), lambda i: (0, i))] * 3
        + [pl.BlockSpec((rank, cols), lambda i: (0, 0))] * 3
        + [pl.BlockSpec((1, cols), lambda i: (0, 0))],
        out_specs=pl.BlockSpec((4, cols), lambda i: (0, 0)),
        out_shape=jax.ShapeDtypeStruct((4, cols), jnp.float32),
        scratch_shapes=[pltpu.VMEM((3, 8, cols), jnp.float32)],
        compiler_params=pltpu.CompilerParams(vmem_limit_bytes=GRANT),
        name="tops",
        cost_estimate=pl.CostEstimate(
            flops=3 * 2 * rows * cols * rank, bytes_accessed=6 * rows * cols, transcendentals=0
        ),
    )(*trains, *lows, *highs, norm)


def join_kernel(count, place, *refs):
    parts, (factor, norm) = refs[:count], refs[count:]
    total = parts[0][...]
    for part in parts[1:]:
        total = jnp.maximum(total, part[...])
    factor[...] = total
    for shift, part in enumerate(parts):
        owner = lax.rem(place[0] - shift + count, count)
        norm[pl.ds(owner, 1), :] = part[pl.ds(3, 1), :]


def join_tops(place, parts):
    count, cols = len(parts), parts[0].shape[1]
    return pl.pallas_call(
        functools.partial(join_kernel, count),
        in_specs=[pl.BlockSpec(memory_space=pltpu.MemorySpace.SMEM)]
        + [pl.BlockSpec(memory_space=VMEM)] * count,
        out_specs=[pl.BlockSpec(memory_space=VMEM)] * 2,
        out_shape=[
            jax.ShapeDtypeStruct((4, cols), jnp.float32),
            jax.ShapeDtypeStruct((max(8, count), cols), jnp.float32),
        ],
        compiler_params=pltpu.CompilerParams(vmem_limit_bytes=GRANT),
        name="join",
    )(place, *parts)


def scale_kernel(index, train, low_t, high, factor, serve):
    fresh = merged(train[...], low_t[...], high[...])
    serve[...] = (fresh / factor[pl.ds(index, 1), :]).astype(serve.dtype)


def scaled(index, train, low_t, high, factor, low_at=0):
    rows, cols = train.shape
    rank = high.shape[0]
    tile = tile_of(rows)
    first = low_at // tile
    return pl.pallas_call(
        functools.partial(scale_kernel, index),
        grid=(rows // tile,),
        in_specs=[
            pl.BlockSpec((tile, cols), lambda i: (i, 0)),
            pl.BlockSpec((rank, tile), lambda i: (0, i + first)),
            pl.BlockSpec((rank, cols), lambda i: (0, 0)),
            pl.BlockSpec((4, cols), lambda i: (0, 0)),
        ],
        out_specs=pl.BlockSpec((tile, cols), lambda i: (i, 0)),
        out_shape=jax.ShapeDtypeStruct((rows, cols), jnp.bfloat16),
        compiler_params=pltpu.CompilerParams(vmem_limit_bytes=GRANT),
        name="scale",
        cost_estimate=pl.CostEstimate(
            flops=2 * rows * cols * rank, bytes_accessed=4 * rows * cols, transcendentals=0
        ),
    )(train, low_t, high, factor)


def owner_of(mine, side, hop):
    return mine + hop * (1 - 2 * lax.rem(mine + side, 2))


def place_kernel(hop, sides, at, shard, count, place, *refs):
    sources, out, sems = refs[1 : 1 + len(sides)], refs[1 + len(sides)], refs[2 + len(sides)]
    for index, (side, source) in enumerate(zip(sides, sources)):
        owner = owner_of(place[0], side, hop)
        rows = source.shape[0]
        part = tile_of(rows)

        @pl.when((owner >= 0) & (owner < count))
        def _(index=index, source=source, owner=owner, rows=rows, part=part):
            stores = []
            for p, begin in enumerate(range(0, rows, part)):
                start = pl.multiple_of(owner * shard + at + begin, part)
                stores.append(
                    pltpu.make_async_copy(
                        source.at[pl.ds(begin, part)], out.at[pl.ds(start, part)], sems.at[index, p]
                    )
                )
                stores[-1].start()
            for store in stores:
                store.wait()


def placed(place, out, count, hop, at, shard, arrived):
    sides = tuple(side for side, _ in arrived)
    sources = [pltpu.with_memory_space_constraint(source, VMEM) for _, source in arrived]
    rows, size = sources[0].shape[0], sum(source.size for source in sources)
    return pl.pallas_call(
        functools.partial(place_kernel, hop, sides, at, shard, count),
        in_specs=[pl.BlockSpec(memory_space=pltpu.MemorySpace.SMEM)]
        + [pl.BlockSpec(memory_space=HBM)]
        + [pl.BlockSpec(memory_space=VMEM)] * len(sources),
        out_specs=pl.BlockSpec(memory_space=HBM),
        out_shape=jax.ShapeDtypeStruct(out.shape, out.dtype),
        scratch_shapes=[pltpu.SemaphoreType.DMA((len(sources), rows // tile_of(rows)))],
        input_output_aliases={1: 0},
        compiler_params=pltpu.CompilerParams(vmem_limit_bytes=GRANT),
        name="place",
        cost_estimate=pl.CostEstimate(flops=size, bytes_accessed=4 * size, transcendentals=0),
    )(place, out, *sources)


def own_kernel(index, first, place, train, low_t, high, factor, out, *serve):
    del place
    fresh = merged(train[...], low_t[...], high[...])
    block = (fresh / factor[pl.ds(index, 1), :]).astype(out.dtype)
    out[...] = block
    if serve:

        @pl.when(pl.program_id(0) >= first)
        def _():
            serve[0][...] = block


def own_scaled(index, place, count, train, low_t, high, factor, sent):
    rows, cols = train.shape
    rank = high.shape[0]
    tile = tile_of(rows)
    steps, first = rows // tile, sent // tile
    specs = [pl.BlockSpec((tile, cols), lambda i, place: (place[0] * steps + i, 0))]
    shapes = [jax.ShapeDtypeStruct((count * rows, cols), jnp.bfloat16)]
    if sent < rows:
        specs.append(pl.BlockSpec((tile, cols), lambda i, place: (jnp.maximum(i - first, 0), 0)))
        shapes.append(jax.ShapeDtypeStruct((rows - sent, cols), jnp.bfloat16))
    return pl.pallas_call(
        functools.partial(own_kernel, index, first),
        grid_spec=pltpu.PrefetchScalarGridSpec(
            num_scalar_prefetch=1,
            grid=(steps,),
            in_specs=[
                pl.BlockSpec((tile, cols), lambda i, place: (i, 0)),
                pl.BlockSpec((rank, tile), lambda i, place: (0, i)),
                pl.BlockSpec((rank, cols), lambda i, place: (0, 0)),
                pl.BlockSpec((4, cols), lambda i, place: (0, 0)),
            ],
            out_specs=specs,
        ),
        out_shape=shapes,
        compiler_params=pltpu.CompilerParams(vmem_limit_bytes=GRANT),
        name="own",
        cost_estimate=pl.CostEstimate(
            flops=2 * rows * cols * rank, bytes_accessed=6 * rows * cols, transcendentals=0
        ),
    )(place, train, low_t, high, factor)


def pairs_of(count, side, hop):
    pairs = []
    for i in range(count):
        to = i + 1 - 2 * ((i + side) % 2)
        owner = to + hop * (i - to)
        if 0 <= to < count and 0 <= owner < count:
            pairs.append((i, to))
    return pairs


def per_device(count, *operands):
    return merged_for_serving(count, *operands)


def merged_for_serving(
    count,
    train_query,
    low_query,
    high_query,
    train_key,
    low_key,
    high_key,
    train_value,
    low_value,
    high_value,
    norm_train,
    norm_step,
):
    rows, cols = train_query.shape
    half = rows // 2
    place = lax.axis_index("zero").astype(jnp.int32).reshape(1)
    lows = (low_query.T, low_key.T, low_value.T)
    highs = (high_query, high_key, high_value)
    trains = (train_query, train_key, train_value)

    def sent(hop, first, second):
        moved = []
        for side, x in ((0, first), (1, second)):
            pairs = pairs_of(count, side, hop)
            if pairs:
                moved.append((side, lax.ppermute(x, "zero", pairs)))
        return moved

    raw = {"q": sent(1, train_query, train_query)}
    norm = jnp.pad(norm_train + norm_step, (0, cols - norm_train.shape[0])).reshape(1, cols)
    tops = column_tops(trains, lows, highs, norm)
    parts = [tops]
    for s in range(1, count):
        parts.append(lax.ppermute(tops, "zero", [(i, (i + s) % count) for i in range(count)]))
    early = train_key[:half]
    raw["ka"] = sent(1, early, early)
    low = jnp.concatenate((lows[0], lows[1][:, :half]), axis=1)
    near = dict(sent(1, low, low))
    factor, norms = join_tops(place, parts)

    outs, serves = [None] * 3, [None] * 3
    for index, begin in ((1, half), (2, 0), (0, rows)):
        outs[index], *serves[index] = own_scaled(
            index, place, count, trains[index], lows[index], highs[index], factor, begin
        )
    pieces = []
    for name, index, low_at in (("q", 0, 0), ("ka", 1, rows)):
        arrived = []
        for side, got in raw[name]:
            arrived.append((side, scaled(index, got, near[side], highs[index], factor, low_at)))
        pieces.append((name, index, 0, arrived))
    for name, index, at in (("kb", 1, half), ("v", 2, 0)):
        pieces.append((name, index, at, sent(1, serves[index][0], serves[index][0])))

    for hop in range(1, count):
        later = []
        for name, index, at, arrived in pieces:
            if hop + 1 < count:
                brought = dict(arrived)
                later.append((name, index, at, sent(hop + 1, brought.get(1), brought.get(0))))
            outs[index] = placed(place, outs[index], count, hop, at, rows, arrived)
        pieces = later

    size = norm_train.shape[0]
    wide = lax.all_gather(norms[:count, :size].astype(jnp.bfloat16), "width", axis=1, tiled=True)
    serve_norm = wide.reshape(-1)
    return (*outs, factor[0], factor[1], factor[2], serve_norm)


def solution(mesh):
    count = mesh.shape["zero"]
    return jax.shard_map(
        functools.partial(per_device, count),
        mesh=mesh,
        in_specs=(
            P(("unit", "zero"), "width"),
            P(("unit", "zero"), None),
            P("unit", "width"),
            P(("unit", "zero"), "width"),
            P(("unit", "zero"), None),
            P("unit", "width"),
            P(("unit", "zero"), "width"),
            P(("unit", "zero"), None),
            P("unit", "width"),
            P(("unit", "zero", "width")),
            P(("unit", "zero", "width")),
        ),
        out_specs=(
            P("unit", "width"),
            P("unit", "width"),
            P("unit", "width"),
            P(("unit", "width")),
            P(("unit", "width")),
            P(("unit", "width")),
            P("unit"),
        ),
        check_vma=False,
    )
```

time: 439 us -> 531 us (1.21)
  the two profiles are of different devices: /device:TPU:24 before, /device:TPU:0 now
where the time goes in v1:
time: 531 us; the launch traced here: 530 us
  waiting for transfers between devices  445 us (84%)
  starting transfers between devices  32.4 us (6%)
  Pallas kernels  30.3 us (6%)
  local copies, waits for them, and re-layouts  11.4 us (2%)
  blocking collectives  8.1 us (2%)
    ppermute x22, waiting for transfers between devices, sent(): moved.append((side, lax.ppermute(x, 'zero', pairs)))  444 us
    ppermute x22, starting transfers between devices, sent(): moved.append((side, lax.ppermute(x, 'zero', pairs)))  25.5 us
    pallas_call x12, Pallas kernels, placed(): pl.pallas_call(functools.partial(place_kernel, hop, sides, at, shard, cou...  14.3 us
  transfers between devices with their start and end apart: 25, of which 8 were waited for; matrix products, arithmetic and copies ran while one was open for 0% of the time, Pallas kernels for 5%

profile of v1, /device:TPU:0, one launch (start us, length us, event | category | flops | bytes accessed | tf_op | source)
XLA Modules:
  0.0 529.8 jit_solution(2974230820106764041)
XLA Ops:
  2.1 3.1 collective-permute-start.4
  6.5 1.6 copy-done
  8.1 1.6 copy-done.2
  9.7 1.6 copy-done.4
  15.9 4.0 tops.1.refs_0_
  19.9 4.5 collective-permute-start
  24.3 2.4 collective-permute-start.2
  26.9 1.2 collective-permute-start.10
  28.1 1.0 collective-permute-done.1.refs_2_
  29.8 2.2 collective-permute-start.3
  32.0 2.7 own.4
  34.7 2.7 own.5
  37.4 2.0 collective-permute-start.20
  39.4 13.5 %collective-permute-done.10.train = bf16[512,1024]{1,0:T(8,128)(2,1)S(1)} collective-permute-done((bf16[512,1024]{1,0:T(8,128)(2,1)S(1)}, bf16[512,1024]{1,0:T(8,128)(2,1)S(1)}, u32[]{:S(2)}, u32[]{:S(2)}) %collective-permute-start.10) | collective-permute-done | bytes 1048608 | tf_op jit(solution)/shard_map/ppermute | solution.py:262
  53.7 0.8 collective-permute-start.5
  55.2 65.2 %collective-permute-done.12.refs_1_ = bf16[512,1024]{1,0:T(8,128)(2,1)S(1)} collective-permute-done((bf16[512,1024]{1,0:T(8,128)(2,1)S(1)}, bf16[512,1024]{1,0:T(8,128)(2,1)S(1)}, u32[]{:S(2)}, u32[]{:S(2)}) %collective-permute-start.12) | collective-permute-done | bytes 1048608 | tf_op jit(solution)/shard_map/ppermute | solution.py:262
  121.8 1.3 collective-permute-start.14
  123.1 0.8 collective-permute-start.21
  123.9 1.4 scale.4.refs_1_
  125.3 0.8 collective-permute-start.8
  126.1 39.2 %collective-permute-done.20.refs_1_ = bf16[1024,1024]{1,0:T(8,128)(2,1)S(1)} collective-permute-done((bf16[1024,1024]{1,0:T(8,128)(2,1)S(1)}, bf16[1024,1024]{1,0:T(8,128)(2,1)S(1)}, u32[]{:S(2)}, u32[]{:S(2)}) %collective-permute-start.20) | collective-permute-done | bytes 2097184 | tf_op jit(solution)/shard_map/ppermute | solution.py:262
  165.3 0.8 collective-permute-start.23
  166.1 19.6 %collective-permute-done.14.refs_1_ = bf16[512,1024]{1,0:T(8,128)(2,1)S(1)} collective-permute-done((bf16[512,1024]{1,0:T(8,128)(2,1)S(1)}, bf16[512,1024]{1,0:T(8,128)(2,1)S(1)}, u32[]{:S(2)}, u32[]{:S(2)}) %collective-permute-start.14) | collective-permute-done | bytes 1048608 | tf_op jit(solution)/shard_map/ppermute | solution.py:262
  186.4 1.3 collective-permute-start.16
  187.8 1.3 collective-permute-start.18
  189.1 1.3 scale.5.refs_2_
  190.4 21.0 %collective-permute-done.16.refs_1_ = bf16[512,1024]{1,0:T(8,128)(2,1)S(1)} collective-permute-done((bf16[512,1024]{1,0:T(8,128)(2,1)S(1)}, bf16[512,1024]{1,0:T(8,128)(2,1)S(1)}, u32[]{:S(2)}, u32[]{:S(2)}) %collective-permute-start.16) | collective-permute-done | bytes 1048608 | tf_op jit(solution)/shard_map/ppermute | solution.py:262
  211.4 1.3 collective-permute-start.7
  212.7 1.3 collective-permute-start.22
  214.0 1.3 collective-permute-start.9
  215.4 1.3 collective-permute-start.24
  216.7 110.1 %collective-permute-done.18.refs_1_ = bf16[512,1024]{1,0:T(8,128)(2,1)S(1)} collective-permute-done((bf16[512,1024]{1,0:T(8,128)(2,1)S(1)}, bf16[512,1024]{1,0:T(8,128)(2,1)S(1)}, u32[]{:S(2)}, u32[]{:S(2)}) %collective-permute-start.18) | collective-permute-done | bytes 1048608 | tf_op jit(solution)/shard_map/ppermute | solution.py:262
  326.8 1.3 collective-permute-start.19
  328.1 8.1 %all_gather.3 = bf16[4,1024]{1,0:T(4,128)(2,1)S(1)} all-gather(bf16[4,256]{1,0:T(4,128)(2,1)S(1)} %slice.28), channel_id=1, replica_groups=mesh['zero'=4,'width'=4,'unit'=2] {'width'}, dimensions={1}, use_global_device_ids=true | all-gather | bytes 10240 | tf_op jit(solution)/shard_map/all_gather | solution.py:301
  336.8 2.6 own.3.refs_0_
  340.0 1.0 place.15.refs_0_
  341.0 1.0 place.16.refs_0_
  342.0 1.0 place.17.refs_0_
  343.0 1.4 place.12.refs_0_
  344.4 1.0 place.18.refs_0_
  345.5 1.4 place.21.refs_0_
  346.9 1.0 place.19.refs_0_
  347.9 175.4 %collective-permute-done.19.refs_1_ = bf16[512,1024]{1,0:T(8,128)(2,1)S(1)} collective-permute-done((bf16[512,1024]{1,0:T(8,128)(2,1)S(1)}, bf16[512,1024]{1,0:T(8,128)(2,1)S(1)}, u32[]{:S(2)}, u32[]{:S(2)}) %collective-permute-start.19) | collective-permute-done | bytes 1048608 | tf_op jit(solution)/shard_map/ppermute | solution.py:262
  523.3 1.0 place.20
  524.3 1.4 place.13.refs_0_
  525.7 1.4 place.22.refs_0_
  527.1 1.4 place.14
  528.4 1.4 place.23
  (68 shorter events, 13.1 us)
Async XLA Ops:
  2.1 32.6 %collective-permute-start.4 = (bf16[16,1536]{1,0:T(8,128)(2,1)S(1)}, bf16[16,1536]{1,0:T(8,128)(2,1)S(1)}, u32[]{:S(2)}, u32[]{:S(2)}) collective-permute-start(bf16[16,1536]{1,0:T(8,128)(2,1)S(1)} %pad_maximum_fusion), channel_id=1, source_target_pairs={{0,8},{8,0},{16,24},{24,16},{1,9},{9,1},{17,25},{25,17},{2,10},{10... | collective-permute-start | bytes 147464 | tf_op jit(solution)/shard_map/ppermute | solution.py:262
  5.2 32.3 %collective-permute-start.6 = (bf16[16,1536]{1,0:T(8,128)(2,1)S(1)}, bf16[16,1536]{1,0:T(8,128)(2,1)S(1)}, u32[]{:S(2)}, u32[]{:S(2)}) collective-permute-start(bf16[16,1536]{1,0:T(8,128)(2,1)S(1)} %pad_maximum_fusion), channel_id=1, source_target_pairs={{8,16},{16,8},{9,17},{17,9},{10,18},{18,10},{11,19},{19,11},{12,20... | collective-permute-start | bytes 147464 | tf_op jit(solution)/shard_map/ppermute | solution.py:262
  6.5 1.6 copy-start
  8.1 1.6 copy-start.2
  9.7 1.6 copy-start.4
  11.3 0.8 copy-start.6
  12.1 0.8 copy-start.8
  12.8 0.8 copy-start.10
  13.6 0.8 copy-start.12
  14.3 0.8 copy-start.14
  15.1 0.8 copy-start.16
  19.8 12.2 %copy-start.1 = (bf16[1024,1024]{1,0:T(8,128)(2,1)S(1)}, bf16[1024,1024]{1,0:T(8,128)(2,1)}, u32[]{:S(2)}) copy-start(bf16[1024,1024]{1,0:T(8,128)(2,1)} %train.4) | copy-start | bytes 6291460
  19.8 12.2 %copy-start.7 = (bf16[16,1024]{1,0:T(8,128)(2,1)S(1)}, bf16[16,1024]{1,0:T(8,128)(2,1)}, u32[]{:S(2)}) copy-start(bf16[16,1024]{1,0:T(8,128)(2,1)} %high.12) | copy-start | bytes 98308
  19.9 12.2 %copy-start.13 = (bf16[1024,16]{0,1:T(8,128)(2,1)S(1)}, bf16[1024,16]{0,1:T(8,128)(2,1)}, u32[]{:S(2)}) copy-start(bf16[1024,16]{0,1:T(8,128)(2,1)} %param.15) | copy-start | bytes 98308
  19.9 7.0 %collective-permute-start = (f32[4,1024]{1,0:T(4,128)S(1)}, f32[4,1024]{1,0:T(4,128)S(1)}, u32[]{:S(2)}, u32[]{:S(2)}) collective-permute-start(f32[4,1024]{1,0:T(4,128)S(1)} %tops.1.refs_0_), channel_id=1, source_target_pairs={{0,8},{8,16},{16,24},{24,0},{1,9},{9,17},{17,25},{25,1},{2,10},{10... | collective-permute-start | bytes 49160 | tf_op jit(solution)/shard_map/ppermute | solution.py:270
  24.3 4.7 collective-permute-start.1
  24.3 5.5 %collective-permute-start.2 = (f32[4,1024]{1,0:T(4,128)S(1)}, f32[4,1024]{1,0:T(4,128)S(1)}, u32[]{:S(2)}, u32[]{:S(2)}) collective-permute-start(f32[4,1024]{1,0:T(4,128)S(1)} %tops.1.refs_0_), channel_id=1, source_target_pairs={{0,24},{8,0},{16,8},{24,16},{1,25},{9,1},{17,9},{25,17},{2,26},{10... | collective-permute-start | bytes 49160 | tf_op jit(solution)/shard_map/ppermute | solution.py:270
  26.8 8.0 %copy-start.15 = (bf16[1024,16]{0,1:T(8,128)(2,1)S(1)}, bf16[1024,16]{0,1:T(8,128)(2,1)}, u32[]{:S(2)}) copy-start(bf16[1024,16]{0,1:T(8,128)(2,1)} %param.18) | copy-start | bytes 98308
  26.8 8.0 %copy-start.17 = (bf16[16,1024]{1,0:T(8,128)(2,1)S(1)}, bf16[16,1024]{1,0:T(8,128)(2,1)}, u32[]{:S(2)}) copy-start(bf16[16,1024]{1,0:T(8,128)(2,1)} %high.13) | copy-start | bytes 98308
  26.8 7.9 %copy-start.3 = (bf16[1024,1024]{1,0:T(8,128)(2,1)S(1)}, bf16[1024,1024]{1,0:T(8,128)(2,1)}, u32[]{:S(2)}) copy-start(bf16[1024,1024]{1,0:T(8,128)(2,1)} %train.5) | copy-start | bytes 6291460
  26.9 26.1 %collective-permute-start.10 = (bf16[512,1024]{1,0:T(8,128)(2,1)S(1)}, bf16[512,1024]{1,0:T(8,128)(2,1)S(1)}, u32[]{:S(2)}, u32[]{:S(2)}) collective-permute-start(bf16[512,1024]{1,0:T(8,128)(2,1)S(1)} %slice.20), channel_id=1, source_target_pairs={{0,8},{8,0},{16,24},{24,16},{1,9},{9,1},{17,25},{25,17},{2,10},{10... | collective-permute-start | bytes 3145736 | tf_op jit(solution)/shard_map/ppermute | solution.py:262
  29.1 24.6 %collective-permute-start.11 = (bf16[512,1024]{1,0:T(8,128)(2,1)S(1)}, bf16[512,1024]{1,0:T(8,128)(2,1)S(1)}, u32[]{:S(2)}, u32[]{:S(2)}) collective-permute-start(bf16[512,1024]{1,0:T(8,128)(2,1)S(1)} %slice.20), channel_id=1, source_target_pairs={{8,16},{16,8},{9,17},{17,9},{10,18},{18,10},{11,19},{19,11},{12,20... | collective-permute-start | bytes 3145736 | tf_op jit(solution)/shard_map/ppermute | solution.py:262
  29.8 93.3 %collective-permute-start.3 = (bf16[1024,1024]{1,0:T(8,128)(2,1)}, bf16[1024,1024]{1,0:T(8,128)(2,1)S(1)}, u32[]{:S(2)}, u32[]{:S(2)}) collective-permute-start(bf16[1024,1024]{1,0:T(8,128)(2,1)} %train.3), channel_id=1, source_target_pairs={{0,8},{8,0},{16,24},{24,16},{1,9},{9,1},{17,25},{25,17},{2,10},{10... | collective-permute-start | bytes 6291464 | tf_op jit(solution)/shard_map/ppermute | solution.py:262
  32.0 21.7 %copy-start.5 = (bf16[1024,1024]{1,0:T(8,128)(2,1)S(1)}, bf16[1024,1024]{1,0:T(8,128)(2,1)}, u32[]{:S(2)}) copy-start(bf16[1024,1024]{1,0:T(8,128)(2,1)} %train.3) | copy-start | bytes 6291460
  34.7 85.7 %collective-permute-start.12 = (bf16[512,1024]{1,0:T(8,128)(2,1)S(1)}, bf16[512,1024]{1,0:T(8,128)(2,1)S(1)}, u32[]{:S(2)}, u32[]{:S(2)}) collective-permute-start(bf16[512,1024]{1,0:T(8,128)(2,1)S(1)} %get-tuple-element.15), channel_id=1, source_target_pairs={{0,8},{8,0},{16,24},{24,16},{1,9},{9,1},{17,25},{25,17},{2,10},{10... | collective-permute-start | bytes 3145736 | tf_op jit(solution)/shard_map/ppermute | solution.py:262
  37.4 86.5 %copy-start.9 = (bf16[16,1024]{1,0:T(8,128)(2,1)S(1)}, bf16[16,1024]{1,0:T(8,128)(2,1)}, u32[]{:S(2)}) copy-start(bf16[16,1024]{1,0:T(8,128)(2,1)} %high.9) | copy-start | bytes 98308
  37.4 127.9 %collective-permute-start.20 = (bf16[1024,1024]{1,0:T(8,128)(2,1)S(1)}, bf16[1024,1024]{1,0:T(8,128)(2,1)S(1)}, u32[]{:S(2)}, u32[]{:S(2)}) collective-permute-start(bf16[1024,1024]{1,0:T(8,128)(2,1)S(1)} %get-tuple-element.17), channel_id=1, source_target_pairs={{0,8},{8,0},{16,24},{24,16},{1,9},{9,1},{17,25},{25,17},{2,10},{10... | collective-permute-start | bytes 6291464 | tf_op jit(solution)/shard_map/ppermute | solution.py:262
  53.0 68.8 %collective-permute-start.13 = (bf16[512,1024]{1,0:T(8,128)(2,1)S(1)}, bf16[512,1024]{1,0:T(8,128)(2,1)S(1)}, u32[]{:S(2)}, u32[]{:S(2)}) collective-permute-start(bf16[512,1024]{1,0:T(8,128)(2,1)S(1)} %get-tuple-element.15), channel_id=1, source_target_pairs={{8,16},{16,8},{9,17},{17,9},{10,18},{18,10},{11,19},{19,11},{12,20... | collective-permute-start | bytes 3145736 | tf_op jit(solution)/shard_map/ppermute | solution.py:262
  53.7 132.7 %collective-permute-start.5 = (bf16[1024,1024]{1,0:T(8,128)(2,1)S(1)}, bf16[1024,1024]{1,0:T(8,128)(2,1)S(1)}, u32[]{:S(2)}, u32[]{:S(2)}) collective-permute-start(bf16[1024,1024]{1,0:T(8,128)(2,1)S(1)} %copy-done.5), channel_id=1, source_target_pairs={{8,16},{16,8},{9,17},{17,9},{10,18},{18,10},{11,19},{19,11},{12,20... | collective-permute-start | bytes 6291464 | tf_op jit(solution)/shard_map/ppermute | solution.py:262
  120.4 4.9 collective-permute-start.15
  121.8 63.9 %collective-permute-start.14 = (bf16[512,1024]{1,0:T(8,128)(2,1)S(1)}, bf16[512,1024]{1,0:T(8,128)(2,1)S(1)}, u32[]{:S(2)}, u32[]{:S(2)}) collective-permute-start(bf16[512,1024]{1,0:T(8,128)(2,1)S(1)} %scale.7.refs_2_), channel_id=1, source_target_pairs={{8,0},{16,24},{9,1},{17,25},{10,2},{18,26},{11,3},{19,27},{12,4},{... | collective-permute-start | bytes 3145736 | tf_op jit(solution)/shard_map/ppermute | solution.py:262
  123.1 89.6 %collective-permute-start.21 = (bf16[1024,1024]{1,0:T(8,128)(2,1)S(1)}, bf16[1024,1024]{1,0:T(8,128)(2,1)S(1)}, u32[]{:S(2)}, u32[]{:S(2)}) collective-permute-start(bf16[1024,1024]{1,0:T(8,128)(2,1)S(1)} %get-tuple-element.17), channel_id=1, source_target_pairs={{8,16},{16,8},{9,17},{17,9},{10,18},{18,10},{11,19},{19,11},{12,20... | collective-permute-start | bytes 6291464 | tf_op jit(solution)/shard_map/ppermute | solution.py:262
  125.3 211.5 %copy-start.11 = (bf16[1024,16]{0,1:T(8,128)(2,1)S(1)}, bf16[1024,16]{0,1:T(8,128)(2,1)}, u32[]{:S(2)}) copy-start(bf16[1024,16]{0,1:T(8,128)(2,1)} %param.12) | copy-start | bytes 98308
  125.3 88.7 %collective-permute-start.8 = (bf16[1024,1024]{1,0:T(8,128)(2,1)S(1)}, bf16[1024,1024]{1,0:T(8,128)(2,1)S(1)}, u32[]{:S(2)}, u32[]{:S(2)}) collective-permute-start(bf16[1024,1024]{1,0:T(8,128)(2,1)S(1)} %scale.4.refs_1_), channel_id=1, source_target_pairs={{8,16},{16,8},{9,17},{17,9},{10,18},{18,10},{11,19},{19,11},{12,20... | collective-permute-start | bytes 6291464 | tf_op jit(solution)/shard_map/ppermute | solution.py:262
  165.3 50.0 %collective-permute-start.23 = (bf16[1024,1024]{1,0:T(8,128)(2,1)S(1)}, bf16[1024,1024]{1,0:T(8,128)(2,1)S(1)}, u32[]{:S(2)}, u32[]{:S(2)}) collective-permute-start(bf16[1024,1024]{1,0:T(8,128)(2,1)S(1)} %collective-permute-done.20.refs_1_), channel_id=1, source_target_pairs={{8,16},{16,8},{9,17},{17,9},{10,18},{18,10},{11,19},{19,11},{12,20... | collective-permute-start | bytes 6291464 | tf_op jit(solution)/shard_map/ppermute | solution.py:262
  185.7 2.0 collective-permute-start.17
  186.4 25.0 %collective-permute-start.16 = (bf16[512,1024]{1,0:T(8,128)(2,1)S(1)}, bf16[512,1024]{1,0:T(8,128)(2,1)S(1)}, u32[]{:S(2)}, u32[]{:S(2)}) collective-permute-start(bf16[512,1024]{1,0:T(8,128)(2,1)S(1)} %collective-permute-done.13.refs_2_), channel_id=1, source_target_pairs={{8,0},{16,24},{9,1},{17,25},{10,2},{18,26},{11,3},{19,27},{12,4},{... | collective-permute-start | bytes 3145736 | tf_op jit(solution)/shard_map/ppermute | solution.py:262
  187.8 139.0 %collective-permute-start.18 = (bf16[512,1024]{1,0:T(8,128)(2,1)S(1)}, bf16[512,1024]{1,0:T(8,128)(2,1)S(1)}, u32[]{:S(2)}, u32[]{:S(2)}) collective-permute-start(bf16[512,1024]{1,0:T(8,128)(2,1)S(1)} %collective-permute-done.15.refs_2_), channel_id=1, source_target_pairs={{8,0},{16,24},{9,1},{17,25},{10,2},{18,26},{11,3},{19,27},{12,4},{... | collective-permute-start | bytes 3145736 | tf_op jit(solution)/shard_map/ppermute | solution.py:262
  211.4 312.8 %collective-permute-start.7 = (bf16[1024,1024]{1,0:T(8,128)(2,1)S(1)}, bf16[1024,1024]{1,0:T(8,128)(2,1)S(1)}, u32[]{:S(2)}, u32[]{:S(2)}) collective-permute-start(bf16[1024,1024]{1,0:T(8,128)(2,1)S(1)} %scale.5.refs_2_), channel_id=1, source_target_pairs={{8,0},{16,24},{9,1},{17,25},{10,2},{18,26},{11,3},{19,27},{12,4},{... | collective-permute-start | bytes 6291464 | tf_op jit(solution)/shard_map/ppermute | solution.py:262
  212.7 312.9 %collective-permute-start.22 = (bf16[1024,1024]{1,0:T(8,128)(2,1)S(1)}, bf16[1024,1024]{1,0:T(8,128)(2,1)S(1)}, u32[]{:S(2)}, u32[]{:S(2)}) collective-permute-start(bf16[1024,1024]{1,0:T(8,128)(2,1)S(1)} %collective-permute-done.21.refs_2_), channel_id=1, source_target_pairs={{8,0},{16,24},{9,1},{17,25},{10,2},{18,26},{11,3},{19,27},{12,4},{... | collective-permute-start | bytes 6291464 | tf_op jit(solution)/shard_map/ppermute | solution.py:262
  214.0 313.0 %collective-permute-start.9 = (bf16[1024,1024]{1,0:T(8,128)(2,1)S(1)}, bf16[1024,1024]{1,0:T(8,128)(2,1)S(1)}, u32[]{:S(2)}, u32[]{:S(2)}) collective-permute-start(bf16[1024,1024]{1,0:T(8,128)(2,1)S(1)} %collective-permute-done.8.refs_2_), channel_id=1, source_target_pairs={{8,0},{16,24},{9,1},{17,25},{10,2},{18,26},{11,3},{19,27},{12,4},{... | collective-permute-start | bytes 6291464 | tf_op jit(solution)/shard_map/ppermute | solution.py:262
  215.4 313.1 %collective-permute-start.24 = (bf16[1024,1024]{1,0:T(8,128)(2,1)S(1)}, bf16[1024,1024]{1,0:T(8,128)(2,1)S(1)}, u32[]{:S(2)}, u32[]{:S(2)}) collective-permute-start(bf16[1024,1024]{1,0:T(8,128)(2,1)S(1)} %collective-permute-done.23.refs_2_), channel_id=1, source_target_pairs={{8,0},{16,24},{9,1},{17,25},{10,2},{18,26},{11,3},{19,27},{12,4},{... | collective-permute-start | bytes 6291464 | tf_op jit(solution)/shard_map/ppermute | solution.py:262
  326.8 196.5 %collective-permute-start.19 = (bf16[512,1024]{1,0:T(8,128)(2,1)S(1)}, bf16[512,1024]{1,0:T(8,128)(2,1)S(1)}, u32[]{:S(2)}, u32[]{:S(2)}) collective-permute-start(bf16[512,1024]{1,0:T(8,128)(2,1)S(1)} %collective-permute-done.17.refs_2_), channel_id=1, source_target_pairs={{8,0},{16,24},{9,1},{17,25},{10,2},{18,26},{11,3},{19,27},{12,4},{... | collective-permute-start | bytes 3145736 | tf_op jit(solution)/shard_map/ppermute | solution.py:262

commit v2 on v1

--- a/solution.py
+++ b/solution.py
@@ -1,4 +1,5 @@
 import functools
+import math
 
 import jax
 import jax.numpy as jnp
@@ -190,7 +191,7 @@
 def own_scaled(index, place, count, train, low_t, high, factor, sent):
     rows, cols = train.shape
     rank = high.shape[0]
-    tile = tile_of(rows)
+    tile = tile_of(math.gcd(rows, sent))
     steps, first = rows // tile, sent // tile
     specs = [pl.BlockSpec((tile, cols), lambda i, place: (place[0] * steps + i, 0))]
     shapes = [jax.ShapeDtypeStruct((count * rows, cols), jnp.bfloat16)]
@@ -271,7 +272,18 @@
     early = train_key[:half]
     raw["ka"] = sent(1, early, early)
     low = jnp.concatenate((lows[0], lows[1][:, :half]), axis=1)
+    whole = low.shape[1]
+    devices = lax.axis_size("width")
+    shared = whole % devices == 0
+    if shared:
+        part = whole // devices
+        low = lax.dynamic_slice_in_dim(low, lax.axis_index("width") * part, part, axis=1)
     near = dict(sent(1, low, low))
+    sides = sorted(near)
+    joined = jnp.stack([near[side] for side in sides])
+    if shared:
+        joined = lax.all_gather(joined, "width", axis=2, tiled=True)
+    near = {side: joined[index] for index, side in enumerate(sides)}
     factor, norms = join_tops(place, parts)
 
     outs, serves = [None] * 3, [None] * 3
@@ -285,8 +297,13 @@
         for side, got in raw[name]:
             arrived.append((side, scaled(index, got, near[side], highs[index], factor, low_at)))
         pieces.append((name, index, 0, arrived))
-    for name, index, at in (("kb", 1, half), ("v", 2, 0)):
-        pieces.append((name, index, at, sent(1, serves[index][0], serves[index][0])))
+    cut = rows * 3 // 4
+    for name, index, at, ready in (
+        ("kb", 1, half, serves[1][0]),
+        ("v", 2, 0, serves[2][0][:cut]),
+        ("w", 2, cut, serves[2][0][cut:]),
+    ):
+        pieces.append((name, index, at, sent(1, ready, ready)))
 
     for hop in range(1, count):
         later = []

time: 531 us -> 511 us (0.962)
  waiting for transfers between devices: 445 us -> 402 us
  starting transfers between devices: 32.4 us -> 44.1 us
  blocking collectives: 8.1 us -> 16.6 us
    ppermute x22 -> x27, waiting for transfers between devices: 444 us -> 402 us  [sent(): moved.append((side, lax.ppermute(x, 'zero', pairs)))]
    ppermute x22 -> x27, starting transfers between devices: 25.5 us -> 37.1 us  [sent(): moved.append((side, lax.ppermute(x, 'zero', pairs)))]
    all_gather x0 -> x1, blocking collectives: none -> 8.46 us  [merged_for_serving(): joined = lax.all_gather(joined, 'width', axis=2, tiled=True)]
    pallas_call x12 -> x15, Pallas kernels: 14.3 us -> 16.2 us  [placed(): pl.pallas_call(functools.partial(place_kernel, hop, sides, at, shard, cou...]
  transfers between devices with their start and end apart: 25 -> 30, of which waited for: 8 -> 10; matrix products, arithmetic and copies ran while one was open for 0% -> 0% of each run, Pallas kernels for 5% -> 5%
where the time goes in v2:
time: 511 us; the launch traced here: 510 us
  waiting for transfers between devices  402 us (79%)
  starting transfers between devices  44.1 us (9%)
  Pallas kernels  32.2 us (6%)
  blocking collectives  16.6 us (3%)
  local copies, waits for them, and re-layouts  13.4 us (3%)
    ppermute x27, waiting for transfers between devices, sent(): moved.append((side, lax.ppermute(x, 'zero', pairs)))  402 us
    ppermute x27, starting transfers between devices, sent(): moved.append((side, lax.ppermute(x, 'zero', pairs)))  37.1 us
    pallas_call x15, Pallas kernels, placed(): pl.pallas_call(functools.partial(place_kernel, hop, sides, at, shard, cou...  16.2 us
    unnamed x37, local copies, waits for them, and re-layouts  11.5 us
  transfers between devices with their start and end apart: 30, of which 10 were waited for; matrix products, arithmetic and copies ran while one was open for 0% of the time, Pallas kernels for 5%

profile of v2, /device:TPU:0, one launch (start us, length us, event | category | flops | bytes accessed | tf_op | source)
XLA Modules:
  0.0 509.8 jit_solution(5058013758340396561)
XLA Ops:
  1.3 1.6 copy-done
  2.9 1.6 copy-done.2
  4.5 1.6 copy-done.4
  10.7 4.0 tops.1.refs_0_
  14.7 3.1 collective-permute-start
  17.8 2.6 collective-permute-start.1
  20.4 1.3 collective-permute-start.2
  21.8 1.0 slice.34
  23.5 1.4 collective-permute-start.4
  26.4 1.6 copy-done.3
  28.0 2.7 own.5
  30.7 5.2 %collective-permute-start.22 = (bf16[256,1024]{1,0:T(8,128)(2,1)S(1)}, bf16[256,1024]{1,0:T(8,128)(2,1)S(1)}, u32[]{:S(2)}, u32[]{:S(2)}) collective-permute-start(bf16[256,1024]{1,0:T(8,128)(2,1)S(1)} %slice.36), channel_id=1, source_target_pairs={{0,8},{8,0},{16,24},{24,16},{1,9},{9,1},{17,25},{25,17},{2,10},{10... | collective-permute-start | bytes 1572872 | tf_op jit(solution)/shard_map/ppermute | solution.py:263
  35.9 13.4 %collective-permute-done.4 = bf16[16,384]{1,0:T(8,128)(2,1)S(1)} collective-permute-done((bf16[16,384]{1,0:T(8,128)(2,1)S(1)}, bf16[16,384]{1,0:T(8,128)(2,1)S(1)}, u32[]{:S(2)}, u32[]{:S(2)}) %collective-permute-start.4) | collective-permute-done | bytes 12320 | tf_op jit(solution)/shard_map/ppermute | solution.py:263
  50.7 9.9 %collective-permute-done.22.refs_1_ = bf16[256,1024]{1,0:T(8,128)(2,1)S(1)} collective-permute-done((bf16[256,1024]{1,0:T(8,128)(2,1)S(1)}, bf16[256,1024]{1,0:T(8,128)(2,1)S(1)}, u32[]{:S(2)}, u32[]{:S(2)}) %collective-permute-start.22) | collective-permute-done | bytes 524320 | tf_op jit(solution)/shard_map/ppermute | solution.py:263
  61.4 5.6 %collective-permute-start.20 = (bf16[768,1024]{1,0:T(8,128)(2,1)S(1)}, bf16[768,1024]{1,0:T(8,128)(2,1)S(1)}, u32[]{:S(2)}, u32[]{:S(2)}) collective-permute-start(bf16[768,1024]{1,0:T(8,128)(2,1)S(1)} %slice.35), channel_id=1, source_target_pairs={{0,8},{8,0},{16,24},{24,16},{1,9},{9,1},{17,25},{25,17},{2,10},{10... | collective-permute-start | bytes 4718600 | tf_op jit(solution)/shard_map/ppermute | solution.py:263
  66.9 1.3 collective-permute-start.26
  68.3 2.7 own.4
  70.9 2.7 collective-permute-start.12
  74.3 76.1 %collective-permute-done.26.refs_1_ = bf16[256,1024]{1,0:T(8,128)(2,1)S(1)} collective-permute-done((bf16[256,1024]{1,0:T(8,128)(2,1)S(1)}, bf16[256,1024]{1,0:T(8,128)(2,1)S(1)}, u32[]{:S(2)}, u32[]{:S(2)}) %collective-permute-start.26) | collective-permute-done | bytes 524320 | tf_op jit(solution)/shard_map/ppermute | solution.py:263
  151.2 8.5 %all_gather.6 = bf16[2,16,1536]{2,1,0:T(8,128)(2,1)S(1)} all-gather(bf16[2,16,384]{2,1,0:T(8,128)(2,1)S(1)} %pad_maximum_fusion), channel_id=1, replica_groups=mesh['zero'=4,'width'=4,'unit'=2] {'width'}, dimensions={2}, use_global_device_ids=true | all-gather | bytes 122880 | tf_op jit(solution)/shard_map/all_gather | solution.py:285
  160.4 10.6 %collective-permute-done.12.refs_1_ = bf16[512,1024]{1,0:T(8,128)(2,1)S(1)} collective-permute-done((bf16[512,1024]{1,0:T(8,128)(2,1)S(1)}, bf16[512,1024]{1,0:T(8,128)(2,1)S(1)}, u32[]{:S(2)}, u32[]{:S(2)}) %collective-permute-start.12) | collective-permute-done | bytes 1048608 | tf_op jit(solution)/shard_map/ppermute | solution.py:263
  173.2 1.3 collective-permute-start.14
  174.5 1.4 scale.4.refs_1_
  178.2 21.0 %collective-permute-done.14.refs_1_ = bf16[512,1024]{1,0:T(8,128)(2,1)S(1)} collective-permute-done((bf16[512,1024]{1,0:T(8,128)(2,1)S(1)}, bf16[512,1024]{1,0:T(8,128)(2,1)S(1)}, u32[]{:S(2)}, u32[]{:S(2)}) %collective-permute-start.14) | collective-permute-done | bytes 1048608 | tf_op jit(solution)/shard_map/ppermute | solution.py:263
  199.2 1.3 collective-permute-start.16
  200.5 1.3 collective-permute-start.18
  201.8 1.4 scale.5.refs_2_
  203.2 1.3 collective-permute-start.7
  204.5 79.3 %collective-permute-done.16.refs_1_ = bf16[512,1024]{1,0:T(8,128)(2,1)S(1)} collective-permute-done((bf16[512,1024]{1,0:T(8,128)(2,1)S(1)}, bf16[512,1024]{1,0:T(8,128)(2,1)S(1)}, u32[]{:S(2)}, u32[]{:S(2)}) %collective-permute-start.16) | collective-permute-done | bytes 1048608 | tf_op jit(solution)/shard_map/ppermute | solution.py:263
  283.7 1.3 collective-permute-start.24
  285.0 1.3 collective-permute-start.9
  286.4 1.3 collective-permute-start.28
  287.6 8.7 %collective-permute-done.18.refs_1_ = bf16[512,1024]{1,0:T(8,128)(2,1)S(1)} collective-permute-done((bf16[512,1024]{1,0:T(8,128)(2,1)S(1)}, bf16[512,1024]{1,0:T(8,128)(2,1)S(1)}, u32[]{:S(2)}, u32[]{:S(2)}) %collective-permute-start.18) | collective-permute-done | bytes 1048608 | tf_op jit(solution)/shard_map/ppermute | solution.py:263
  296.3 1.3 collective-permute-start.19
  297.6 107.8 %collective-permute-done.24.refs_1_ = bf16[768,1024]{1,0:T(8,128)(2,1)S(1)} collective-permute-done((bf16[768,1024]{1,0:T(8,128)(2,1)S(1)}, bf16[768,1024]{1,0:T(8,128)(2,1)S(1)}, u32[]{:S(2)}, u32[]{:S(2)}) %collective-permute-start.24) | collective-permute-done | bytes 1572896 | tf_op jit(solution)/shard_map/ppermute | solution.py:263
  405.4 1.3 collective-permute-start.29
  406.7 8.1 %all_gather.7 = bf16[4,1024]{1,0:T(4,128)(2,1)S(1)} all-gather(bf16[4,256]{1,0:T(4,128)(2,1)S(1)} %slice.48), channel_id=1, replica_groups=mesh['zero'=4,'width'=4,'unit'=2] {'width'}, dimensions={1}, use_global_device_ids=true | all-gather | bytes 10240 | tf_op jit(solution)/shard_map/all_gather | solution.py:318
  415.4 2.6 own.3.refs_0_
  420.6 1.2 place.24.refs_0_
  422.6 1.0 place.20.refs_0_
  423.7 1.4 place.15.refs_0_
  425.1 1.0 place.21.refs_0_
  427.1 1.2 place.26.refs_0_
  429.1 72.8 %collective-permute-done.19.refs_1_ = bf16[512,1024]{1,0:T(8,128)(2,1)S(1)} collective-permute-done((bf16[512,1024]{1,0:T(8,128)(2,1)S(1)}, bf16[512,1024]{1,0:T(8,128)(2,1)S(1)}, u32[]{:S(2)}, u32[]{:S(2)}) %collective-permute-start.19) | collective-permute-done | bytes 1048608 | tf_op jit(solution)/shard_map/ppermute | solution.py:263
  503.0 1.4 place.16.refs_0_
  504.4 1.2 place.28.refs_0_
  505.6 2.0 collective-permute-done.29.refs_1_
  508.4 1.4 place.17
  (86 shorter events, 24.0 us)
Async XLA Ops:
  1.3 1.6 copy-start
  2.9 1.6 copy-start.2
  4.5 1.6 copy-start.4
  6.1 0.8 copy-start.6
  6.9 0.8 copy-start.8
  7.6 0.8 copy-start.10
  8.4 0.8 copy-start.12
  9.1 0.8 copy-start.14
  9.9 0.8 copy-start.16
  10.7 12.8 %copy-start.11 = (bf16[1024,16]{0,1:T(8,128)(2,1)S(1)}, bf16[1024,16]{0,1:T(8,128)(2,1)}, u32[]{:S(2)}) copy-start(bf16[1024,16]{0,1:T(8,128)(2,1)} %param.12) | copy-start | bytes 98308
  10.7 15.7 %copy-start.15 = (bf16[1024,16]{0,1:T(8,128)(2,1)S(1)}, bf16[1024,16]{0,1:T(8,128)(2,1)}, u32[]{:S(2)}) copy-start(bf16[1024,16]{0,1:T(8,128)(2,1)} %param.18) | copy-start | bytes 98308
  10.7 15.7 %copy-start.17 = (bf16[16,1024]{1,0:T(8,128)(2,1)S(1)}, bf16[16,1024]{1,0:T(8,128)(2,1)}, u32[]{:S(2)}) copy-start(bf16[16,1024]{1,0:T(8,128)(2,1)} %high.13) | copy-start | bytes 98308
  10.7 57.6 %copy-start.1 = (bf16[1024,1024]{1,0:T(8,128)(2,1)S(1)}, bf16[1024,1024]{1,0:T(8,128)(2,1)}, u32[]{:S(2)}) copy-start(bf16[1024,1024]{1,0:T(8,128)(2,1)} %train.4) | copy-start | bytes 6291460
  10.7 57.6 %copy-start.7 = (bf16[16,1024]{1,0:T(8,128)(2,1)S(1)}, bf16[16,1024]{1,0:T(8,128)(2,1)}, u32[]{:S(2)}) copy-start(bf16[16,1024]{1,0:T(8,128)(2,1)} %high.12) | copy-start | bytes 98308
  10.7 57.6 %copy-start.13 = (bf16[1024,16]{0,1:T(8,128)(2,1)S(1)}, bf16[1024,16]{0,1:T(8,128)(2,1)}, u32[]{:S(2)}) copy-start(bf16[1024,16]{0,1:T(8,128)(2,1)} %param.15) | copy-start | bytes 98308
  14.7 159.8 %copy-start.9 = (bf16[16,1024]{1,0:T(8,128)(2,1)S(1)}, bf16[16,1024]{1,0:T(8,128)(2,1)}, u32[]{:S(2)}) copy-start(bf16[16,1024]{1,0:T(8,128)(2,1)} %high.9) | copy-start | bytes 98308
  14.7 10.2 %collective-permute-start = (f32[4,1024]{1,0:T(4,128)S(1)}, f32[4,1024]{1,0:T(4,128)S(1)}, u32[]{:S(2)}, u32[]{:S(2)}) collective-permute-start(f32[4,1024]{1,0:T(4,128)S(1)} %tops.1.refs_0_), channel_id=1, source_target_pairs={{0,8},{8,16},{16,24},{24,0},{1,9},{9,17},{17,25},{25,1},{2,10},{10... | collective-permute-start | bytes 49160 | tf_op jit(solution)/shard_map/ppermute | solution.py:271
  17.8 7.8 %collective-permute-start.1 = (f32[4,1024]{1,0:T(4,128)S(1)}, f32[4,1024]{1,0:T(4,128)S(1)}, u32[]{:S(2)}, u32[]{:S(2)}) collective-permute-start(f32[4,1024]{1,0:T(4,128)S(1)} %tops.1.refs_0_), channel_id=1, source_target_pairs={{0,16},{8,24},{16,0},{24,8},{1,17},{9,25},{17,1},{25,9},{2,18},{10... | collective-permute-start | bytes 49160 | tf_op jit(solution)/shard_map/ppermute | solution.py:271
  20.4 5.9 %collective-permute-start.2 = (f32[4,1024]{1,0:T(4,128)S(1)}, f32[4,1024]{1,0:T(4,128)S(1)}, u32[]{:S(2)}, u32[]{:S(2)}) collective-permute-start(f32[4,1024]{1,0:T(4,128)S(1)} %tops.1.refs_0_), channel_id=1, source_target_pairs={{0,24},{8,0},{16,8},{24,16},{1,25},{9,1},{17,9},{25,17},{2,26},{10... | collective-permute-start | bytes 49160 | tf_op jit(solution)/shard_map/ppermute | solution.py:271
  22.8 44.1 %collective-permute-start.10 = (bf16[512,1024]{1,0:T(8,128)(2,1)}, bf16[512,1024]{1,0:T(8,128)(2,1)S(1)}, u32[]{:S(2)}, u32[]{:S(2)}) collective-permute-start(bf16[512,1024]{1,0:T(8,128)(2,1)} %slice.34), channel_id=1, source_target_pairs={{0,8},{8,0},{16,24},{24,16},{1,9},{9,1},{17,25},{25,17},{2,10},{10... | collective-permute-start | bytes 3145736 | tf_op jit(solution)/shard_map/ppermute | solution.py:263
  23.5 25.8 %collective-permute-start.4 = (bf16[16,384]{1,0:T(8,128)(2,1)S(1)}, bf16[16,384]{1,0:T(8,128)(2,1)S(1)}, u32[]{:S(2)}, u32[]{:S(2)}) collective-permute-start(bf16[16,384]{1,0:T(8,128)(2,1)S(1)} %fusion), channel_id=1, source_target_pairs={{0,8},{8,0},{16,24},{24,16},{1,9},{9,1},{17,25},{25,17},{2,10},{10... | collective-permute-start | bytes 36872 | tf_op jit(solution)/shard_map/ppermute | solution.py:263
  24.9 25.1 %collective-permute-start.5 = (bf16[16,384]{1,0:T(8,128)(2,1)S(1)}, bf16[16,384]{1,0:T(8,128)(2,1)S(1)}, u32[]{:S(2)}, u32[]{:S(2)}) collective-permute-start(bf16[16,384]{1,0:T(8,128)(2,1)S(1)} %fusion), channel_id=1, source_target_pairs={{8,16},{16,8},{9,17},{17,9},{10,18},{18,10},{11,19},{19,11},{12,20... | collective-permute-start | bytes 36872 | tf_op jit(solution)/shard_map/ppermute | solution.py:263
  25.6 45.3 %collective-permute-start.11 = (bf16[512,1024]{1,0:T(8,128)(2,1)}, bf16[512,1024]{1,0:T(8,128)(2,1)S(1)}, u32[]{:S(2)}, u32[]{:S(2)}) collective-permute-start(bf16[512,1024]{1,0:T(8,128)(2,1)} %slice.34), channel_id=1, source_target_pairs={{8,16},{16,8},{9,17},{17,9},{10,18},{18,10},{11,19},{19,11},{12,20... | collective-permute-start | bytes 3145736 | tf_op jit(solution)/shard_map/ppermute | solution.py:263
  26.4 1.6 copy-start.3
  28.0 142.9 %copy-start.5 = (bf16[1024,1024]{1,0:T(8,128)(2,1)S(1)}, bf16[1024,1024]{1,0:T(8,128)(2,1)}, u32[]{:S(2)}) copy-start(bf16[1024,1024]{1,0:T(8,128)(2,1)} %train.3) | copy-start | bytes 6291460
  30.7 29.9 %collective-permute-start.22 = (bf16[256,1024]{1,0:T(8,128)(2,1)S(1)}, bf16[256,1024]{1,0:T(8,128)(2,1)S(1)}, u32[]{:S(2)}, u32[]{:S(2)}) collective-permute-start(bf16[256,1024]{1,0:T(8,128)(2,1)S(1)} %slice.36), channel_id=1, source_target_pairs={{0,8},{8,0},{16,24},{24,16},{1,9},{9,1},{17,25},{25,17},{2,10},{10... | collective-permute-start | bytes 1572872 | tf_op jit(solution)/shard_map/ppermute | solution.py:263
  49.3 123.9 %collective-permute-start.3 = (bf16[1024,1024]{1,0:T(8,128)(2,1)}, bf16[1024,1024]{1,0:T(8,128)(2,1)S(1)}, u32[]{:S(2)}, u32[]{:S(2)}) collective-permute-start(bf16[1024,1024]{1,0:T(8,128)(2,1)} %train.3), channel_id=1, source_target_pairs={{0,8},{8,0},{16,24},{24,16},{1,9},{9,1},{17,25},{25,17},{2,10},{10... | collective-permute-start | bytes 6291464 | tf_op jit(solution)/shard_map/ppermute | solution.py:263
  50.0 11.4 %collective-permute-start.23 = (bf16[256,1024]{1,0:T(8,128)(2,1)S(1)}, bf16[256,1024]{1,0:T(8,128)(2,1)S(1)}, u32[]{:S(2)}, u32[]{:S(2)}) collective-permute-start(bf16[256,1024]{1,0:T(8,128)(2,1)S(1)} %slice.36), channel_id=1, source_target_pairs={{8,16},{16,8},{9,17},{17,9},{10,18},{18,10},{11,19},{19,11},{12,20... | collective-permute-start | bytes 1572872 | tf_op jit(solution)/shard_map/ppermute | solution.py:263
  60.5 13.1 %collective-permute-start.27 = (bf16[256,1024]{1,0:T(8,128)(2,1)S(1)}, bf16[256,1024]{1,0:T(8,128)(2,1)S(1)}, u32[]{:S(2)}, u32[]{:S(2)}) collective-permute-start(bf16[256,1024]{1,0:T(8,128)(2,1)S(1)} %collective-permute-done.22.refs_1_), channel_id=1, source_target_pairs={{8,16},{16,8},{9,17},{17,9},{10,18},{18,10},{11,19},{19,11},{12,20... | collective-permute-start | bytes 1572872 | tf_op jit(solution)/shard_map/ppermute | solution.py:263
  61.4 114.5 %collective-permute-start.20 = (bf16[768,1024]{1,0:T(8,128)(2,1)S(1)}, bf16[768,1024]{1,0:T(8,128)(2,1)S(1)}, u32[]{:S(2)}, u32[]{:S(2)}) collective-permute-start(bf16[768,1024]{1,0:T(8,128)(2,1)S(1)} %slice.35), channel_id=1, source_target_pairs={{0,8},{8,0},{16,24},{24,16},{1,9},{9,1},{17,25},{25,17},{2,10},{10... | collective-permute-start | bytes 4718600 | tf_op jit(solution)/shard_map/ppermute | solution.py:263
  66.9 83.5 %collective-permute-start.26 = (bf16[256,1024]{1,0:T(8,128)(2,1)S(1)}, bf16[256,1024]{1,0:T(8,128)(2,1)S(1)}, u32[]{:S(2)}, u32[]{:S(2)}) collective-permute-start(bf16[256,1024]{1,0:T(8,128)(2,1)S(1)} %collective-permute-done.23.refs_2_), channel_id=1, source_target_pairs={{8,0},{16,24},{9,1},{17,25},{10,2},{18,26},{11,3},{19,27},{12,4},{... | collective-permute-start | bytes 1572872 | tf_op jit(solution)/shard_map/ppermute | solution.py:263
  70.9 100.0 %collective-permute-start.12 = (bf16[512,1024]{1,0:T(8,128)(2,1)S(1)}, bf16[512,1024]{1,0:T(8,128)(2,1)S(1)}, u32[]{:S(2)}, u32[]{:S(2)}) collective-permute-start(bf16[512,1024]{1,0:T(8,128)(2,1)S(1)} %get-tuple-element.15), channel_id=1, source_target_pairs={{0,8},{8,0},{16,24},{24,16},{1,9},{9,1},{17,25},{25,17},{2,10},{10... | collective-permute-start | bytes 3145736 | tf_op jit(solution)/shard_map/ppermute | solution.py:263
  73.6 98.8 %collective-permute-start.13 = (bf16[512,1024]{1,0:T(8,128)(2,1)S(1)}, bf16[512,1024]{1,0:T(8,128)(2,1)S(1)}, u32[]{:S(2)}, u32[]{:S(2)}) collective-permute-start(bf16[512,1024]{1,0:T(8,128)(2,1)S(1)} %get-tuple-element.15), channel_id=1, source_target_pairs={{8,16},{16,8},{9,17},{17,9},{10,18},{18,10},{11,19},{19,11},{12,20... | collective-permute-start | bytes 3145736 | tf_op jit(solution)/shard_map/ppermute | solution.py:263
  150.4 26.2 %collective-permute-start.21 = (bf16[768,1024]{1,0:T(8,128)(2,1)S(1)}, bf16[768,1024]{1,0:T(8,128)(2,1)S(1)}, u32[]{:S(2)}, u32[]{:S(2)}) collective-permute-start(bf16[768,1024]{1,0:T(8,128)(2,1)S(1)} %slice.35), channel_id=1, source_target_pairs={{8,16},{16,8},{9,17},{17,9},{10,18},{18,10},{11,19},{19,11},{12,20... | collective-permute-start | bytes 4718600 | tf_op jit(solution)/shard_map/ppermute | solution.py:263
  170.9 29.6 %collective-permute-start.6 = (bf16[1024,1024]{1,0:T(8,128)(2,1)S(1)}, bf16[1024,1024]{1,0:T(8,128)(2,1)S(1)}, u32[]{:S(2)}, u32[]{:S(2)}) collective-permute-start(bf16[1024,1024]{1,0:T(8,128)(2,1)S(1)} %copy-done.5), channel_id=1, source_target_pairs={{8,16},{16,8},{9,17},{17,9},{10,18},{18,10},{11,19},{19,11},{12,20... | collective-permute-start | bytes 6291464 | tf_op jit(solution)/shard_map/ppermute | solution.py:263
  172.4 5.0 collective-permute-start.15
  173.2 26.0 %collective-permute-start.14 = (bf16[512,1024]{1,0:T(8,128)(2,1)S(1)}, bf16[512,1024]{1,0:T(8,128)(2,1)S(1)}, u32[]{:S(2)}, u32[]{:S(2)}) collective-permute-start(bf16[512,1024]{1,0:T(8,128)(2,1)S(1)} %scale.7.refs_2_), channel_id=1, source_target_pairs={{8,0},{16,24},{9,1},{17,25},{10,2},{18,26},{11,3},{19,27},{12,4},{... | collective-permute-start | bytes 3145736 | tf_op jit(solution)/shard_map/ppermute | solution.py:263
  175.9 109.2 %collective-permute-start.8 = (bf16[1024,1024]{1,0:T(8,128)(2,1)S(1)}, bf16[1024,1024]{1,0:T(8,128)(2,1)S(1)}, u32[]{:S(2)}, u32[]{:S(2)}) collective-permute-start(bf16[1024,1024]{1,0:T(8,128)(2,1)S(1)} %scale.4.refs_1_), channel_id=1, source_target_pairs={{8,16},{16,8},{9,17},{17,9},{10,18},{18,10},{11,19},{19,11},{12,20... | collective-permute-start | bytes 6291464 | tf_op jit(solution)/shard_map/ppermute | solution.py:263
  176.7 26.5 %collective-permute-start.17 = (bf16[512,1024]{1,0:T(8,128)(2,1)S(1)}, bf16[512,1024]{1,0:T(8,128)(2,1)S(1)}, u32[]{:S(2)}, u32[]{:S(2)}) collective-permute-start(bf16[512,1024]{1,0:T(8,128)(2,1)S(1)} %collective-permute-done.12.refs_1_), channel_id=1, source_target_pairs={{8,16},{16,8},{9,17},{17,9},{10,18},{18,10},{11,19},{19,11},{12,20... | collective-permute-start | bytes 3145736 | tf_op jit(solution)/shard_map/ppermute | solution.py:263
  177.4 108.9 %collective-permute-start.25 = (bf16[768,1024]{1,0:T(8,128)(2,1)S(1)}, bf16[768,1024]{1,0:T(8,128)(2,1)S(1)}, u32[]{:S(2)}, u32[]{:S(2)}) collective-permute-start(bf16[768,1024]{1,0:T(8,128)(2,1)S(1)} %collective-permute-done.20.refs_1_), channel_id=1, source_target_pairs={{8,16},{16,8},{9,17},{17,9},{10,18},{18,10},{11,19},{19,11},{12,20... | collective-permute-start | bytes 4718600 | tf_op jit(solution)/shard_map/ppermute | solution.py:263
  199.2 84.5 %collective-permute-start.16 = (bf16[512,1024]{1,0:T(8,128)(2,1)S(1)}, bf16[512,1024]{1,0:T(8,128)(2,1)S(1)}, u32[]{:S(2)}, u32[]{:S(2)}) collective-permute-start(bf16[512,1024]{1,0:T(8,128)(2,1)S(1)} %collective-permute-done.13.refs_2_), channel_id=1, source_target_pairs={{8,0},{16,24},{9,1},{17,25},{10,2},{18,26},{11,3},{19,27},{12,4},{... | collective-permute-start | bytes 3145736 | tf_op jit(solution)/shard_map/ppermute | solution.py:263
  200.5 95.8 %collective-permute-start.18 = (bf16[512,1024]{1,0:T(8,128)(2,1)S(1)}, bf16[512,1024]{1,0:T(8,128)(2,1)S(1)}, u32[]{:S(2)}, u32[]{:S(2)}) collective-permute-start(bf16[512,1024]{1,0:T(8,128)(2,1)S(1)} %collective-permute-done.15.refs_2_), channel_id=1, source_target_pairs={{8,0},{16,24},{9,1},{17,25},{10,2},{18,26},{11,3},{19,27},{12,4},{... | collective-permute-start | bytes 3145736 | tf_op jit(solution)/shard_map/ppermute | solution.py:263
  203.2 299.8 %collective-permute-start.7 = (bf16[1024,1024]{1,0:T(8,128)(2,1)S(1)}, bf16[1024,1024]{1,0:T(8,128)(2,1)S(1)}, u32[]{:S(2)}, u32[]{:S(2)}) collective-permute-start(bf16[1024,1024]{1,0:T(8,128)(2,1)S(1)} %scale.5.refs_2_), channel_id=1, source_target_pairs={{8,0},{16,24},{9,1},{17,25},{10,2},{18,26},{11,3},{19,27},{12,4},{... | collective-permute-start | bytes 6291464 | tf_op jit(solution)/shard_map/ppermute | solution.py:263
  283.7 121.6 %collective-permute-start.24 = (bf16[768,1024]{1,0:T(8,128)(2,1)S(1)}, bf16[768,1024]{1,0:T(8,128)(2,1)S(1)}, u32[]{:S(2)}, u32[]{:S(2)}) collective-permute-start(bf16[768,1024]{1,0:T(8,128)(2,1)S(1)} %collective-permute-done.21.refs_2_), channel_id=1, source_target_pairs={{8,0},{16,24},{9,1},{17,25},{10,2},{18,26},{11,3},{19,27},{12,4},{... | collective-permute-start | bytes 4718600 | tf_op jit(solution)/shard_map/ppermute | solution.py:263
  285.0 223.3 %collective-permute-start.9 = (bf16[1024,1024]{1,0:T(8,128)(2,1)S(1)}, bf16[1024,1024]{1,0:T(8,128)(2,1)S(1)}, u32[]{:S(2)}, u32[]{:S(2)}) collective-permute-start(bf16[1024,1024]{1,0:T(8,128)(2,1)S(1)} %collective-permute-done.8.refs_2_), channel_id=1, source_target_pairs={{8,0},{16,24},{9,1},{17,25},{10,2},{18,26},{11,3},{19,27},{12,4},{... | collective-permute-start | bytes 6291464 | tf_op jit(solution)/shard_map/ppermute | solution.py:263
  286.4 218.0 %collective-permute-start.28 = (bf16[768,1024]{1,0:T(8,128)(2,1)S(1)}, bf16[768,1024]{1,0:T(8,128)(2,1)S(1)}, u32[]{:S(2)}, u32[]{:S(2)}) collective-permute-start(bf16[768,1024]{1,0:T(8,128)(2,1)S(1)} %collective-permute-done.25.refs_2_), channel_id=1, source_target_pairs={{8,0},{16,24},{9,1},{17,25},{10,2},{18,26},{11,3},{19,27},{12,4},{... | collective-permute-start | bytes 4718600 | tf_op jit(solution)/shard_map/ppermute | solution.py:263
  296.3 205.6 %collective-permute-start.19 = (bf16[512,1024]{1,0:T(8,128)(2,1)S(1)}, bf16[512,1024]{1,0:T(8,128)(2,1)S(1)}, u32[]{:S(2)}, u32[]{:S(2)}) collective-permute-start(bf16[512,1024]{1,0:T(8,128)(2,1)S(1)} %collective-permute-done.17.refs_2_), channel_id=1, source_target_pairs={{8,0},{16,24},{9,1},{17,25},{10,2},{18,26},{11,3},{19,27},{12,4},{... | collective-permute-start | bytes 3145736 | tf_op jit(solution)/shard_map/ppermute | solution.py:263
  405.4 102.2 %collective-permute-start.29 = (bf16[256,1024]{1,0:T(8,128)(2,1)S(1)}, bf16[256,1024]{1,0:T(8,128)(2,1)S(1)}, u32[]{:S(2)}, u32[]{:S(2)}) collective-permute-start(bf16[256,1024]{1,0:T(8,128)(2,1)S(1)} %collective-permute-done.27.refs_2_), channel_id=1, source_target_pairs={{8,0},{16,24},{9,1},{17,25},{10,2},{18,26},{11,3},{19,27},{12,4},{... | collective-permute-start | bytes 1572872 | tf_op jit(solution)/shard_map/ppermute | solution.py:263

commit v3 on v2

--- a/solution.py
+++ b/solution.py
@@ -135,10 +135,10 @@
     return mine + hop * (1 - 2 * lax.rem(mine + side, 2))
 
 
-def place_kernel(hop, sides, at, shard, count, place, *refs):
+def place_kernel(hop, sides, at, shard, count, *refs):
     sources, out, sems = refs[1 : 1 + len(sides)], refs[1 + len(sides)], refs[2 + len(sides)]
     for index, (side, source) in enumerate(zip(sides, sources)):
-        owner = owner_of(place[0], side, hop)
+        owner = owner_of(lax.axis_index("zero").astype(jnp.int32), side, hop)
         rows = source.shape[0]
         part = tile_of(rows)
 
@@ -157,23 +157,22 @@
                 store.wait()
 
 
-def placed(place, out, count, hop, at, shard, arrived):
+def placed(out, count, hop, at, shard, arrived):
     sides = tuple(side for side, _ in arrived)
     sources = [pltpu.with_memory_space_constraint(source, VMEM) for _, source in arrived]
     rows, size = sources[0].shape[0], sum(source.size for source in sources)
     return pl.pallas_call(
         functools.partial(place_kernel, hop, sides, at, shard, count),
-        in_specs=[pl.BlockSpec(memory_space=pltpu.MemorySpace.SMEM)]
-        + [pl.BlockSpec(memory_space=HBM)]
+        in_specs=[pl.BlockSpec(memory_space=HBM)]
         + [pl.BlockSpec(memory_space=VMEM)] * len(sources),
         out_specs=pl.BlockSpec(memory_space=HBM),
         out_shape=jax.ShapeDtypeStruct(out.shape, out.dtype),
         scratch_shapes=[pltpu.SemaphoreType.DMA((len(sources), rows // tile_of(rows)))],
-        input_output_aliases={1: 0},
+        input_output_aliases={0: 0},
         compiler_params=pltpu.CompilerParams(vmem_limit_bytes=GRANT),
         name="place",
         cost_estimate=pl.CostEstimate(flops=size, bytes_accessed=4 * size, transcendentals=0),
-    )(place, out, *sources)
+    )(out, *sources)
 
 
 def own_kernel(index, first, place, train, low_t, high, factor, out, *serve):
@@ -268,10 +267,10 @@
     tops = column_tops(trains, lows, highs, norm)
     parts = [tops]
     for s in range(1, count):
-        parts.append(lax.ppermute(tops, "zero", [(i, (i + s) % count) for i in range(count)]))
-    early = train_key[:half]
-    raw["ka"] = sent(1, early, early)
-    low = jnp.concatenate((lows[0], lows[1][:, :half]), axis=1)
+        pairs = [(i, (i + s) % count) for i in range(count) if (i + s) % count]
+        parts.append(lax.ppermute(tops, "zero", pairs))
+    raw["ka"] = sent(1, train_key[:half], train_key[:half])
+    low = jnp.concatenate((lows[0], lows[1]), axis=1)
     whole = low.shape[1]
     devices = lax.axis_size("width")
     shared = whole % devices == 0
@@ -284,22 +283,23 @@
     if shared:
         joined = lax.all_gather(joined, "width", axis=2, tiled=True)
     near = {side: joined[index] for index, side in enumerate(sides)}
-    factor, norms = join_tops(place, parts)
+    joined_tops, norms = join_tops(place, parts)
+    factor = jnp.maximum(joined_tops, lax.ppermute(joined_tops, "zero", [(1, 0)]))
+    raw["kb"] = sent(1, train_key[half:], train_key[half:])
 
     outs, serves = [None] * 3, [None] * 3
-    for index, begin in ((1, half), (2, 0), (0, rows)):
+    for index, begin in ((2, 0), (1, rows), (0, rows)):
         outs[index], *serves[index] = own_scaled(
             index, place, count, trains[index], lows[index], highs[index], factor, begin
         )
     pieces = []
-    for name, index, low_at in (("q", 0, 0), ("ka", 1, rows)):
+    for name, index, at, low_at in (("q", 0, 0, 0), ("ka", 1, 0, rows), ("kb", 1, half, rows + half)):
         arrived = []
         for side, got in raw[name]:
             arrived.append((side, scaled(index, got, near[side], highs[index], factor, low_at)))
-        pieces.append((name, index, 0, arrived))
+        pieces.append((name, index, at, arrived))
     cut = rows * 3 // 4
     for name, index, at, ready in (
-        ("kb", 1, half, serves[1][0]),
         ("v", 2, 0, serves[2][0][:cut]),
         ("w", 2, cut, serves[2][0][cut:]),
     ):
@@ -311,11 +311,14 @@
             if hop + 1 < count:
                 brought = dict(arrived)
                 later.append((name, index, at, sent(hop + 1, brought.get(1), brought.get(0))))
-            outs[index] = placed(place, outs[index], count, hop, at, rows, arrived)
+            outs[index] = placed(outs[index], count, hop, at, rows, arrived)
         pieces = later
 
     size = norm_train.shape[0]
-    wide = lax.all_gather(norms[:count, :size].astype(jnp.bfloat16), "width", axis=1, tiled=True)
+    narrow = norms[:count, :size].astype(jnp.bfloat16)
+    moved = lax.ppermute(narrow, "zero", [(1, 0)])
+    narrow = jnp.where(place == 0, moved, narrow)
+    wide = lax.all_gather(narrow, "width", axis=1, tiled=True)
     serve_norm = wide.reshape(-1)
     return (*outs, factor[0], factor[1], factor[2], serve_norm)
 

time: 511 us -> 534 us (1.045)
  waiting for transfers between devices: 402 us -> 416 us
    ppermute x3 -> x5, waiting for transfers between devices: 0.01 us -> 12.5 us  [the longest x1 6.77 us: merged_for_serving(): moved = lax.ppermute(narrow, 'zero', [(1, 0)])]
    ppermute x3 -> x5, starting transfers between devices: 7.04 us -> 13.8 us  [the longest x3 11.2 us: merged_for_serving(): parts.append(lax.ppermute(tops, 'zero', pairs))]
    unnamed x37 -> x39, local copies, waits for them, and re-layouts: 11.5 us -> 11.3 us
  transfers between devices with their start and end apart: 30 -> 32, of which waited for: 10 -> 12; matrix products, arithmetic and copies ran while one was open for 0% -> 1% of each run, Pallas kernels for 5% -> 6%
where the time goes in v3:
time: 534 us; the launch traced here: 533 us
  waiting for transfers between devices  416 us (78%)
  starting transfers between devices  45.6 us (9%)
  Pallas kernels  34.8 us (7%)
  local copies, waits for them, and re-layouts  17.5 us (3%)
  blocking collectives  16.6 us (3%)
    ppermute x27, waiting for transfers between devices, sent(): moved.append((side, lax.ppermute(x, 'zero', pairs)))  404 us
    ppermute x27, starting transfers between devices, sent(): moved.append((side, lax.ppermute(x, 'zero', pairs)))  31.8 us
    pallas_call x15, Pallas kernels, placed(): pl.pallas_call(functools.partial(place_kernel, hop, sides, at, shard, cou...  17.5 us
    unnamed x39, local copies, waits for them, and re-layouts  11.3 us
    ppermute x3, starting transfers between devices, merged_for_serving(): parts.append(lax.ppermute(tops, 'zero', pairs))  11.2 us
  transfers between devices with their start and end apart: 32, of which 12 were waited for; matrix products, arithmetic and copies ran while one was open for 1% of the time, Pallas kernels for 6%

profile of v3, /device:TPU:0, one launch (start us, length us, event | category | flops | bytes accessed | tf_op | source)
XLA Modules:
  0.0 532.6 jit_solution(12289306741385316070)
XLA Ops:
  0.7 3.2 fusion.1
  3.9 3.1 collective-permute-start.11
  7.7 1.6 copy-done
  9.3 1.6 copy-done.2
  10.9 1.6 copy-done.4
  17.0 4.0 tops.1.refs_0_
  21.0 1.9 collective-permute-start
  22.9 4.9 collective-permute-start.1
  27.8 4.4 collective-permute-start.2
  32.3 1.4 collective-permute-done.2.refs_3_
  33.7 1.3 collective-permute-start.3
  35.0 4.3 collective-permute-done.3
  39.3 2.7 own.5
  42.0 1.3 copy-done.6
  44.2 1.4 collective-permute-start.24
  45.6 2.6 collective-permute-start.4
  48.3 52.2 %collective-permute-done.5 = bf16[16,512]{1,0:T(8,128)(2,1)S(1)} collective-permute-done((bf16[16,512]{1,0:T(8,128)(2,1)S(1)}, bf16[16,512]{1,0:T(8,128)(2,1)S(1)}, u32[]{:S(2)}, u32[]{:S(2)}) %collective-permute-start.5) | collective-permute-done | bytes 16416 | tf_op jit(solution)/shard_map/ppermute | solution.py:262
  101.2 1.3 collective-permute-start.31
  102.5 6.8 %collective-permute-done.31 = bf16[4,256]{1,0:T(4,128)(2,1)S(1)} collective-permute-done((bf16[4,256]{1,0:T(4,128)(2,1)S(1)}, bf16[4,256]{1,0:T(4,128)(2,1)S(1)}, u32[]{:S(2)}, u32[]{:S(2)}) %collective-permute-start.31) | collective-permute-done | bytes 2080 | tf_op jit(solution)/shard_map/ppermute | solution.py:319
  111.7 1.5 slice.37
  113.2 3.3 collective-permute-start.21
  117.3 19.0 %collective-permute-done.13.train = bf16[512,1024]{1,0:T(8,128)(2,1)S(1)} collective-permute-done((bf16[512,1024]{1,0:T(8,128)(2,1)}, bf16[512,1024]{1,0:T(8,128)(2,1)S(1)}, u32[]{:S(2)}, u32[]{:S(2)}) %collective-permute-start.13) | collective-permute-done | bytes 1048608 | tf_op jit(solution)/shard_map/ppermute | solution.py:262
  137.8 8.5 %all_gather.6 = bf16[2,16,2048]{2,1,0:T(8,128)(2,1)S(1)} all-gather(bf16[2,16,512]{2,1,0:T(8,128)(2,1)S(1)} %pad_maximum_fusion), channel_id=1, replica_groups=mesh['zero'=4,'width'=4,'unit'=2] {'width'}, dimensions={2}, use_global_device_ids=true | all-gather | bytes 163840 | tf_op jit(solution)/shard_map/all_gather | solution.py:284
  148.4 1.3 collective-permute-start.15
  149.8 1.4 scale.6.refs_1_
  151.1 12.3 %collective-permute-done.21.refs_1_ = bf16[768,1024]{1,0:T(8,128)(2,1)S(1)} collective-permute-done((bf16[768,1024]{1,0:T(8,128)(2,1)S(1)}, bf16[768,1024]{1,0:T(8,128)(2,1)S(1)}, u32[]{:S(2)}, u32[]{:S(2)}) %collective-permute-start.21) | collective-permute-done | bytes 1572896 | tf_op jit(solution)/shard_map/ppermute | solution.py:262
  167.3 97.4 %collective-permute-done.15.refs_1_ = bf16[512,1024]{1,0:T(8,128)(2,1)S(1)} collective-permute-done((bf16[512,1024]{1,0:T(8,128)(2,1)S(1)}, bf16[512,1024]{1,0:T(8,128)(2,1)S(1)}, u32[]{:S(2)}, u32[]{:S(2)}) %collective-permute-start.15) | collective-permute-done | bytes 1048608 | tf_op jit(solution)/shard_map/ppermute | solution.py:262
  264.7 1.3 collective-permute-start.17
  266.0 1.3 collective-permute-start.19
  267.3 1.4 scale.7.refs_2_
  268.6 1.3 collective-permute-start.8
  269.9 27.6 %collective-permute-done.17.refs_1_ = bf16[512,1024]{1,0:T(8,128)(2,1)S(1)} collective-permute-done((bf16[512,1024]{1,0:T(8,128)(2,1)S(1)}, bf16[512,1024]{1,0:T(8,128)(2,1)S(1)}, u32[]{:S(2)}, u32[]{:S(2)}) %collective-permute-start.17) | collective-permute-done | bytes 1048608 | tf_op jit(solution)/shard_map/ppermute | solution.py:262
  297.5 1.3 collective-permute-start.25
  298.8 1.3 collective-permute-start.10
  300.1 8.6 %collective-permute-done.19.refs_1_ = bf16[512,1024]{1,0:T(8,128)(2,1)S(1)} collective-permute-done((bf16[512,1024]{1,0:T(8,128)(2,1)S(1)}, bf16[512,1024]{1,0:T(8,128)(2,1)S(1)}, u32[]{:S(2)}, u32[]{:S(2)}) %collective-permute-start.19) | collective-permute-done | bytes 1048608 | tf_op jit(solution)/shard_map/ppermute | solution.py:262
  308.8 1.3 collective-permute-start.20
  310.1 1.3 collective-permute-start.29
  311.4 177.7 %collective-permute-done.20.refs_1_ = bf16[512,1024]{1,0:T(8,128)(2,1)S(1)} collective-permute-done((bf16[512,1024]{1,0:T(8,128)(2,1)S(1)}, bf16[512,1024]{1,0:T(8,128)(2,1)S(1)}, u32[]{:S(2)}, u32[]{:S(2)}) %collective-permute-start.20) | collective-permute-done | bytes 1048608 | tf_op jit(solution)/shard_map/ppermute | solution.py:262
  490.4 1.3 collective-permute-start.30
  491.7 8.1 %all_gather.7 = bf16[4,1024]{1,0:T(4,128)(2,1)S(1)} all-gather(bf16[4,256]{1,0:T(4,128)(2,1)S(1)} %broadcast_select_fusion), channel_id=1, replica_groups=mesh['zero'=4,'width'=4,'unit'=2] {'width'}, dimensions={1}, use_global_device_ids=true | all-gather | bytes 10240 | tf_op jit(solution)/shard_map/all_gather | solution.py:321
  500.4 2.6 own.4.refs_0_
  502.9 2.6 own.3.refs_0_
  509.4 2.0 place.25.refs_0_
  513.5 1.4 place.15.refs_0_
  518.1 6.7 %collective-permute-done.27.refs_1_ = bf16[256,1024]{1,0:T(8,128)(2,1)S(1)} collective-permute-done((bf16[256,1024]{1,0:T(8,128)(2,1)}, bf16[256,1024]{1,0:T(8,128)(2,1)S(1)}, u32[]{:S(2)}, u32[]{:S(2)}) %collective-permute-start.27) | collective-permute-done | bytes 524320 | tf_op jit(solution)/shard_map/ppermute | solution.py:262
  525.6 1.4 place.16.refs_0_
  528.2 2.2 collective-permute-done.30.refs_1_
  531.2 1.4 place.17
  (95 shorter events, 31.4 us)
Async XLA Ops:
  0.6 47.6 %copy-start.14 = (bf16[1024,16]{0,1:T(8,128)(2,1)S(1)}, bf16[1024,16]{0,1:T(8,128)(2,1)}, u32[]{:S(2)}) copy-start(bf16[1024,16]{0,1:T(8,128)(2,1)} %param.12) | copy-start | bytes 98308
  0.6 47.5 %copy-start.12 = (bf16[1024,16]{0,1:T(8,128)(2,1)S(1)}, bf16[1024,16]{0,1:T(8,128)(2,1)}, u32[]{:S(2)}) copy-start(bf16[1024,16]{0,1:T(8,128)(2,1)} %param.15) | copy-start | bytes 98308
  0.7 38.7 %copy-start.16 = (bf16[1024,16]{0,1:T(8,128)(2,1)S(1)}, bf16[1024,16]{0,1:T(8,128)(2,1)}, u32[]{:S(2)}) copy-start(bf16[1024,16]{0,1:T(8,128)(2,1)} %param.18) | copy-start | bytes 98308
  0.7 145.6 %copy-start.8 = (bf16[16,1024]{1,0:T(8,128)(2,1)S(1)}, bf16[16,1024]{1,0:T(8,128)(2,1)}, u32[]{:S(2)}) copy-start(bf16[16,1024]{1,0:T(8,128)(2,1)} %high.16) | copy-start | bytes 98308
  0.7 38.6 %copy-start.3 = (bf16[1024,1024]{1,0:T(8,128)(2,1)S(1)}, bf16[1024,1024]{1,0:T(8,128)(2,1)}, u32[]{:S(2)}) copy-start(bf16[1024,1024]{1,0:T(8,128)(2,1)} %train.5) | copy-start | bytes 6291460
  0.7 38.6 %copy-start.18 = (bf16[16,1024]{1,0:T(8,128)(2,1)S(1)}, bf16[16,1024]{1,0:T(8,128)(2,1)}, u32[]{:S(2)}) copy-start(bf16[16,1024]{1,0:T(8,128)(2,1)} %high.17) | copy-start | bytes 98308
  3.9 109.3 %collective-permute-start.11 = (bf16[512,1024]{1,0:T(8,128)(2,1)}, bf16[512,1024]{1,0:T(8,128)(2,1)S(1)}, u32[]{:S(2)}, u32[]{:S(2)}) collective-permute-start(bf16[512,1024]{1,0:T(8,128)(2,1)} %get-tuple-element.16), channel_id=1, source_target_pairs={{0,8},{8,0},{16,24},{24,16},{1,9},{9,1},{17,25},{25,17},{2,10},{10... | collective-permute-start | bytes 3145736 | tf_op jit(solution)/shard_map/ppermute | solution.py:262
  7.7 1.6 copy-start
  9.3 1.6 copy-start.2
  10.9 1.6 copy-start.4
  14.7 0.8 copy-start.13
  15.5 0.8 copy-start.15
  16.2 0.8 copy-start.17
  17.0 132.8 %copy-start.10 = (bf16[16,1024]{1,0:T(8,128)(2,1)S(1)}, bf16[16,1024]{1,0:T(8,128)(2,1)}, u32[]{:S(2)}) copy-start(bf16[16,1024]{1,0:T(8,128)(2,1)} %high.11) | copy-start | bytes 98308
  21.0 11.3 %collective-permute-start = (f32[4,1024]{1,0:T(4,128)S(1)}, f32[4,1024]{1,0:T(4,128)S(1)}, u32[]{:S(2)}, u32[]{:S(2)}) collective-permute-start(f32[4,1024]{1,0:T(4,128)S(1)} %tops.1.refs_0_), channel_id=1, source_target_pairs={{0,8},{8,16},{16,24},{1,9},{9,17},{17,25},{2,10},{10,18},{18,26},{... | collective-permute-start | bytes 49160 | tf_op jit(solution)/shard_map/ppermute | solution.py:271
  22.9 9.4 %collective-permute-start.1 = (f32[4,1024]{1,0:T(4,128)S(1)}, f32[4,1024]{1,0:T(4,128)S(1)}, u32[]{:S(2)}, u32[]{:S(2)}) collective-permute-start(f32[4,1024]{1,0:T(4,128)S(1)} %tops.1.refs_0_), channel_id=1, source_target_pairs={{0,16},{8,24},{24,8},{1,17},{9,25},{25,9},{2,18},{10,26},{26,10},{... | collective-permute-start | bytes 49160 | tf_op jit(solution)/shard_map/ppermute | solution.py:271
  27.8 5.8 %collective-permute-start.2 = (f32[4,1024]{1,0:T(4,128)S(1)}, f32[4,1024]{1,0:T(4,128)S(1)}, u32[]{:S(2)}, u32[]{:S(2)}) collective-permute-start(f32[4,1024]{1,0:T(4,128)S(1)} %tops.1.refs_0_), channel_id=1, source_target_pairs={{0,24},{16,8},{24,16},{1,25},{17,9},{25,17},{2,26},{18,10},{26,18}... | collective-permute-start | bytes 49160 | tf_op jit(solution)/shard_map/ppermute | solution.py:271
  33.7 5.6 %collective-permute-start.3 = (f32[4,1024]{1,0:T(4,128)S(1)}, f32[4,1024]{1,0:T(4,128)S(1)}, u32[]{:S(2)}, u32[]{:S(2)}) collective-permute-start(f32[4,1024]{1,0:T(4,128)S(1)} %get-tuple-element.11), channel_id=1, source_target_pairs={{8,0},{9,1},{10,2},{11,3},{12,4},{13,5},{14,6},{15,7}} | collective-permute-start | bytes 49160 | tf_op jit(solution)/shard_map/ppermute | solution.py:287
  42.0 1.3 copy-start.6
  44.2 65.8 %collective-permute-start.23 = (bf16[256,1024]{1,0:T(8,128)(2,1)}, bf16[256,1024]{1,0:T(8,128)(2,1)}, u32[]{:S(2)}, u32[]{:S(2)}) collective-permute-start(bf16[256,1024]{1,0:T(8,128)(2,1)} %slice.38), channel_id=1, source_target_pairs={{0,8},{8,0},{16,24},{24,16},{1,9},{9,1},{17,25},{25,17},{2,10},{10... | collective-permute-start | bytes 1572872 | tf_op jit(solution)/shard_map/ppermute | solution.py:262
  44.2 66.8 %collective-permute-start.24 = (bf16[256,1024]{1,0:T(8,128)(2,1)}, bf16[256,1024]{1,0:T(8,128)(2,1)}, u32[]{:S(2)}, u32[]{:S(2)}) collective-permute-start(bf16[256,1024]{1,0:T(8,128)(2,1)} %slice.38), channel_id=1, source_target_pairs={{8,16},{16,8},{9,17},{17,9},{10,18},{18,10},{11,19},{19,11},{12,20... | collective-permute-start | bytes 1572872 | tf_op jit(solution)/shard_map/ppermute | solution.py:262
  45.6 102.8 %collective-permute-start.4 = (bf16[1024,1024]{1,0:T(8,128)(2,1)}, bf16[1024,1024]{1,0:T(8,128)(2,1)S(1)}, u32[]{:S(2)}, u32[]{:S(2)}) collective-permute-start(bf16[1024,1024]{1,0:T(8,128)(2,1)} %train.3), channel_id=1, source_target_pairs={{0,8},{8,0},{16,24},{24,16},{1,9},{9,1},{17,25},{25,17},{2,10},{10... | collective-permute-start | bytes 6291464 | tf_op jit(solution)/shard_map/ppermute | solution.py:262
  48.2 52.3 %collective-permute-start.5 = (bf16[16,512]{1,0:T(8,128)(2,1)S(1)}, bf16[16,512]{1,0:T(8,128)(2,1)S(1)}, u32[]{:S(2)}, u32[]{:S(2)}) collective-permute-start(bf16[16,512]{1,0:T(8,128)(2,1)S(1)} %fusion), channel_id=1, source_target_pairs={{0,8},{8,0},{16,24},{24,16},{1,9},{9,1},{17,25},{25,17},{2,10},{10... | collective-permute-start | bytes 49160 | tf_op jit(solution)/shard_map/ppermute | solution.py:262
  100.5 0.7 collective-permute-start.6
  101.2 8.1 %collective-permute-start.31 = (bf16[4,256]{1,0:T(4,128)(2,1)S(1)}, bf16[4,256]{1,0:T(4,128)(2,1)S(1)}, u32[]{:S(2)}, u32[]{:S(2)}) collective-permute-start(bf16[4,256]{1,0:T(4,128)(2,1)S(1)} %slice.52), channel_id=1, source_target_pairs={{8,0},{9,1},{10,2},{11,3},{12,4},{13,5},{14,6},{15,7}} | collective-permute-start | bytes 6152 | tf_op jit(solution)/shard_map/ppermute | solution.py:319
  109.3 7.3 %collective-permute-start.12 = (bf16[512,1024]{1,0:T(8,128)(2,1)}, bf16[512,1024]{1,0:T(8,128)(2,1)S(1)}, u32[]{:S(2)}, u32[]{:S(2)}) collective-permute-start(bf16[512,1024]{1,0:T(8,128)(2,1)} %get-tuple-element.16), channel_id=1, source_target_pairs={{8,16},{16,8},{9,17},{17,9},{10,18},{18,10},{11,19},{19,11},{12,20... | collective-permute-start | bytes 3145736 | tf_op jit(solution)/shard_map/ppermute | solution.py:262
  110.0 26.3 %collective-permute-start.13 = (bf16[512,1024]{1,0:T(8,128)(2,1)}, bf16[512,1024]{1,0:T(8,128)(2,1)S(1)}, u32[]{:S(2)}, u32[]{:S(2)}) collective-permute-start(bf16[512,1024]{1,0:T(8,128)(2,1)} %get-tuple-element.15), channel_id=1, source_target_pairs={{0,8},{8,0},{16,24},{24,16},{1,9},{9,1},{17,25},{25,17},{2,10},{10... | collective-permute-start | bytes 3145736 | tf_op jit(solution)/shard_map/ppermute | solution.py:262
  111.0 26.1 %collective-permute-start.14 = (bf16[512,1024]{1,0:T(8,128)(2,1)}, bf16[512,1024]{1,0:T(8,128)(2,1)S(1)}, u32[]{:S(2)}, u32[]{:S(2)}) collective-permute-start(bf16[512,1024]{1,0:T(8,128)(2,1)} %get-tuple-element.15), channel_id=1, source_target_pairs={{8,16},{16,8},{9,17},{17,9},{10,18},{18,10},{11,19},{19,11},{12,20... | collective-permute-start | bytes 3145736 | tf_op jit(solution)/shard_map/ppermute | solution.py:262
  113.2 50.2 %collective-permute-start.21 = (bf16[768,1024]{1,0:T(8,128)(2,1)S(1)}, bf16[768,1024]{1,0:T(8,128)(2,1)S(1)}, u32[]{:S(2)}, u32[]{:S(2)}) collective-permute-start(bf16[768,1024]{1,0:T(8,128)(2,1)S(1)} %slice.37), channel_id=1, source_target_pairs={{0,8},{8,0},{16,24},{24,16},{1,9},{9,1},{17,25},{25,17},{2,10},{10... | collective-permute-start | bytes 4718600 | tf_op jit(solution)/shard_map/ppermute | solution.py:262
  116.5 149.4 %collective-permute-start.7 = (bf16[1024,1024]{1,0:T(8,128)(2,1)}, bf16[1024,1024]{1,0:T(8,128)(2,1)S(1)}, u32[]{:S(2)}, u32[]{:S(2)}) collective-permute-start(bf16[1024,1024]{1,0:T(8,128)(2,1)} %train.3), channel_id=1, source_target_pairs={{8,16},{16,8},{9,17},{17,9},{10,18},{18,10},{11,19},{19,11},{12,20... | collective-permute-start | bytes 6291464 | tf_op jit(solution)/shard_map/ppermute | solution.py:262
  136.3 28.6 %collective-permute-start.22 = (bf16[768,1024]{1,0:T(8,128)(2,1)S(1)}, bf16[768,1024]{1,0:T(8,128)(2,1)S(1)}, u32[]{:S(2)}, u32[]{:S(2)}) collective-permute-start(bf16[768,1024]{1,0:T(8,128)(2,1)S(1)} %slice.37), channel_id=1, source_target_pairs={{8,16},{16,8},{9,17},{17,9},{10,18},{18,10},{11,19},{19,11},{12,20... | collective-permute-start | bytes 4718600 | tf_op jit(solution)/shard_map/ppermute | solution.py:262
  137.1 10.6 %collective-permute-start.28 = (bf16[256,1024]{1,0:T(8,128)(2,1)}, bf16[256,1024]{1,0:T(8,128)(2,1)S(1)}, u32[]{:S(2)}, u32[]{:S(2)}) collective-permute-start(bf16[256,1024]{1,0:T(8,128)(2,1)} %collective-permute-done.23.refs_1_), channel_id=1, source_target_pairs={{8,16},{16,8},{9,17},{17,9},{10,18},{18,10},{11,19},{19,11},{12,20... | collective-permute-start | bytes 1572872 | tf_op jit(solution)/shard_map/ppermute | solution.py:262
  146.3 354.1 %copy-start.1 = (bf16[1024,1024]{1,0:T(8,128)(2,1)S(1)}, bf16[1024,1024]{1,0:T(8,128)(2,1)}, u32[]{:S(2)}) copy-start(bf16[1024,1024]{1,0:T(8,128)(2,1)} %train.4) | copy-start | bytes 6291460
  147.7 18.8 %collective-permute-start.16 = (bf16[512,1024]{1,0:T(8,128)(2,1)S(1)}, bf16[512,1024]{1,0:T(8,128)(2,1)S(1)}, u32[]{:S(2)}, u32[]{:S(2)}) collective-permute-start(bf16[512,1024]{1,0:T(8,128)(2,1)S(1)} %scale.8.refs_1_), channel_id=1, source_target_pairs={{8,16},{16,8},{9,17},{17,9},{10,18},{18,10},{11,19},{19,11},{12,20... | collective-permute-start | bytes 3145736 | tf_op jit(solution)/shard_map/ppermute | solution.py:262
  148.4 116.2 %collective-permute-start.15 = (bf16[512,1024]{1,0:T(8,128)(2,1)S(1)}, bf16[512,1024]{1,0:T(8,128)(2,1)S(1)}, u32[]{:S(2)}, u32[]{:S(2)}) collective-permute-start(bf16[512,1024]{1,0:T(8,128)(2,1)S(1)} %scale.9.refs_2_), channel_id=1, source_target_pairs={{8,0},{16,24},{9,1},{17,25},{10,2},{18,26},{11,3},{19,27},{12,4},{... | collective-permute-start | bytes 3145736 | tf_op jit(solution)/shard_map/ppermute | solution.py:262
  163.4 135.4 %collective-permute-start.9 = (bf16[1024,1024]{1,0:T(8,128)(2,1)S(1)}, bf16[1024,1024]{1,0:T(8,128)(2,1)S(1)}, u32[]{:S(2)}, u32[]{:S(2)}) collective-permute-start(bf16[1024,1024]{1,0:T(8,128)(2,1)S(1)} %scale.6.refs_1_), channel_id=1, source_target_pairs={{8,16},{16,8},{9,17},{17,9},{10,18},{18,10},{11,19},{19,11},{12,20... | collective-permute-start | bytes 6291464 | tf_op jit(solution)/shard_map/ppermute | solution.py:262
  164.9 338.0 %copy-start.5 = (bf16[1024,1024]{1,0:T(8,128)(2,1)S(1)}, bf16[1024,1024]{1,0:T(8,128)(2,1)}, u32[]{:S(2)}) copy-start(bf16[1024,1024]{1,0:T(8,128)(2,1)} %train.3) | copy-start | bytes 6291460
  164.9 103.7 %collective-permute-start.18 = (bf16[512,1024]{1,0:T(8,128)(2,1)S(1)}, bf16[512,1024]{1,0:T(8,128)(2,1)S(1)}, u32[]{:S(2)}, u32[]{:S(2)}) collective-permute-start(bf16[512,1024]{1,0:T(8,128)(2,1)S(1)} %scale.10.refs_1_), channel_id=1, source_target_pairs={{8,16},{16,8},{9,17},{17,9},{10,18},{18,10},{11,19},{19,11},{12,20... | collective-permute-start | bytes 3145736 | tf_op jit(solution)/shard_map/ppermute | solution.py:262
  166.5 143.5 %collective-permute-start.26 = (bf16[768,1024]{1,0:T(8,128)(2,1)S(1)}, bf16[768,1024]{1,0:T(8,128)(2,1)S(1)}, u32[]{:S(2)}, u32[]{:S(2)}) collective-permute-start(bf16[768,1024]{1,0:T(8,128)(2,1)S(1)} %collective-permute-done.21.refs_1_), channel_id=1, source_target_pairs={{8,16},{16,8},{9,17},{17,9},{10,18},{18,10},{11,19},{19,11},{12,20... | collective-permute-start | bytes 4718600 | tf_op jit(solution)/shard_map/ppermute | solution.py:262
  264.7 32.9 %collective-permute-start.17 = (bf16[512,1024]{1,0:T(8,128)(2,1)S(1)}, bf16[512,1024]{1,0:T(8,128)(2,1)S(1)}, u32[]{:S(2)}, u32[]{:S(2)}) collective-permute-start(bf16[512,1024]{1,0:T(8,128)(2,1)S(1)} %scale.11.refs_2_), channel_id=1, source_target_pairs={{8,0},{16,24},{9,1},{17,25},{10,2},{18,26},{11,3},{19,27},{12,4},{... | collective-permute-start | bytes 3145736 | tf_op jit(solution)/shard_map/ppermute | solution.py:262
  266.0 42.8 %collective-permute-start.19 = (bf16[512,1024]{1,0:T(8,128)(2,1)S(1)}, bf16[512,1024]{1,0:T(8,128)(2,1)S(1)}, u32[]{:S(2)}, u32[]{:S(2)}) collective-permute-start(bf16[512,1024]{1,0:T(8,128)(2,1)S(1)} %collective-permute-done.16.refs_2_), channel_id=1, source_target_pairs={{8,0},{16,24},{9,1},{17,25},{10,2},{18,26},{11,3},{19,27},{12,4},{... | collective-permute-start | bytes 3145736 | tf_op jit(solution)/shard_map/ppermute | solution.py:262
  268.6 256.9 %collective-permute-start.8 = (bf16[1024,1024]{1,0:T(8,128)(2,1)S(1)}, bf16[1024,1024]{1,0:T(8,128)(2,1)S(1)}, u32[]{:S(2)}, u32[]{:S(2)}) collective-permute-start(bf16[1024,1024]{1,0:T(8,128)(2,1)S(1)} %scale.7.refs_2_), channel_id=1, source_target_pairs={{8,0},{16,24},{9,1},{17,25},{10,2},{18,26},{11,3},{19,27},{12,4},{... | collective-permute-start | bytes 6291464 | tf_op jit(solution)/shard_map/ppermute | solution.py:262
  297.5 192.8 %collective-permute-start.25 = (bf16[768,1024]{1,0:T(8,128)(2,1)S(1)}, bf16[768,1024]{1,0:T(8,128)(2,1)S(1)}, u32[]{:S(2)}, u32[]{:S(2)}) collective-permute-start(bf16[768,1024]{1,0:T(8,128)(2,1)S(1)} %collective-permute-done.22.refs_2_), channel_id=1, source_target_pairs={{8,0},{16,24},{9,1},{17,25},{10,2},{18,26},{11,3},{19,27},{12,4},{... | collective-permute-start | bytes 4718600 | tf_op jit(solution)/shard_map/ppermute | solution.py:262
  298.8 232.4 %collective-permute-start.10 = (bf16[1024,1024]{1,0:T(8,128)(2,1)S(1)}, bf16[1024,1024]{1,0:T(8,128)(2,1)S(1)}, u32[]{:S(2)}, u32[]{:S(2)}) collective-permute-start(bf16[1024,1024]{1,0:T(8,128)(2,1)S(1)} %collective-permute-done.9.refs_2_), channel_id=1, source_target_pairs={{8,0},{16,24},{9,1},{17,25},{10,2},{18,26},{11,3},{19,27},{12,4},{... | collective-permute-start | bytes 6291464 | tf_op jit(solution)/shard_map/ppermute | solution.py:262
  308.8 180.3 %collective-permute-start.20 = (bf16[512,1024]{1,0:T(8,128)(2,1)S(1)}, bf16[512,1024]{1,0:T(8,128)(2,1)S(1)}, u32[]{:S(2)}, u32[]{:S(2)}) collective-permute-start(bf16[512,1024]{1,0:T(8,128)(2,1)S(1)} %collective-permute-done.18.refs_2_), channel_id=1, source_target_pairs={{8,0},{16,24},{9,1},{17,25},{10,2},{18,26},{11,3},{19,27},{12,4},{... | collective-permute-start | bytes 3145736 | tf_op jit(solution)/shard_map/ppermute | solution.py:262
  310.1 217.0 %collective-permute-start.29 = (bf16[768,1024]{1,0:T(8,128)(2,1)S(1)}, bf16[768,1024]{1,0:T(8,128)(2,1)S(1)}, u32[]{:S(2)}, u32[]{:S(2)}) collective-permute-start(bf16[768,1024]{1,0:T(8,128)(2,1)S(1)} %collective-permute-done.26.refs_2_), channel_id=1, source_target_pairs={{8,0},{16,24},{9,1},{17,25},{10,2},{18,26},{11,3},{19,27},{12,4},{... | collective-permute-start | bytes 4718600 | tf_op jit(solution)/shard_map/ppermute | solution.py:262
  489.1 35.7 %collective-permute-start.27 = (bf16[256,1024]{1,0:T(8,128)(2,1)}, bf16[256,1024]{1,0:T(8,128)(2,1)S(1)}, u32[]{:S(2)}, u32[]{:S(2)}) collective-permute-start(bf16[256,1024]{1,0:T(8,128)(2,1)} %collective-permute-done.24.refs_2_), channel_id=1, source_target_pairs={{8,0},{16,24},{9,1},{17,25},{10,2},{18,26},{11,3},{19,27},{12,4},{... | collective-permute-start | bytes 1572872 | tf_op jit(solution)/shard_map/ppermute | solution.py:262
  490.4 40.0 %collective-permute-start.30 = (bf16[256,1024]{1,0:T(8,128)(2,1)S(1)}, bf16[256,1024]{1,0:T(8,128)(2,1)S(1)}, u32[]{:S(2)}, u32[]{:S(2)}) collective-permute-start(bf16[256,1024]{1,0:T(8,128)(2,1)S(1)} %collective-permute-done.28.refs_2_), channel_id=1, source_target_pairs={{8,0},{16,24},{9,1},{17,25},{10,2},{18,26},{11,3},{19,27},{12,4},{... | collective-permute-start | bytes 1572872 | tf_op jit(solution)/shard_map/ppermute | solution.py:262
  (3 other events, 2.3 us)

commit v4 on v3

--- a/solution.py
+++ b/solution.py
@@ -67,7 +67,6 @@
         out_specs=pl.BlockSpec((4, cols), lambda i: (0, 0)),
         out_shape=jax.ShapeDtypeStruct((4, cols), jnp.float32),
         scratch_shapes=[pltpu.VMEM((3, 8, cols), jnp.float32)],
-        compiler_params=pltpu.CompilerParams(vmem_limit_bytes=GRANT),
         name="tops",
         cost_estimate=pl.CostEstimate(
             flops=3 * 2 * rows * cols * rank, bytes_accessed=6 * rows * cols, transcendentals=0
@@ -265,9 +264,11 @@
     raw = {"q": sent(1, train_query, train_query)}
     norm = jnp.pad(norm_train + norm_step, (0, cols - norm_train.shape[0])).reshape(1, cols)
     tops = column_tops(trains, lows, highs, norm)
+    ends = {0: 1, count - 1: count - 2} if count > 2 else {0: 1}
+    back = [(neighbour, end) for end, neighbour in ends.items()]
     parts = [tops]
     for s in range(1, count):
-        pairs = [(i, (i + s) % count) for i in range(count) if (i + s) % count]
+        pairs = [(i, (i + s) % count) for i in range(count) if (i + s) % count not in ends]
         parts.append(lax.ppermute(tops, "zero", pairs))
     raw["ka"] = sent(1, train_key[:half], train_key[:half])
     low = jnp.concatenate((lows[0], lows[1]), axis=1)
@@ -284,7 +285,7 @@
         joined = lax.all_gather(joined, "width", axis=2, tiled=True)
     near = {side: joined[index] for index, side in enumerate(sides)}
     joined_tops, norms = join_tops(place, parts)
-    factor = jnp.maximum(joined_tops, lax.ppermute(joined_tops, "zero", [(1, 0)]))
+    factor = jnp.maximum(joined_tops, lax.ppermute(joined_tops, "zero", back))
     raw["kb"] = sent(1, train_key[half:], train_key[half:])
 
     outs, serves = [None] * 3, [None] * 3
@@ -316,8 +317,9 @@
 
     size = norm_train.shape[0]
     narrow = norms[:count, :size].astype(jnp.bfloat16)
-    moved = lax.ppermute(narrow, "zero", [(1, 0)])
-    narrow = jnp.where(place == 0, moved, narrow)
+    moved = lax.ppermute(narrow, "zero", back)
+    at_end = functools.reduce(jnp.logical_or, [place == end for end in ends])
+    narrow = jnp.where(at_end, moved, narrow)
     wide = lax.all_gather(narrow, "width", axis=1, tiled=True)
     serve_norm = wide.reshape(-1)
     return (*outs, factor[0], factor[1], factor[2], serve_norm)

time: 534 us -> 534 us (level)
  waiting for transfers between devices: 416 us -> 425 us
  local copies, waits for them, and re-layouts: 17.5 us -> 9.5 us
    unnamed x39 -> x23, local copies, waits for them, and re-layouts: 11.3 us -> 2.69 us
    ppermute x3, waiting for transfers between devices: 1.4 us -> 8.83 us  [merged_for_serving(): parts.append(lax.ppermute(tops, 'zero', pairs))]
  transfers between devices with their start and end apart: 32 -> 32, of which waited for: 12 -> 13; matrix products, arithmetic and copies ran while one was open for 1% -> 1% of each run, Pallas kernels for 6% -> 7%
where the time goes in v4:
time: 534 us; the launch traced here: 533 us
  waiting for transfers between devices  425 us (80%)
  starting transfers between devices  41.9 us (8%)
  Pallas kernels  37.5 us (7%)
  blocking collectives  16.6 us (3%)
  local copies, waits for them, and re-layouts  9.5 us (2%)
    ppermute x27, waiting for transfers between devices, sent(): moved.append((side, lax.ppermute(x, 'zero', pairs)))  404 us
    ppermute x27, starting transfers between devices, sent(): moved.append((side, lax.ppermute(x, 'zero', pairs)))  32.9 us
    pallas_call x15, Pallas kernels, placed(): pl.pallas_call(functools.partial(place_kernel, hop, sides, at, shard, cou...  17.5 us
  transfers between devices with their start and end apart: 32, of which 13 were waited for; matrix products, arithmetic and copies ran while one was open for 1% of the time, Pallas kernels for 7%

profile of v4, /device:TPU:0, one launch (start us, length us, event | category | flops | bytes accessed | tf_op | source)
XLA Modules:
  0.0 532.7 jit_solution(717481914250538911)
XLA Ops:
  0.7 3.2 fusion.1
  3.9 3.1 collective-permute-start.11
  8.3 6.7 %tops.1.refs_0_ = f32[4,1024]{1,0:T(4,128)} custom-call(bf16[1024,1024]{1,0:T(8,128)(2,1)} %train.3, bf16[1024,1024]{1,0:T(8,128)(2,1)} %train.4, bf16[1024,1024]{1,0:T(8,128)(2,1)} %train.5, bf16[16,1024]{1,0:T(8,128)(2,1)} %bitcast.22, bf16[16,1024]{1,0:T(8,128)(2,1)} %bitcast.19, bf16[16,1024]{1,0:T(8,128)(2,1)} %bitcast.25, bf16[16,1024]{1,0:T(8,128)(2,1)} %high.11, ...), custom_call_target="tpu_custom_call" | custom-call | flops 100663296 | bytes 6291456 | tf_op jit(solution)/shard_map/tops/pallas_call | solution.py:60
  15.0 1.9 collective-permute-start
  16.9 3.9 collective-permute-start.1
  21.5 8.7 %collective-permute-done.refs_1_ = f32[4,1024]{1,0:T(4,128)S(1)} collective-permute-done((f32[4,1024]{1,0:T(4,128)}, f32[4,1024]{1,0:T(4,128)S(1)}, u32[]{:S(2)}, u32[]{:S(2)}) %collective-permute-start) | collective-permute-done | bytes 16416 | tf_op jit(solution)/shard_map/ppermute | solution.py:272
  31.0 1.3 collective-permute-start.3
  32.3 5.0 collective-permute-done.3
  37.4 2.7 own.5
  40.1 1.3 copy-done.3
  42.2 1.5 collective-permute-start.24
  43.7 3.4 collective-permute-start.4
  47.3 51.9 %collective-permute-done.5 = bf16[16,512]{1,0:T(8,128)(2,1)S(1)} collective-permute-done((bf16[16,512]{1,0:T(8,128)(2,1)S(1)}, bf16[16,512]{1,0:T(8,128)(2,1)S(1)}, u32[]{:S(2)}, u32[]{:S(2)}) %collective-permute-start.5) | collective-permute-done | bytes 16416 | tf_op jit(solution)/shard_map/ppermute | solution.py:261
  99.9 1.3 collective-permute-start.31
  101.2 6.8 %collective-permute-done.31 = bf16[4,256]{1,0:T(4,128)(2,1)S(1)} collective-permute-done((bf16[4,256]{1,0:T(4,128)(2,1)S(1)}, bf16[4,256]{1,0:T(4,128)(2,1)S(1)}, u32[]{:S(2)}, u32[]{:S(2)}) %collective-permute-start.31) | collective-permute-done | bytes 2080 | tf_op jit(solution)/shard_map/ppermute | solution.py:320
  108.7 2.2 collective-permute-start.13
  111.6 1.5 slice.37
  113.2 2.4 collective-permute-start.21
  116.3 18.8 %collective-permute-done.13.train = bf16[512,1024]{1,0:T(8,128)(2,1)S(1)} collective-permute-done((bf16[512,1024]{1,0:T(8,128)(2,1)}, bf16[512,1024]{1,0:T(8,128)(2,1)S(1)}, u32[]{:S(2)}, u32[]{:S(2)}) %collective-permute-start.13) | collective-permute-done | bytes 1048608 | tf_op jit(solution)/shard_map/ppermute | solution.py:261
  136.6 8.5 %all_gather.6 = bf16[2,16,2048]{2,1,0:T(8,128)(2,1)S(1)} all-gather(bf16[2,16,512]{2,1,0:T(8,128)(2,1)S(1)} %pad_maximum_fusion), channel_id=1, replica_groups=mesh['zero'=4,'width'=4,'unit'=2] {'width'}, dimensions={2}, use_global_device_ids=true | all-gather | bytes 163840 | tf_op jit(solution)/shard_map/all_gather | solution.py:285
  147.3 1.3 collective-permute-start.15
  148.6 1.4 scale.6.refs_1_
  149.9 13.6 %collective-permute-done.21.refs_1_ = bf16[768,1024]{1,0:T(8,128)(2,1)S(1)} collective-permute-done((bf16[768,1024]{1,0:T(8,128)(2,1)S(1)}, bf16[768,1024]{1,0:T(8,128)(2,1)S(1)}, u32[]{:S(2)}, u32[]{:S(2)}) %collective-permute-start.21) | collective-permute-done | bytes 1572896 | tf_op jit(solution)/shard_map/ppermute | solution.py:261
  167.4 98.6 %collective-permute-done.15.refs_1_ = bf16[512,1024]{1,0:T(8,128)(2,1)S(1)} collective-permute-done((bf16[512,1024]{1,0:T(8,128)(2,1)S(1)}, bf16[512,1024]{1,0:T(8,128)(2,1)S(1)}, u32[]{:S(2)}, u32[]{:S(2)}) %collective-permute-start.15) | collective-permute-done | bytes 1048608 | tf_op jit(solution)/shard_map/ppermute | solution.py:261
  265.9 1.3 collective-permute-start.17
  267.2 1.3 collective-permute-start.19
  268.5 1.4 scale.7.refs_2_
  269.9 1.3 collective-permute-start.8
  271.2 27.6 %collective-permute-done.17.refs_1_ = bf16[512,1024]{1,0:T(8,128)(2,1)S(1)} collective-permute-done((bf16[512,1024]{1,0:T(8,128)(2,1)S(1)}, bf16[512,1024]{1,0:T(8,128)(2,1)S(1)}, u32[]{:S(2)}, u32[]{:S(2)}) %collective-permute-start.17) | collective-permute-done | bytes 1048608 | tf_op jit(solution)/shard_map/ppermute | solution.py:261
  298.8 1.3 collective-permute-start.25
  300.1 1.3 collective-permute-start.10
  301.4 8.6 %collective-permute-done.19.refs_1_ = bf16[512,1024]{1,0:T(8,128)(2,1)S(1)} collective-permute-done((bf16[512,1024]{1,0:T(8,128)(2,1)S(1)}, bf16[512,1024]{1,0:T(8,128)(2,1)S(1)}, u32[]{:S(2)}, u32[]{:S(2)}) %collective-permute-start.19) | collective-permute-done | bytes 1048608 | tf_op jit(solution)/shard_map/ppermute | solution.py:261
  310.0 1.3 collective-permute-start.20
  311.3 1.3 collective-permute-start.29
  312.6 175.0 %collective-permute-done.20.refs_1_ = bf16[512,1024]{1,0:T(8,128)(2,1)S(1)} collective-permute-done((bf16[512,1024]{1,0:T(8,128)(2,1)S(1)}, bf16[512,1024]{1,0:T(8,128)(2,1)S(1)}, u32[]{:S(2)}, u32[]{:S(2)}) %collective-permute-start.20) | collective-permute-done | bytes 1048608 | tf_op jit(solution)/shard_map/ppermute | solution.py:261
  487.7 1.3 collective-permute-start.27
  489.0 1.3 collective-permute-start.30
  490.3 8.1 %all_gather.7 = bf16[4,1024]{1,0:T(4,128)(2,1)S(1)} all-gather(bf16[4,256]{1,0:T(4,128)(2,1)S(1)} %broadcast_select_fusion), channel_id=1, replica_groups=mesh['zero'=4,'width'=4,'unit'=2] {'width'}, dimensions={1}, use_global_device_ids=true | all-gather | bytes 10240 | tf_op jit(solution)/shard_map/all_gather | solution.py:323
  499.0 2.6 own.4.refs_0_
  501.6 2.6 own.3.refs_0_
  506.8 1.2 place.24.refs_0_
  508.0 2.0 place.25.refs_0_
  512.1 1.4 place.15.refs_0_
  515.5 1.2 place.26.refs_0_
  516.7 8.1 %collective-permute-done.27.refs_1_ = bf16[256,1024]{1,0:T(8,128)(2,1)S(1)} collective-permute-done((bf16[256,1024]{1,0:T(8,128)(2,1)}, bf16[256,1024]{1,0:T(8,128)(2,1)S(1)}, u32[]{:S(2)}, u32[]{:S(2)}) %collective-permute-start.27) | collective-permute-done | bytes 524320 | tf_op jit(solution)/shard_map/ppermute | solution.py:261
  525.7 1.4 place.16.refs_0_
  528.3 2.2 collective-permute-done.30.refs_1_
  531.3 1.4 place.17
  (79 shorter events, 24.3 us)
Async XLA Ops:
  0.6 46.5 %copy-start.7 = (bf16[1024,16]{0,1:T(8,128)(2,1)S(1)}, bf16[1024,16]{0,1:T(8,128)(2,1)}, u32[]{:S(2)}) copy-start(bf16[1024,16]{0,1:T(8,128)(2,1)} %param.12) | copy-start | bytes 98308
  0.6 46.5 %copy-start.6 = (bf16[1024,16]{0,1:T(8,128)(2,1)S(1)}, bf16[1024,16]{0,1:T(8,128)(2,1)}, u32[]{:S(2)}) copy-start(bf16[1024,16]{0,1:T(8,128)(2,1)} %param.15) | copy-start | bytes 98308
  0.7 36.7 %copy-start.8 = (bf16[1024,16]{0,1:T(8,128)(2,1)S(1)}, bf16[1024,16]{0,1:T(8,128)(2,1)}, u32[]{:S(2)}) copy-start(bf16[1024,16]{0,1:T(8,128)(2,1)} %param.18) | copy-start | bytes 98308
  0.7 144.4 %copy-start.4 = (bf16[16,1024]{1,0:T(8,128)(2,1)S(1)}, bf16[16,1024]{1,0:T(8,128)(2,1)}, u32[]{:S(2)}) copy-start(bf16[16,1024]{1,0:T(8,128)(2,1)} %high.16) | copy-start | bytes 98308
  0.7 36.7 %copy-start.1 = (bf16[1024,1024]{1,0:T(8,128)(2,1)S(1)}, bf16[1024,1024]{1,0:T(8,128)(2,1)}, u32[]{:S(2)}) copy-start(bf16[1024,1024]{1,0:T(8,128)(2,1)} %train.5) | copy-start | bytes 6291460
  0.7 36.7 %copy-start.9 = (bf16[16,1024]{1,0:T(8,128)(2,1)S(1)}, bf16[16,1024]{1,0:T(8,128)(2,1)}, u32[]{:S(2)}) copy-start(bf16[16,1024]{1,0:T(8,128)(2,1)} %high.17) | copy-start | bytes 98308
  3.9 109.2 %collective-permute-start.11 = (bf16[512,1024]{1,0:T(8,128)(2,1)}, bf16[512,1024]{1,0:T(8,128)(2,1)S(1)}, u32[]{:S(2)}, u32[]{:S(2)}) collective-permute-start(bf16[512,1024]{1,0:T(8,128)(2,1)} %get-tuple-element.16), channel_id=1, source_target_pairs={{0,8},{8,0},{16,24},{24,16},{1,9},{9,1},{17,25},{25,17},{2,10},{10... | collective-permute-start | bytes 3145736 | tf_op jit(solution)/shard_map/ppermute | solution.py:261
  8.3 140.3 %copy-start.5 = (bf16[16,1024]{1,0:T(8,128)(2,1)S(1)}, bf16[16,1024]{1,0:T(8,128)(2,1)}, u32[]{:S(2)}) copy-start(bf16[16,1024]{1,0:T(8,128)(2,1)} %high.11) | copy-start | bytes 98308
  15.0 15.1 %collective-permute-start = (f32[4,1024]{1,0:T(4,128)}, f32[4,1024]{1,0:T(4,128)S(1)}, u32[]{:S(2)}, u32[]{:S(2)}) collective-permute-start(f32[4,1024]{1,0:T(4,128)} %tops.1.refs_0_), channel_id=1, source_target_pairs={{0,8},{8,16},{1,9},{9,17},{2,10},{10,18},{3,11},{11,19},{4,12},{12... | collective-permute-start | bytes 49160 | tf_op jit(solution)/shard_map/ppermute | solution.py:272
  16.9 13.4 %collective-permute-start.1 = (f32[4,1024]{1,0:T(4,128)}, f32[4,1024]{1,0:T(4,128)S(1)}, u32[]{:S(2)}, u32[]{:S(2)}) collective-permute-start(f32[4,1024]{1,0:T(4,128)} %tops.1.refs_0_), channel_id=1, source_target_pairs={{0,16},{24,8},{1,17},{25,9},{2,18},{26,10},{3,19},{27,11},{4,20},{... | collective-permute-start | bytes 49160 | tf_op jit(solution)/shard_map/ppermute | solution.py:272
  20.8 9.5 %collective-permute-start.2 = (f32[4,1024]{1,0:T(4,128)}, f32[4,1024]{1,0:T(4,128)S(1)}, u32[]{:S(2)}, u32[]{:S(2)}) collective-permute-start(f32[4,1024]{1,0:T(4,128)} %tops.1.refs_0_), channel_id=1, source_target_pairs={{16,8},{24,16},{17,9},{25,17},{18,10},{26,18},{19,11},{27,19},{20,... | collective-permute-start | bytes 49160 | tf_op jit(solution)/shard_map/ppermute | solution.py:272
  30.3 0.7 copy-start.10
  31.0 6.3 %collective-permute-start.3 = (f32[4,1024]{1,0:T(4,128)S(1)}, f32[4,1024]{1,0:T(4,128)S(1)}, u32[]{:S(2)}, u32[]{:S(2)}) collective-permute-start(f32[4,1024]{1,0:T(4,128)S(1)} %get-tuple-element.11), channel_id=1, source_target_pairs={{8,0},{16,24},{9,1},{17,25},{10,2},{18,26},{11,3},{19,27},{12,4},{... | collective-permute-start | bytes 49160 | tf_op jit(solution)/shard_map/ppermute | solution.py:288
  40.1 1.3 copy-start.3
  42.2 66.4 %collective-permute-start.23 = (bf16[256,1024]{1,0:T(8,128)(2,1)}, bf16[256,1024]{1,0:T(8,128)(2,1)}, u32[]{:S(2)}, u32[]{:S(2)}) collective-permute-start(bf16[256,1024]{1,0:T(8,128)(2,1)} %slice.38), channel_id=1, source_target_pairs={{0,8},{8,0},{16,24},{24,16},{1,9},{9,1},{17,25},{25,17},{2,10},{10... | collective-permute-start | bytes 1572872 | tf_op jit(solution)/shard_map/ppermute | solution.py:261
  42.2 68.6 %collective-permute-start.24 = (bf16[256,1024]{1,0:T(8,128)(2,1)}, bf16[256,1024]{1,0:T(8,128)(2,1)}, u32[]{:S(2)}, u32[]{:S(2)}) collective-permute-start(bf16[256,1024]{1,0:T(8,128)(2,1)} %slice.38), channel_id=1, source_target_pairs={{8,16},{16,8},{9,17},{17,9},{10,18},{18,10},{11,19},{19,11},{12,20... | collective-permute-start | bytes 1572872 | tf_op jit(solution)/shard_map/ppermute | solution.py:261
  43.7 103.5 %collective-permute-start.4 = (bf16[1024,1024]{1,0:T(8,128)(2,1)}, bf16[1024,1024]{1,0:T(8,128)(2,1)S(1)}, u32[]{:S(2)}, u32[]{:S(2)}) collective-permute-start(bf16[1024,1024]{1,0:T(8,128)(2,1)} %train.3), channel_id=1, source_target_pairs={{0,8},{8,0},{16,24},{24,16},{1,9},{9,1},{17,25},{25,17},{2,10},{10... | collective-permute-start | bytes 6291464 | tf_op jit(solution)/shard_map/ppermute | solution.py:261
  47.2 52.0 %collective-permute-start.5 = (bf16[16,512]{1,0:T(8,128)(2,1)S(1)}, bf16[16,512]{1,0:T(8,128)(2,1)S(1)}, u32[]{:S(2)}, u32[]{:S(2)}) collective-permute-start(bf16[16,512]{1,0:T(8,128)(2,1)S(1)} %fusion), channel_id=1, source_target_pairs={{0,8},{8,0},{16,24},{24,16},{1,9},{9,1},{17,25},{25,17},{2,10},{10... | collective-permute-start | bytes 49160 | tf_op jit(solution)/shard_map/ppermute | solution.py:261
  99.2 0.7 collective-permute-start.6
  99.9 8.1 %collective-permute-start.31 = (bf16[4,256]{1,0:T(4,128)(2,1)S(1)}, bf16[4,256]{1,0:T(4,128)(2,1)S(1)}, u32[]{:S(2)}, u32[]{:S(2)}) collective-permute-start(bf16[4,256]{1,0:T(4,128)(2,1)S(1)} %slice.52), channel_id=1, source_target_pairs={{8,0},{16,24},{9,1},{17,25},{10,2},{18,26},{11,3},{19,27},{12,4},{... | collective-permute-start | bytes 6152 | tf_op jit(solution)/shard_map/ppermute | solution.py:320
  108.0 7.6 %collective-permute-start.12 = (bf16[512,1024]{1,0:T(8,128)(2,1)}, bf16[512,1024]{1,0:T(8,128)(2,1)S(1)}, u32[]{:S(2)}, u32[]{:S(2)}) collective-permute-start(bf16[512,1024]{1,0:T(8,128)(2,1)} %get-tuple-element.16), channel_id=1, source_target_pairs={{8,16},{16,8},{9,17},{17,9},{10,18},{18,10},{11,19},{19,11},{12,20... | collective-permute-start | bytes 3145736 | tf_op jit(solution)/shard_map/ppermute | solution.py:261
  108.7 26.4 %collective-permute-start.13 = (bf16[512,1024]{1,0:T(8,128)(2,1)}, bf16[512,1024]{1,0:T(8,128)(2,1)S(1)}, u32[]{:S(2)}, u32[]{:S(2)}) collective-permute-start(bf16[512,1024]{1,0:T(8,128)(2,1)} %get-tuple-element.15), channel_id=1, source_target_pairs={{0,8},{8,0},{16,24},{24,16},{1,9},{9,1},{17,25},{25,17},{2,10},{10... | collective-permute-start | bytes 3145736 | tf_op jit(solution)/shard_map/ppermute | solution.py:261
  110.9 25.0 %collective-permute-start.14 = (bf16[512,1024]{1,0:T(8,128)(2,1)}, bf16[512,1024]{1,0:T(8,128)(2,1)S(1)}, u32[]{:S(2)}, u32[]{:S(2)}) collective-permute-start(bf16[512,1024]{1,0:T(8,128)(2,1)} %get-tuple-element.15), channel_id=1, source_target_pairs={{8,16},{16,8},{9,17},{17,9},{10,18},{18,10},{11,19},{19,11},{12,20... | collective-permute-start | bytes 3145736 | tf_op jit(solution)/shard_map/ppermute | solution.py:261
  113.2 50.4 %collective-permute-start.21 = (bf16[768,1024]{1,0:T(8,128)(2,1)S(1)}, bf16[768,1024]{1,0:T(8,128)(2,1)S(1)}, u32[]{:S(2)}, u32[]{:S(2)}) collective-permute-start(bf16[768,1024]{1,0:T(8,128)(2,1)S(1)} %slice.37), channel_id=1, source_target_pairs={{0,8},{8,0},{16,24},{24,16},{1,9},{9,1},{17,25},{25,17},{2,10},{10... | collective-permute-start | bytes 4718600 | tf_op jit(solution)/shard_map/ppermute | solution.py:261
  115.5 151.7 %collective-permute-start.7 = (bf16[1024,1024]{1,0:T(8,128)(2,1)}, bf16[1024,1024]{1,0:T(8,128)(2,1)S(1)}, u32[]{:S(2)}, u32[]{:S(2)}) collective-permute-start(bf16[1024,1024]{1,0:T(8,128)(2,1)} %train.3), channel_id=1, source_target_pairs={{8,16},{16,8},{9,17},{17,9},{10,18},{18,10},{11,19},{19,11},{12,20... | collective-permute-start | bytes 6291464 | tf_op jit(solution)/shard_map/ppermute | solution.py:261
  135.1 29.9 %collective-permute-start.22 = (bf16[768,1024]{1,0:T(8,128)(2,1)S(1)}, bf16[768,1024]{1,0:T(8,128)(2,1)S(1)}, u32[]{:S(2)}, u32[]{:S(2)}) collective-permute-start(bf16[768,1024]{1,0:T(8,128)(2,1)S(1)} %slice.37), channel_id=1, source_target_pairs={{8,16},{16,8},{9,17},{17,9},{10,18},{18,10},{11,19},{19,11},{12,20... | collective-permute-start | bytes 4718600 | tf_op jit(solution)/shard_map/ppermute | solution.py:261
  135.9 10.6 %collective-permute-start.28 = (bf16[256,1024]{1,0:T(8,128)(2,1)}, bf16[256,1024]{1,0:T(8,128)(2,1)S(1)}, u32[]{:S(2)}, u32[]{:S(2)}) collective-permute-start(bf16[256,1024]{1,0:T(8,128)(2,1)} %collective-permute-done.23.refs_1_), channel_id=1, source_target_pairs={{8,16},{16,8},{9,17},{17,9},{10,18},{18,10},{11,19},{19,11},{12,20... | collective-permute-start | bytes 1572872 | tf_op jit(solution)/shard_map/ppermute | solution.py:261
  145.1 353.9 %copy-start = (bf16[1024,1024]{1,0:T(8,128)(2,1)S(1)}, bf16[1024,1024]{1,0:T(8,128)(2,1)}, u32[]{:S(2)}) copy-start(bf16[1024,1024]{1,0:T(8,128)(2,1)} %train.4) | copy-start | bytes 6291460
  146.5 20.1 %collective-permute-start.16 = (bf16[512,1024]{1,0:T(8,128)(2,1)S(1)}, bf16[512,1024]{1,0:T(8,128)(2,1)S(1)}, u32[]{:S(2)}, u32[]{:S(2)}) collective-permute-start(bf16[512,1024]{1,0:T(8,128)(2,1)S(1)} %scale.8.refs_1_), channel_id=1, source_target_pairs={{8,16},{16,8},{9,17},{17,9},{10,18},{18,10},{11,19},{19,11},{12,20... | collective-permute-start | bytes 3145736 | tf_op jit(solution)/shard_map/ppermute | solution.py:261
  147.3 118.7 %collective-permute-start.15 = (bf16[512,1024]{1,0:T(8,128)(2,1)S(1)}, bf16[512,1024]{1,0:T(8,128)(2,1)S(1)}, u32[]{:S(2)}, u32[]{:S(2)}) collective-permute-start(bf16[512,1024]{1,0:T(8,128)(2,1)S(1)} %scale.9.refs_2_), channel_id=1, source_target_pairs={{8,0},{16,24},{9,1},{17,25},{10,2},{18,26},{11,3},{19,27},{12,4},{... | collective-permute-start | bytes 3145736 | tf_op jit(solution)/shard_map/ppermute | solution.py:261
  163.5 136.6 %collective-permute-start.9 = (bf16[1024,1024]{1,0:T(8,128)(2,1)S(1)}, bf16[1024,1024]{1,0:T(8,128)(2,1)S(1)}, u32[]{:S(2)}, u32[]{:S(2)}) collective-permute-start(bf16[1024,1024]{1,0:T(8,128)(2,1)S(1)} %scale.6.refs_1_), channel_id=1, source_target_pairs={{8,16},{16,8},{9,17},{17,9},{10,18},{18,10},{11,19},{19,11},{12,20... | collective-permute-start | bytes 6291464 | tf_op jit(solution)/shard_map/ppermute | solution.py:261
  165.0 336.6 %copy-start.2 = (bf16[1024,1024]{1,0:T(8,128)(2,1)S(1)}, bf16[1024,1024]{1,0:T(8,128)(2,1)}, u32[]{:S(2)}) copy-start(bf16[1024,1024]{1,0:T(8,128)(2,1)} %train.3) | copy-start | bytes 6291460
  165.0 104.9 %collective-permute-start.18 = (bf16[512,1024]{1,0:T(8,128)(2,1)S(1)}, bf16[512,1024]{1,0:T(8,128)(2,1)S(1)}, u32[]{:S(2)}, u32[]{:S(2)}) collective-permute-start(bf16[512,1024]{1,0:T(8,128)(2,1)S(1)} %scale.10.refs_1_), channel_id=1, source_target_pairs={{8,16},{16,8},{9,17},{17,9},{10,18},{18,10},{11,19},{19,11},{12,20... | collective-permute-start | bytes 3145736 | tf_op jit(solution)/shard_map/ppermute | solution.py:261
  166.6 144.7 %collective-permute-start.26 = (bf16[768,1024]{1,0:T(8,128)(2,1)S(1)}, bf16[768,1024]{1,0:T(8,128)(2,1)S(1)}, u32[]{:S(2)}, u32[]{:S(2)}) collective-permute-start(bf16[768,1024]{1,0:T(8,128)(2,1)S(1)} %collective-permute-done.21.refs_1_), channel_id=1, source_target_pairs={{8,16},{16,8},{9,17},{17,9},{10,18},{18,10},{11,19},{19,11},{12,20... | collective-permute-start | bytes 4718600 | tf_op jit(solution)/shard_map/ppermute | solution.py:261
  265.9 32.9 %collective-permute-start.17 = (bf16[512,1024]{1,0:T(8,128)(2,1)S(1)}, bf16[512,1024]{1,0:T(8,128)(2,1)S(1)}, u32[]{:S(2)}, u32[]{:S(2)}) collective-permute-start(bf16[512,1024]{1,0:T(8,128)(2,1)S(1)} %scale.11.refs_2_), channel_id=1, source_target_pairs={{8,0},{16,24},{9,1},{17,25},{10,2},{18,26},{11,3},{19,27},{12,4},{... | collective-permute-start | bytes 3145736 | tf_op jit(solution)/shard_map/ppermute | solution.py:261
  267.2 42.8 %collective-permute-start.19 = (bf16[512,1024]{1,0:T(8,128)(2,1)S(1)}, bf16[512,1024]{1,0:T(8,128)(2,1)S(1)}, u32[]{:S(2)}, u32[]{:S(2)}) collective-permute-start(bf16[512,1024]{1,0:T(8,128)(2,1)S(1)} %collective-permute-done.16.refs_2_), channel_id=1, source_target_pairs={{8,0},{16,24},{9,1},{17,25},{10,2},{18,26},{11,3},{19,27},{12,4},{... | collective-permute-start | bytes 3145736 | tf_op jit(solution)/shard_map/ppermute | solution.py:261
  269.9 255.8 %collective-permute-start.8 = (bf16[1024,1024]{1,0:T(8,128)(2,1)S(1)}, bf16[1024,1024]{1,0:T(8,128)(2,1)S(1)}, u32[]{:S(2)}, u32[]{:S(2)}) collective-permute-start(bf16[1024,1024]{1,0:T(8,128)(2,1)S(1)} %scale.7.refs_2_), channel_id=1, source_target_pairs={{8,0},{16,24},{9,1},{17,25},{10,2},{18,26},{11,3},{19,27},{12,4},{... | collective-permute-start | bytes 6291464 | tf_op jit(solution)/shard_map/ppermute | solution.py:261
  298.8 190.2 %collective-permute-start.25 = (bf16[768,1024]{1,0:T(8,128)(2,1)S(1)}, bf16[768,1024]{1,0:T(8,128)(2,1)S(1)}, u32[]{:S(2)}, u32[]{:S(2)}) collective-permute-start(bf16[768,1024]{1,0:T(8,128)(2,1)S(1)} %collective-permute-done.22.refs_2_), channel_id=1, source_target_pairs={{8,0},{16,24},{9,1},{17,25},{10,2},{18,26},{11,3},{19,27},{12,4},{... | collective-permute-start | bytes 4718600 | tf_op jit(solution)/shard_map/ppermute | solution.py:261
  300.1 231.2 %collective-permute-start.10 = (bf16[1024,1024]{1,0:T(8,128)(2,1)S(1)}, bf16[1024,1024]{1,0:T(8,128)(2,1)S(1)}, u32[]{:S(2)}, u32[]{:S(2)}) collective-permute-start(bf16[1024,1024]{1,0:T(8,128)(2,1)S(1)} %collective-permute-done.9.refs_2_), channel_id=1, source_target_pairs={{8,0},{16,24},{9,1},{17,25},{10,2},{18,26},{11,3},{19,27},{12,4},{... | collective-permute-start | bytes 6291464 | tf_op jit(solution)/shard_map/ppermute | solution.py:261
  310.0 177.6 %collective-permute-start.20 = (bf16[512,1024]{1,0:T(8,128)(2,1)S(1)}, bf16[512,1024]{1,0:T(8,128)(2,1)S(1)}, u32[]{:S(2)}, u32[]{:S(2)}) collective-permute-start(bf16[512,1024]{1,0:T(8,128)(2,1)S(1)} %collective-permute-done.18.refs_2_), channel_id=1, source_target_pairs={{8,0},{16,24},{9,1},{17,25},{10,2},{18,26},{11,3},{19,27},{12,4},{... | collective-permute-start | bytes 3145736 | tf_op jit(solution)/shard_map/ppermute | solution.py:261
  311.3 215.8 %collective-permute-start.29 = (bf16[768,1024]{1,0:T(8,128)(2,1)S(1)}, bf16[768,1024]{1,0:T(8,128)(2,1)S(1)}, u32[]{:S(2)}, u32[]{:S(2)}) collective-permute-start(bf16[768,1024]{1,0:T(8,128)(2,1)S(1)} %collective-permute-done.26.refs_2_), channel_id=1, source_target_pairs={{8,0},{16,24},{9,1},{17,25},{10,2},{18,26},{11,3},{19,27},{12,4},{... | collective-permute-start | bytes 4718600 | tf_op jit(solution)/shard_map/ppermute | solution.py:261
  487.7 37.2 %collective-permute-start.27 = (bf16[256,1024]{1,0:T(8,128)(2,1)}, bf16[256,1024]{1,0:T(8,128)(2,1)S(1)}, u32[]{:S(2)}, u32[]{:S(2)}) collective-permute-start(bf16[256,1024]{1,0:T(8,128)(2,1)} %collective-permute-done.24.refs_2_), channel_id=1, source_target_pairs={{8,0},{16,24},{9,1},{17,25},{10,2},{18,26},{11,3},{19,27},{12,4},{... | collective-permute-start | bytes 1572872 | tf_op jit(solution)/shard_map/ppermute | solution.py:261
  489.0 41.5 %collective-permute-start.30 = (bf16[256,1024]{1,0:T(8,128)(2,1)S(1)}, bf16[256,1024]{1,0:T(8,128)(2,1)S(1)}, u32[]{:S(2)}, u32[]{:S(2)}) collective-permute-start(bf16[256,1024]{1,0:T(8,128)(2,1)S(1)} %collective-permute-done.28.refs_2_), channel_id=1, source_target_pairs={{8,0},{16,24},{9,1},{17,25},{10,2},{18,26},{11,3},{19,27},{12,4},{... | collective-permute-start | bytes 1572872 | tf_op jit(solution)/shard_map/ppermute | solution.py:261

commit v5 on v4

--- a/solution.py
+++ b/solution.py
@@ -31,7 +31,7 @@
     return train.astype(jnp.float32) + mix_rate * step
 
 
-def top_kernel(tq, tk, tv, lq, lk, lv, hq, hk, hv, norm, out, acc):
+def top_kernel(tq, tk, tv, lq, lk, lv, hq, hk, hv, trained, moved, out, acc):
     step = pl.program_id(0)
     for index, (t, l, h) in enumerate(((tq, lq, hq), (tk, lk, hk), (tv, lv, hv))):
         size = jnp.abs(merged(t[...], l[...], h[...]))
@@ -50,10 +50,11 @@
     def _():
         for index in range(3):
             out[pl.ds(index, 1), :] = jnp.max(acc[index], axis=0, keepdims=True)
-        out[pl.ds(3, 1), :] = norm[...]
-
-
-def column_tops(trains, lows, highs, norm):
+        out[pl.ds(3, 1), :] = jnp.zeros((1, out.shape[1]), jnp.float32)
+        out[pl.ds(3, 1), pl.ds(0, trained.shape[1])] = trained[...] + moved[...]
+
+
+def column_tops(trains, lows, highs, norms):
     rows, cols = trains[0].shape
     rank = lows[0].shape[0]
     tile = tile_of(rows)
@@ -63,7 +64,7 @@
         in_specs=[pl.BlockSpec((tile, cols), lambda i: (i, 0))] * 3
         + [pl.BlockSpec((rank, tile), lambda i: (0, i))] * 3
         + [pl.BlockSpec((rank, cols), lambda i: (0, 0))] * 3
-        + [pl.BlockSpec((1, cols), lambda i: (0, 0))],
+        + [pl.BlockSpec(norms[0].shape, lambda i: (0, 0))] * 2,
         out_specs=pl.BlockSpec((4, cols), lambda i: (0, 0)),
         out_shape=jax.ShapeDtypeStruct((4, cols), jnp.float32),
         scratch_shapes=[pltpu.VMEM((3, 8, cols), jnp.float32)],
@@ -71,7 +72,7 @@
         cost_estimate=pl.CostEstimate(
             flops=3 * 2 * rows * cols * rank, bytes_accessed=6 * rows * cols, transcendentals=0
         ),
-    )(*trains, *lows, *highs, norm)
+    )(*trains, *lows, *highs, *norms)
 
 
 def join_kernel(count, place, *refs):
@@ -246,7 +247,7 @@
     norm_train,
     norm_step,
 ):
-    rows, cols = train_query.shape
+    rows, _ = train_query.shape
     half = rows // 2
     place = lax.axis_index("zero").astype(jnp.int32).reshape(1)
     lows = (low_query.T, low_key.T, low_value.T)
@@ -262,8 +263,8 @@
         return moved
 
     raw = {"q": sent(1, train_query, train_query)}
-    norm = jnp.pad(norm_train + norm_step, (0, cols - norm_train.shape[0])).reshape(1, cols)
-    tops = column_tops(trains, lows, highs, norm)
+    gains = norm_train.reshape(1, -1), norm_step.reshape(1, -1)
+    tops = column_tops(trains, lows, highs, gains)
     ends = {0: 1, count - 1: count - 2} if count > 2 else {0: 1}
     back = [(neighbour, end) for end, neighbour in ends.items()]
     parts = [tops]

time: 534 us -> 534 us (level)
  no operation moved by 1% of the time
where the time goes in v5:
time: 534 us; the launch traced here: 533 us
  waiting for transfers between devices  426 us (80%)
  starting transfers between devices  41.9 us (8%)
  Pallas kernels  37.5 us (7%)
  blocking collectives  16.6 us (3%)
  local copies, waits for them, and re-layouts  8.91 us (2%)
    ppermute x27, waiting for transfers between devices, sent(): moved.append((side, lax.ppermute(x, 'zero', pairs)))  404 us
    ppermute x27, starting transfers between devices, sent(): moved.append((side, lax.ppermute(x, 'zero', pairs)))  32.9 us
    pallas_call x15, Pallas kernels, placed(): pl.pallas_call(functools.partial(place_kernel, hop, sides, at, shard, cou...  17.5 us
  transfers between devices with their start and end apart: 32, of which 13 were waited for; matrix products, arithmetic and copies ran while one was open for 1% of the time, Pallas kernels for 7%

profile of v5, /device:TPU:0, one launch (start us, length us, event | category | flops | bytes accessed | tf_op | source)
XLA Modules:
  0.0 532.7 jit_solution(16635820591738347827)
XLA Ops:
  0.7 3.2 fusion.1
  3.9 3.1 collective-permute-start.11
  7.0 6.7 %tops.1.refs_0_ = f32[4,1024]{1,0:T(4,128)} custom-call(bf16[1024,1024]{1,0:T(8,128)(2,1)} %train.3, bf16[1024,1024]{1,0:T(8,128)(2,1)} %train.4, bf16[1024,1024]{1,0:T(8,128)(2,1)} %train.5, bf16[16,1024]{1,0:T(8,128)(2,1)} %bitcast.23, bf16[16,1024]{1,0:T(8,128)(2,1)} %bitcast.20, bf16[16,1024]{1,0:T(8,128)(2,1)} %bitcast.26, bf16[16,1024]{1,0:T(8,128)(2,1)} %high.11, ...), custom_call_target="tpu_custom_call" | custom-call | flops 100663296 | bytes 6291456 | tf_op jit(solution)/shard_map/tops/pallas_call | solution.py:61
  13.7 1.9 collective-permute-start
  15.6 3.9 collective-permute-start.1
  20.2 9.9 %collective-permute-done.refs_1_ = f32[4,1024]{1,0:T(4,128)S(1)} collective-permute-done((f32[4,1024]{1,0:T(4,128)}, f32[4,1024]{1,0:T(4,128)S(1)}, u32[]{:S(2)}, u32[]{:S(2)}) %collective-permute-start) | collective-permute-done | bytes 16416 | tf_op jit(solution)/shard_map/ppermute | solution.py:273
  31.0 1.3 collective-permute-start.3
  32.3 5.0 collective-permute-done.3
  37.4 2.7 own.5
  40.1 1.3 copy-done.3
  42.2 1.5 collective-permute-start.24
  43.7 3.4 collective-permute-start.4
  47.3 51.9 %collective-permute-done.5 = bf16[16,512]{1,0:T(8,128)(2,1)S(1)} collective-permute-done((bf16[16,512]{1,0:T(8,128)(2,1)S(1)}, bf16[16,512]{1,0:T(8,128)(2,1)S(1)}, u32[]{:S(2)}, u32[]{:S(2)}) %collective-permute-start.5) | collective-permute-done | bytes 16416 | tf_op jit(solution)/shard_map/ppermute | solution.py:262
  99.9 1.3 collective-permute-start.31
  101.2 6.8 %collective-permute-done.31 = bf16[4,256]{1,0:T(4,128)(2,1)S(1)} collective-permute-done((bf16[4,256]{1,0:T(4,128)(2,1)S(1)}, bf16[4,256]{1,0:T(4,128)(2,1)S(1)}, u32[]{:S(2)}, u32[]{:S(2)}) %collective-permute-start.31) | collective-permute-done | bytes 2080 | tf_op jit(solution)/shard_map/ppermute | solution.py:321
  108.7 2.2 collective-permute-start.13
  111.6 1.5 slice.37
  113.2 2.4 collective-permute-start.21
  116.3 18.8 %collective-permute-done.13.train = bf16[512,1024]{1,0:T(8,128)(2,1)S(1)} collective-permute-done((bf16[512,1024]{1,0:T(8,128)(2,1)}, bf16[512,1024]{1,0:T(8,128)(2,1)S(1)}, u32[]{:S(2)}, u32[]{:S(2)}) %collective-permute-start.13) | collective-permute-done | bytes 1048608 | tf_op jit(solution)/shard_map/ppermute | solution.py:262
  136.6 8.5 %all_gather.6 = bf16[2,16,2048]{2,1,0:T(8,128)(2,1)S(1)} all-gather(bf16[2,16,512]{2,1,0:T(8,128)(2,1)S(1)} %pad_maximum_fusion), channel_id=1, replica_groups=mesh['zero'=4,'width'=4,'unit'=2] {'width'}, dimensions={2}, use_global_device_ids=true | all-gather | bytes 163840 | tf_op jit(solution)/shard_map/all_gather | solution.py:286
  147.3 1.3 collective-permute-start.15
  148.6 1.4 scale.6.refs_1_
  149.9 13.6 %collective-permute-done.21.refs_1_ = bf16[768,1024]{1,0:T(8,128)(2,1)S(1)} collective-permute-done((bf16[768,1024]{1,0:T(8,128)(2,1)S(1)}, bf16[768,1024]{1,0:T(8,128)(2,1)S(1)}, u32[]{:S(2)}, u32[]{:S(2)}) %collective-permute-start.21) | collective-permute-done | bytes 1572896 | tf_op jit(solution)/shard_map/ppermute | solution.py:262
  167.4 98.6 %collective-permute-done.15.refs_1_ = bf16[512,1024]{1,0:T(8,128)(2,1)S(1)} collective-permute-done((bf16[512,1024]{1,0:T(8,128)(2,1)S(1)}, bf16[512,1024]{1,0:T(8,128)(2,1)S(1)}, u32[]{:S(2)}, u32[]{:S(2)}) %collective-permute-start.15) | collective-permute-done | bytes 1048608 | tf_op jit(solution)/shard_map/ppermute | solution.py:262
  265.9 1.3 collective-permute-start.17
  267.2 1.3 collective-permute-start.19
  268.5 1.4 scale.7.refs_2_
  269.9 1.3 collective-permute-start.8
  271.2 27.6 %collective-permute-done.17.refs_1_ = bf16[512,1024]{1,0:T(8,128)(2,1)S(1)} collective-permute-done((bf16[512,1024]{1,0:T(8,128)(2,1)S(1)}, bf16[512,1024]{1,0:T(8,128)(2,1)S(1)}, u32[]{:S(2)}, u32[]{:S(2)}) %collective-permute-start.17) | collective-permute-done | bytes 1048608 | tf_op jit(solution)/shard_map/ppermute | solution.py:262
  298.8 1.3 collective-permute-start.25
  300.1 1.3 collective-permute-start.10
  301.4 8.6 %collective-permute-done.19.refs_1_ = bf16[512,1024]{1,0:T(8,128)(2,1)S(1)} collective-permute-done((bf16[512,1024]{1,0:T(8,128)(2,1)S(1)}, bf16[512,1024]{1,0:T(8,128)(2,1)S(1)}, u32[]{:S(2)}, u32[]{:S(2)}) %collective-permute-start.19) | collective-permute-done | bytes 1048608 | tf_op jit(solution)/shard_map/ppermute | solution.py:262
  310.0 1.3 collective-permute-start.20
  311.3 1.3 collective-permute-start.29
  312.6 175.0 %collective-permute-done.20.refs_1_ = bf16[512,1024]{1,0:T(8,128)(2,1)S(1)} collective-permute-done((bf16[512,1024]{1,0:T(8,128)(2,1)S(1)}, bf16[512,1024]{1,0:T(8,128)(2,1)S(1)}, u32[]{:S(2)}, u32[]{:S(2)}) %collective-permute-start.20) | collective-permute-done | bytes 1048608 | tf_op jit(solution)/shard_map/ppermute | solution.py:262
  487.7 1.3 collective-permute-start.27
  489.0 1.3 collective-permute-start.30
  490.3 8.1 %all_gather.7 = bf16[4,1024]{1,0:T(4,128)(2,1)S(1)} all-gather(bf16[4,256]{1,0:T(4,128)(2,1)S(1)} %broadcast_select_fusion), channel_id=1, replica_groups=mesh['zero'=4,'width'=4,'unit'=2] {'width'}, dimensions={1}, use_global_device_ids=true | all-gather | bytes 10240 | tf_op jit(solution)/shard_map/all_gather | solution.py:324
  499.0 2.6 own.4.refs_0_
  501.6 2.6 own.3.refs_0_
  506.8 1.2 place.24.refs_0_
  508.0 2.0 place.25.refs_0_
  512.1 1.4 place.15.refs_0_
  515.5 1.2 place.26.refs_0_
  516.7 8.1 %collective-permute-done.27.refs_1_ = bf16[256,1024]{1,0:T(8,128)(2,1)S(1)} collective-permute-done((bf16[256,1024]{1,0:T(8,128)(2,1)}, bf16[256,1024]{1,0:T(8,128)(2,1)S(1)}, u32[]{:S(2)}, u32[]{:S(2)}) %collective-permute-start.27) | collective-permute-done | bytes 524320 | tf_op jit(solution)/shard_map/ppermute | solution.py:262
  525.7 1.4 place.16.refs_0_
  528.3 2.2 collective-permute-done.30.refs_1_
  531.3 1.4 place.17
  (77 shorter events, 23.0 us)
Async XLA Ops:
  0.6 46.5 %copy-start.7 = (bf16[1024,16]{0,1:T(8,128)(2,1)S(1)}, bf16[1024,16]{0,1:T(8,128)(2,1)}, u32[]{:S(2)}) copy-start(bf16[1024,16]{0,1:T(8,128)(2,1)} %param.12) | copy-start | bytes 98308
  0.6 46.5 %copy-start.6 = (bf16[1024,16]{0,1:T(8,128)(2,1)S(1)}, bf16[1024,16]{0,1:T(8,128)(2,1)}, u32[]{:S(2)}) copy-start(bf16[1024,16]{0,1:T(8,128)(2,1)} %param.15) | copy-start | bytes 98308
  0.7 36.7 %copy-start.8 = (bf16[1024,16]{0,1:T(8,128)(2,1)S(1)}, bf16[1024,16]{0,1:T(8,128)(2,1)}, u32[]{:S(2)}) copy-start(bf16[1024,16]{0,1:T(8,128)(2,1)} %param.18) | copy-start | bytes 98308
  0.7 144.4 %copy-start.4 = (bf16[16,1024]{1,0:T(8,128)(2,1)S(1)}, bf16[16,1024]{1,0:T(8,128)(2,1)}, u32[]{:S(2)}) copy-start(bf16[16,1024]{1,0:T(8,128)(2,1)} %high.16) | copy-start | bytes 98308
  0.7 36.7 %copy-start.1 = (bf16[1024,1024]{1,0:T(8,128)(2,1)S(1)}, bf16[1024,1024]{1,0:T(8,128)(2,1)}, u32[]{:S(2)}) copy-start(bf16[1024,1024]{1,0:T(8,128)(2,1)} %train.5) | copy-start | bytes 6291460
  0.7 36.7 %copy-start.9 = (bf16[16,1024]{1,0:T(8,128)(2,1)S(1)}, bf16[16,1024]{1,0:T(8,128)(2,1)}, u32[]{:S(2)}) copy-start(bf16[16,1024]{1,0:T(8,128)(2,1)} %high.17) | copy-start | bytes 98308
  3.9 109.2 %collective-permute-start.11 = (bf16[512,1024]{1,0:T(8,128)(2,1)}, bf16[512,1024]{1,0:T(8,128)(2,1)S(1)}, u32[]{:S(2)}, u32[]{:S(2)}) collective-permute-start(bf16[512,1024]{1,0:T(8,128)(2,1)} %get-tuple-element.16), channel_id=1, source_target_pairs={{0,8},{8,0},{16,24},{24,16},{1,9},{9,1},{17,25},{25,17},{2,10},{10... | collective-permute-start | bytes 3145736 | tf_op jit(solution)/shard_map/ppermute | solution.py:262
  7.0 141.6 %copy-start.5 = (bf16[16,1024]{1,0:T(8,128)(2,1)S(1)}, bf16[16,1024]{1,0:T(8,128)(2,1)}, u32[]{:S(2)}) copy-start(bf16[16,1024]{1,0:T(8,128)(2,1)} %high.11) | copy-start | bytes 98308
  13.7 16.4 %collective-permute-start = (f32[4,1024]{1,0:T(4,128)}, f32[4,1024]{1,0:T(4,128)S(1)}, u32[]{:S(2)}, u32[]{:S(2)}) collective-permute-start(f32[4,1024]{1,0:T(4,128)} %tops.1.refs_0_), channel_id=1, source_target_pairs={{0,8},{8,16},{1,9},{9,17},{2,10},{10,18},{3,11},{11,19},{4,12},{12... | collective-permute-start | bytes 49160 | tf_op jit(solution)/shard_map/ppermute | solution.py:273
  15.6 14.7 %collective-permute-start.1 = (f32[4,1024]{1,0:T(4,128)}, f32[4,1024]{1,0:T(4,128)S(1)}, u32[]{:S(2)}, u32[]{:S(2)}) collective-permute-start(f32[4,1024]{1,0:T(4,128)} %tops.1.refs_0_), channel_id=1, source_target_pairs={{0,16},{24,8},{1,17},{25,9},{2,18},{26,10},{3,19},{27,11},{4,20},{... | collective-permute-start | bytes 49160 | tf_op jit(solution)/shard_map/ppermute | solution.py:273
  19.5 10.8 %collective-permute-start.2 = (f32[4,1024]{1,0:T(4,128)}, f32[4,1024]{1,0:T(4,128)S(1)}, u32[]{:S(2)}, u32[]{:S(2)}) collective-permute-start(f32[4,1024]{1,0:T(4,128)} %tops.1.refs_0_), channel_id=1, source_target_pairs={{16,8},{24,16},{17,9},{25,17},{18,10},{26,18},{19,11},{27,19},{20,... | collective-permute-start | bytes 49160 | tf_op jit(solution)/shard_map/ppermute | solution.py:273
  30.3 0.7 copy-start.10
  31.0 6.3 %collective-permute-start.3 = (f32[4,1024]{1,0:T(4,128)S(1)}, f32[4,1024]{1,0:T(4,128)S(1)}, u32[]{:S(2)}, u32[]{:S(2)}) collective-permute-start(f32[4,1024]{1,0:T(4,128)S(1)} %get-tuple-element.11), channel_id=1, source_target_pairs={{8,0},{16,24},{9,1},{17,25},{10,2},{18,26},{11,3},{19,27},{12,4},{... | collective-permute-start | bytes 49160 | tf_op jit(solution)/shard_map/ppermute | solution.py:289
  40.1 1.3 copy-start.3
  42.2 66.4 %collective-permute-start.23 = (bf16[256,1024]{1,0:T(8,128)(2,1)}, bf16[256,1024]{1,0:T(8,128)(2,1)}, u32[]{:S(2)}, u32[]{:S(2)}) collective-permute-start(bf16[256,1024]{1,0:T(8,128)(2,1)} %slice.38), channel_id=1, source_target_pairs={{0,8},{8,0},{16,24},{24,16},{1,9},{9,1},{17,25},{25,17},{2,10},{10... | collective-permute-start | bytes 1572872 | tf_op jit(solution)/shard_map/ppermute | solution.py:262
  42.2 68.6 %collective-permute-start.24 = (bf16[256,1024]{1,0:T(8,128)(2,1)}, bf16[256,1024]{1,0:T(8,128)(2,1)}, u32[]{:S(2)}, u32[]{:S(2)}) collective-permute-start(bf16[256,1024]{1,0:T(8,128)(2,1)} %slice.38), channel_id=1, source_target_pairs={{8,16},{16,8},{9,17},{17,9},{10,18},{18,10},{11,19},{19,11},{12,20... | collective-permute-start | bytes 1572872 | tf_op jit(solution)/shard_map/ppermute | solution.py:262
  43.7 103.5 %collective-permute-start.4 = (bf16[1024,1024]{1,0:T(8,128)(2,1)}, bf16[1024,1024]{1,0:T(8,128)(2,1)S(1)}, u32[]{:S(2)}, u32[]{:S(2)}) collective-permute-start(bf16[1024,1024]{1,0:T(8,128)(2,1)} %train.3), channel_id=1, source_target_pairs={{0,8},{8,0},{16,24},{24,16},{1,9},{9,1},{17,25},{25,17},{2,10},{10... | collective-permute-start | bytes 6291464 | tf_op jit(solution)/shard_map/ppermute | solution.py:262
  47.2 52.0 %collective-permute-start.5 = (bf16[16,512]{1,0:T(8,128)(2,1)S(1)}, bf16[16,512]{1,0:T(8,128)(2,1)S(1)}, u32[]{:S(2)}, u32[]{:S(2)}) collective-permute-start(bf16[16,512]{1,0:T(8,128)(2,1)S(1)} %fusion), channel_id=1, source_target_pairs={{0,8},{8,0},{16,24},{24,16},{1,9},{9,1},{17,25},{25,17},{2,10},{10... | collective-permute-start | bytes 49160 | tf_op jit(solution)/shard_map/ppermute | solution.py:262
  99.2 0.7 collective-permute-start.6
  99.9 8.1 %collective-permute-start.31 = (bf16[4,256]{1,0:T(4,128)(2,1)S(1)}, bf16[4,256]{1,0:T(4,128)(2,1)S(1)}, u32[]{:S(2)}, u32[]{:S(2)}) collective-permute-start(bf16[4,256]{1,0:T(4,128)(2,1)S(1)} %slice.52), channel_id=1, source_target_pairs={{8,0},{16,24},{9,1},{17,25},{10,2},{18,26},{11,3},{19,27},{12,4},{... | collective-permute-start | bytes 6152 | tf_op jit(solution)/shard_map/ppermute | solution.py:321
  108.0 7.6 %collective-permute-start.12 = (bf16[512,1024]{1,0:T(8,128)(2,1)}, bf16[512,1024]{1,0:T(8,128)(2,1)S(1)}, u32[]{:S(2)}, u32[]{:S(2)}) collective-permute-start(bf16[512,1024]{1,0:T(8,128)(2,1)} %get-tuple-element.16), channel_id=1, source_target_pairs={{8,16},{16,8},{9,17},{17,9},{10,18},{18,10},{11,19},{19,11},{12,20... | collective-permute-start | bytes 3145736 | tf_op jit(solution)/shard_map/ppermute | solution.py:262
  108.7 26.4 %collective-permute-start.13 = (bf16[512,1024]{1,0:T(8,128)(2,1)}, bf16[512,1024]{1,0:T(8,128)(2,1)S(1)}, u32[]{:S(2)}, u32[]{:S(2)}) collective-permute-start(bf16[512,1024]{1,0:T(8,128)(2,1)} %get-tuple-element.15), channel_id=1, source_target_pairs={{0,8},{8,0},{16,24},{24,16},{1,9},{9,1},{17,25},{25,17},{2,10},{10... | collective-permute-start | bytes 3145736 | tf_op jit(solution)/shard_map/ppermute | solution.py:262
  110.9 25.0 %collective-permute-start.14 = (bf16[512,1024]{1,0:T(8,128)(2,1)}, bf16[512,1024]{1,0:T(8,128)(2,1)S(1)}, u32[]{:S(2)}, u32[]{:S(2)}) collective-permute-start(bf16[512,1024]{1,0:T(8,128)(2,1)} %get-tuple-element.15), channel_id=1, source_target_pairs={{8,16},{16,8},{9,17},{17,9},{10,18},{18,10},{11,19},{19,11},{12,20... | collective-permute-start | bytes 3145736 | tf_op jit(solution)/shard_map/ppermute | solution.py:262
  113.2 50.4 %collective-permute-start.21 = (bf16[768,1024]{1,0:T(8,128)(2,1)S(1)}, bf16[768,1024]{1,0:T(8,128)(2,1)S(1)}, u32[]{:S(2)}, u32[]{:S(2)}) collective-permute-start(bf16[768,1024]{1,0:T(8,128)(2,1)S(1)} %slice.37), channel_id=1, source_target_pairs={{0,8},{8,0},{16,24},{24,16},{1,9},{9,1},{17,25},{25,17},{2,10},{10... | collective-permute-start | bytes 4718600 | tf_op jit(solution)/shard_map/ppermute | solution.py:262
  115.5 151.7 %collective-permute-start.7 = (bf16[1024,1024]{1,0:T(8,128)(2,1)}, bf16[1024,1024]{1,0:T(8,128)(2,1)S(1)}, u32[]{:S(2)}, u32[]{:S(2)}) collective-permute-start(bf16[1024,1024]{1,0:T(8,128)(2,1)} %train.3), channel_id=1, source_target_pairs={{8,16},{16,8},{9,17},{17,9},{10,18},{18,10},{11,19},{19,11},{12,20... | collective-permute-start | bytes 6291464 | tf_op jit(solution)/shard_map/ppermute | solution.py:262
  135.1 29.9 %collective-permute-start.22 = (bf16[768,1024]{1,0:T(8,128)(2,1)S(1)}, bf16[768,1024]{1,0:T(8,128)(2,1)S(1)}, u32[]{:S(2)}, u32[]{:S(2)}) collective-permute-start(bf16[768,1024]{1,0:T(8,128)(2,1)S(1)} %slice.37), channel_id=1, source_target_pairs={{8,16},{16,8},{9,17},{17,9},{10,18},{18,10},{11,19},{19,11},{12,20... | collective-permute-start | bytes 4718600 | tf_op jit(solution)/shard_map/ppermute | solution.py:262
  135.9 10.6 %collective-permute-start.28 = (bf16[256,1024]{1,0:T(8,128)(2,1)}, bf16[256,1024]{1,0:T(8,128)(2,1)S(1)}, u32[]{:S(2)}, u32[]{:S(2)}) collective-permute-start(bf16[256,1024]{1,0:T(8,128)(2,1)} %collective-permute-done.23.refs_1_), channel_id=1, source_target_pairs={{8,16},{16,8},{9,17},{17,9},{10,18},{18,10},{11,19},{19,11},{12,20... | collective-permute-start | bytes 1572872 | tf_op jit(solution)/shard_map/ppermute | solution.py:262
  145.1 353.9 %copy-start = (bf16[1024,1024]{1,0:T(8,128)(2,1)S(1)}, bf16[1024,1024]{1,0:T(8,128)(2,1)}, u32[]{:S(2)}) copy-start(bf16[1024,1024]{1,0:T(8,128)(2,1)} %train.4) | copy-start | bytes 6291460
  146.5 20.1 %collective-permute-start.16 = (bf16[512,1024]{1,0:T(8,128)(2,1)S(1)}, bf16[512,1024]{1,0:T(8,128)(2,1)S(1)}, u32[]{:S(2)}, u32[]{:S(2)}) collective-permute-start(bf16[512,1024]{1,0:T(8,128)(2,1)S(1)} %scale.8.refs_1_), channel_id=1, source_target_pairs={{8,16},{16,8},{9,17},{17,9},{10,18},{18,10},{11,19},{19,11},{12,20... | collective-permute-start | bytes 3145736 | tf_op jit(solution)/shard_map/ppermute | solution.py:262
  147.3 118.7 %collective-permute-start.15 = (bf16[512,1024]{1,0:T(8,128)(2,1)S(1)}, bf16[512,1024]{1,0:T(8,128)(2,1)S(1)}, u32[]{:S(2)}, u32[]{:S(2)}) collective-permute-start(bf16[512,1024]{1,0:T(8,128)(2,1)S(1)} %scale.9.refs_2_), channel_id=1, source_target_pairs={{8,0},{16,24},{9,1},{17,25},{10,2},{18,26},{11,3},{19,27},{12,4},{... | collective-permute-start | bytes 3145736 | tf_op jit(solution)/shard_map/ppermute | solution.py:262
  163.5 136.6 %collective-permute-start.9 = (bf16[1024,1024]{1,0:T(8,128)(2,1)S(1)}, bf16[1024,1024]{1,0:T(8,128)(2,1)S(1)}, u32[]{:S(2)}, u32[]{:S(2)}) collective-permute-start(bf16[1024,1024]{1,0:T(8,128)(2,1)S(1)} %scale.6.refs_1_), channel_id=1, source_target_pairs={{8,16},{16,8},{9,17},{17,9},{10,18},{18,10},{11,19},{19,11},{12,20... | collective-permute-start | bytes 6291464 | tf_op jit(solution)/shard_map/ppermute | solution.py:262
  165.0 336.6 %copy-start.2 = (bf16[1024,1024]{1,0:T(8,128)(2,1)S(1)}, bf16[1024,1024]{1,0:T(8,128)(2,1)}, u32[]{:S(2)}) copy-start(bf16[1024,1024]{1,0:T(8,128)(2,1)} %train.3) | copy-start | bytes 6291460
  165.0 104.9 %collective-permute-start.18 = (bf16[512,1024]{1,0:T(8,128)(2,1)S(1)}, bf16[512,1024]{1,0:T(8,128)(2,1)S(1)}, u32[]{:S(2)}, u32[]{:S(2)}) collective-permute-start(bf16[512,1024]{1,0:T(8,128)(2,1)S(1)} %scale.10.refs_1_), channel_id=1, source_target_pairs={{8,16},{16,8},{9,17},{17,9},{10,18},{18,10},{11,19},{19,11},{12,20... | collective-permute-start | bytes 3145736 | tf_op jit(solution)/shard_map/ppermute | solution.py:262
  166.6 144.7 %collective-permute-start.26 = (bf16[768,1024]{1,0:T(8,128)(2,1)S(1)}, bf16[768,1024]{1,0:T(8,128)(2,1)S(1)}, u32[]{:S(2)}, u32[]{:S(2)}) collective-permute-start(bf16[768,1024]{1,0:T(8,128)(2,1)S(1)} %collective-permute-done.21.refs_1_), channel_id=1, source_target_pairs={{8,16},{16,8},{9,17},{17,9},{10,18},{18,10},{11,19},{19,11},{12,20... | collective-permute-start | bytes 4718600 | tf_op jit(solution)/shard_map/ppermute | solution.py:262
  265.9 32.9 %collective-permute-start.17 = (bf16[512,1024]{1,0:T(8,128)(2,1)S(1)}, bf16[512,1024]{1,0:T(8,128)(2,1)S(1)}, u32[]{:S(2)}, u32[]{:S(2)}) collective-permute-start(bf16[512,1024]{1,0:T(8,128)(2,1)S(1)} %scale.11.refs_2_), channel_id=1, source_target_pairs={{8,0},{16,24},{9,1},{17,25},{10,2},{18,26},{11,3},{19,27},{12,4},{... | collective-permute-start | bytes 3145736 | tf_op jit(solution)/shard_map/ppermute | solution.py:262
  267.2 42.8 %collective-permute-start.19 = (bf16[512,1024]{1,0:T(8,128)(2,1)S(1)}, bf16[512,1024]{1,0:T(8,128)(2,1)S(1)}, u32[]{:S(2)}, u32[]{:S(2)}) collective-permute-start(bf16[512,1024]{1,0:T(8,128)(2,1)S(1)} %collective-permute-done.16.refs_2_), channel_id=1, source_target_pairs={{8,0},{16,24},{9,1},{17,25},{10,2},{18,26},{11,3},{19,27},{12,4},{... | collective-permute-start | bytes 3145736 | tf_op jit(solution)/shard_map/ppermute | solution.py:262
  269.9 255.8 %collective-permute-start.8 = (bf16[1024,1024]{1,0:T(8,128)(2,1)S(1)}, bf16[1024,1024]{1,0:T(8,128)(2,1)S(1)}, u32[]{:S(2)}, u32[]{:S(2)}) collective-permute-start(bf16[1024,1024]{1,0:T(8,128)(2,1)S(1)} %scale.7.refs_2_), channel_id=1, source_target_pairs={{8,0},{16,24},{9,1},{17,25},{10,2},{18,26},{11,3},{19,27},{12,4},{... | collective-permute-start | bytes 6291464 | tf_op jit(solution)/shard_map/ppermute | solution.py:262
  298.8 190.2 %collective-permute-start.25 = (bf16[768,1024]{1,0:T(8,128)(2,1)S(1)}, bf16[768,1024]{1,0:T(8,128)(2,1)S(1)}, u32[]{:S(2)}, u32[]{:S(2)}) collective-permute-start(bf16[768,1024]{1,0:T(8,128)(2,1)S(1)} %collective-permute-done.22.refs_2_), channel_id=1, source_target_pairs={{8,0},{16,24},{9,1},{17,25},{10,2},{18,26},{11,3},{19,27},{12,4},{... | collective-permute-start | bytes 4718600 | tf_op jit(solution)/shard_map/ppermute | solution.py:262
  300.1 231.2 %collective-permute-start.10 = (bf16[1024,1024]{1,0:T(8,128)(2,1)S(1)}, bf16[1024,1024]{1,0:T(8,128)(2,1)S(1)}, u32[]{:S(2)}, u32[]{:S(2)}) collective-permute-start(bf16[1024,1024]{1,0:T(8,128)(2,1)S(1)} %collective-permute-done.9.refs_2_), channel_id=1, source_target_pairs={{8,0},{16,24},{9,1},{17,25},{10,2},{18,26},{11,3},{19,27},{12,4},{... | collective-permute-start | bytes 6291464 | tf_op jit(solution)/shard_map/ppermute | solution.py:262
  310.0 177.6 %collective-permute-start.20 = (bf16[512,1024]{1,0:T(8,128)(2,1)S(1)}, bf16[512,1024]{1,0:T(8,128)(2,1)S(1)}, u32[]{:S(2)}, u32[]{:S(2)}) collective-permute-start(bf16[512,1024]{1,0:T(8,128)(2,1)S(1)} %collective-permute-done.18.refs_2_), channel_id=1, source_target_pairs={{8,0},{16,24},{9,1},{17,25},{10,2},{18,26},{11,3},{19,27},{12,4},{... | collective-permute-start | bytes 3145736 | tf_op jit(solution)/shard_map/ppermute | solution.py:262
  311.3 215.8 %collective-permute-start.29 = (bf16[768,1024]{1,0:T(8,128)(2,1)S(1)}, bf16[768,1024]{1,0:T(8,128)(2,1)S(1)}, u32[]{:S(2)}, u32[]{:S(2)}) collective-permute-start(bf16[768,1024]{1,0:T(8,128)(2,1)S(1)} %collective-permute-done.26.refs_2_), channel_id=1, source_target_pairs={{8,0},{16,24},{9,1},{17,25},{10,2},{18,26},{11,3},{19,27},{12,4},{... | collective-permute-start | bytes 4718600 | tf_op jit(solution)/shard_map/ppermute | solution.py:262
  487.7 37.2 %collective-permute-start.27 = (bf16[256,1024]{1,0:T(8,128)(2,1)}, bf16[256,1024]{1,0:T(8,128)(2,1)S(1)}, u32[]{:S(2)}, u32[]{:S(2)}) collective-permute-start(bf16[256,1024]{1,0:T(8,128)(2,1)} %collective-permute-done.24.refs_2_), channel_id=1, source_target_pairs={{8,0},{16,24},{9,1},{17,25},{10,2},{18,26},{11,3},{19,27},{12,4},{... | collective-permute-start | bytes 1572872 | tf_op jit(solution)/shard_map/ppermute | solution.py:262
  489.0 41.5 %collective-permute-start.30 = (bf16[256,1024]{1,0:T(8,128)(2,1)S(1)}, bf16[256,1024]{1,0:T(8,128)(2,1)S(1)}, u32[]{:S(2)}, u32[]{:S(2)}) collective-permute-start(bf16[256,1024]{1,0:T(8,128)(2,1)S(1)} %collective-permute-done.28.refs_2_), channel_id=1, source_target_pairs={{8,0},{16,24},{9,1},{17,25},{10,2},{18,26},{11,3},{19,27},{12,4},{... | collective-permute-start | bytes 1572872 | tf_op jit(solution)/shard_map/ppermute | solution.py:262
